TPU v7x, 32 devices: a whole 2x2x4 slice. The times are simulated.
32 devices in a mesh: fsdp: 8 (over y, x, core), sp: 4 (over z).
Axes of the slice: x: 2, y: 2, z: 4, core: 2. Of those that a mesh axis runs over, the one named last changes fastest.
Arguments:
- hidden_in: bfloat16 [8192, 2048], P(('fsdp', 'sp')), may hold values from -6 to 6
- positions: int32 [8192], P(('fsdp', 'sp')), may hold values from 0 to 1023, as said below
- attn_gain: float32 [2048], replicated, may hold values from 0.5 to 1.5
- qkv_weight: bfloat16 [4096, 2048], P('fsdp'), may hold values from -0.125 to 0.125
- query_gain: float32 [128], replicated, may hold values from 0.5 to 1.5
- key_gain: float32 [128], replicated, may hold values from 0.5 to 1.5
- out_weight: bfloat16 [2048, 2048], P('fsdp'), may hold values from -0.75 to 0.75
- mlp_gain: float32 [2048], replicated, may hold values from 0.5 to 1.5
- gate_up_weight: bfloat16 [12288, 2048], P('fsdp'), may hold values from -0.125 to 0.125
- down_weight: bfloat16 [2048, 6144], P('fsdp'), may hold values from -0.078125 to 0.078125
- cotangent: bfloat16 [8192, 2048], P(('fsdp', 'sp')), may hold values from -6 to 6
Outputs:
- hidden_out: bfloat16 [8192, 2048], P(('fsdp', 'sp'))
- grad_input: float32 [8192, 2048], P(('fsdp', 'sp'))
- grad_attn_gain: float32 [2048], replicated
- grad_qkv: float32 [4096, 2048], P('fsdp')
- grad_query_gain: float32 [128], replicated
- grad_key_gain: float32 [128], replicated
- grad_out: float32 [2048, 2048], P('fsdp')
- grad_mlp_gain: float32 [2048], replicated
- grad_gate_up: float32 [12288, 2048], P('fsdp')
- grad_down: float32 [2048, 6144], P('fsdp')
Inputs may be any that keep to these rules, and one draw needn't show every extreme that they name: Within each sequence of 1024 tokens the positions count up by one from 0 and restart at 0 at most once; the first sequence counts from 0 to 1023 without a restart.
All inputs are finite; a program needn't handle non-finite values.
Results may differ from a plain program's by a relative error of at most 0.02.
Values may be sent and summed in bfloat16 or wider, within the bound.
A program may use at most 576 MiB of HBM per device.

v0:
```python
import jax
import jax.numpy as jnp
from jax import lax
from jax.sharding import PartitionSpec as P

H = 16
KV = 8
HD = 128
FF = 6144


EPS = 1e-06
THETA = 1000000.0
NEGATIVE = -1e30


def rms_forward(values, gain):
    inverse = lax.rsqrt(jnp.mean(values * values, axis=-1, keepdims=True) + EPS)
    return (values * inverse * gain, inverse)


def rms_backward(values, inverse, gain, upstream):
    scaled = upstream * gain
    cubed = inverse * inverse * inverse
    gradient = inverse * scaled - values * cubed * jnp.mean(scaled * values, axis=-1, keepdims=True)
    return (gradient, upstream * values * inverse)


def rotary_tables(positions):
    half = HD // 2
    frequency = THETA ** (-(jnp.arange(half, dtype=jnp.float32) * 2.0 / HD))
    angle = positions.astype(jnp.float32)[:, None] * frequency[None, :]
    cosine = jnp.cos(angle)
    sine = jnp.sin(angle)
    return (
        jnp.concatenate([cosine, cosine], -1)[:, None, :],
        jnp.concatenate([sine, sine], -1)[:, None, :],
    )


def rotate(values, cosine, sine):
    half = HD // 2
    turned = jnp.concatenate([-values[..., half:], values[..., :half]], -1)
    return values * cosine + turned * sine


def rotate_back(gradient, cosine, sine):
    half = HD // 2
    scaled = gradient * sine
    return gradient * cosine + jnp.concatenate([scaled[..., half:], -scaled[..., :half]], -1)


def scores_block(query_block, keys, start, block):
    factor = HD ** (-0.5)
    scores = (
        jnp.einsum("qhd,khd->hqk", query_block, keys, preferred_element_type=jnp.float32) * factor
    )
    query_rows = start + jnp.arange(block)
    key_rows = jnp.arange(keys.shape[0])
    allowed = key_rows[None, :] <= query_rows[:, None]
    return jnp.where(allowed[None], scores, NEGATIVE)


def attention_forward(query, keys, values):
    length = query.shape[0]
    block = min(512, length)

    def one_block(index):
        start = index * block
        query_block = lax.dynamic_slice_in_dim(query, start, block, 0)
        scores = scores_block(query_block, keys, start, block)
        top = jnp.max(scores, axis=-1, keepdims=True)
        logsum = top + jnp.log(jnp.sum(jnp.exp(scores - top), axis=-1, keepdims=True))
        weights = jnp.exp(scores - logsum).astype(jnp.bfloat16)
        mixed = jnp.einsum("hqk,khd->qhd", weights, values, preferred_element_type=jnp.float32)
        return (mixed.astype(jnp.bfloat16), logsum[..., 0])

    mixed_all, logsums = lax.map(one_block, jnp.arange(length // block))
    return (mixed_all.reshape(query.shape), logsums)


def attention_backward(query, keys, values, mixed_all, logsums, grad_mixed):
    length = query.shape[0]
    block = min(512, length)
    factor = HD ** (-0.5)

    def one_block(carry, inputs):
        index, logsum = inputs
        start = index * block
        query_block = lax.dynamic_slice_in_dim(query, start, block, 0)
        grad_block = lax.dynamic_slice_in_dim(grad_mixed, start, block, 0)
        mixed_block = lax.dynamic_slice_in_dim(mixed_all, start, block, 0)
        scores = scores_block(query_block, keys, start, block)
        chances = jnp.exp(scores - logsum[..., None])
        weights_low = chances.astype(jnp.bfloat16)
        delta = jnp.sum(grad_block.astype(jnp.float32) * mixed_block.astype(jnp.float32), axis=-1)
        grad_weights = jnp.einsum(
            "qhd,khd->hqk", grad_block, values, preferred_element_type=jnp.float32
        )
        grad_scores = (chances * (grad_weights - delta.T[:, :, None])).astype(jnp.bfloat16)
        grad_query = (
            jnp.einsum("hqk,khd->qhd", grad_scores, keys, preferred_element_type=jnp.float32)
            * factor
        )
        key_total = (
            carry[0]
            + jnp.einsum(
                "hqk,qhd->khd", grad_scores, query_block, preferred_element_type=jnp.float32
            )
            * factor
        )
        value_total = carry[1] + jnp.einsum(
            "hqk,qhd->khd", weights_low, grad_block, preferred_element_type=jnp.float32
        )
        return ((key_total, value_total), grad_query)

    zeros = jnp.zeros(keys.shape, jnp.float32)
    totals, grad_query = lax.scan(one_block, (zeros, zeros), (jnp.arange(length // block), logsums))
    return (grad_query.reshape(query.shape), totals[0], totals[1])


def forward_project(inputs, weight):
    return lax.dot_general(
        inputs,
        lax.all_gather(weight, "fsdp", axis=0, tiled=True),
        (((1,), (1,)), ((), ())),
        preferred_element_type=jnp.float32,
    )


def backward_input(grad_low, weight):
    return jnp.dot(
        grad_low,
        lax.all_gather(weight, "fsdp", axis=0, tiled=True),
        preferred_element_type=jnp.float32,
    )


def weight_grad(grad_low, inputs):
    shard = lax.psum_scatter(
        lax.dot_general(
            grad_low, inputs, (((0,), (0,)), ((), ())), preferred_element_type=jnp.float32
        ).astype(jnp.bfloat16),
        "fsdp",
        scatter_dimension=0,
        tiled=True,
    )
    return lax.psum(shard, "sp").astype(jnp.float32)


def on_device(
    hidden_in,
    positions,
    attn_gain,
    qkv_weight,
    query_gain,
    key_gain,
    out_weight,
    mlp_gain,
    gate_up_weight,
    down_weight,
    cotangent,
):
    f32 = jnp.float32
    low = jnp.bfloat16
    rows = hidden_in.shape[0]
    group = H // KV
    hidden = hidden_in.astype(f32)
    normed1, inverse1 = rms_forward(hidden, attn_gain)
    normed1_low = normed1.astype(low)
    projected = forward_project(normed1_low, qkv_weight)
    query = projected[:, : H * HD].reshape(rows, H, HD)
    key = projected[:, H * HD : (H + KV) * HD].reshape(rows, KV, HD)
    value_low = projected[:, (H + KV) * HD :].astype(low)
    cosine, sine = rotary_tables(positions)
    query_normed, query_inverse = rms_forward(query, query_gain)
    key_normed, key_inverse = rms_forward(key, key_gain)
    query_low = rotate(query_normed, cosine, sine).astype(low).reshape(rows, H * HD)
    key_low = rotate(key_normed, cosine, sine).astype(low).reshape(rows, KV * HD)
    query_heads, key_heads, value_heads = (
        lax.all_to_all(query_low, "sp", split_axis=1, concat_axis=0, tiled=True),
        lax.all_to_all(key_low, "sp", split_axis=1, concat_axis=0, tiled=True),
        lax.all_to_all(value_low, "sp", split_axis=1, concat_axis=0, tiled=True),
    )
    length = query_heads.shape[0]
    local_kv = key_heads.shape[1] // HD
    query_local = query_heads.reshape(length, -1, HD)
    keys_local = jnp.repeat(key_heads.reshape(length, local_kv, HD), group, axis=1)
    values_local = jnp.repeat(value_heads.reshape(length, local_kv, HD), group, axis=1)
    mixed_heads, logsums = attention_forward(query_local, keys_local, values_local)
    attended = lax.all_to_all(
        mixed_heads.reshape(length, -1), "sp", split_axis=0, concat_axis=1, tiled=True
    )
    middle = hidden + forward_project(attended, out_weight)
    normed2, inverse2 = rms_forward(middle, mlp_gain)
    normed2_low = normed2.astype(low)
    gate_up = forward_project(normed2_low, gate_up_weight)
    gate = gate_up[:, :FF]
    upper = gate_up[:, FF:]
    sigmoid = jax.nn.sigmoid(gate)
    activation = (gate * sigmoid * upper).astype(low)
    hidden_out = (middle + forward_project(activation, down_weight)).astype(low)
    upstream = cotangent.astype(f32)
    grad_down = weight_grad(cotangent, activation)
    grad_act = backward_input(cotangent, down_weight)
    grad_gate = grad_act * upper * sigmoid * (1.0 + gate * (1.0 - sigmoid))
    grad_upper = grad_act * gate * sigmoid
    grad_gate_up_low = jnp.concatenate([grad_gate, grad_upper], 1).astype(low)
    grad_gate_up = weight_grad(grad_gate_up_low, normed2_low)
    grad_normed2 = backward_input(grad_gate_up_low, gate_up_weight)
    back_two, mlp_term = rms_backward(middle, inverse2, mlp_gain, grad_normed2)
    grad_middle = upstream + back_two
    grad_mixed_low = grad_middle.astype(low)
    grad_out = weight_grad(grad_mixed_low, attended)
    grad_attended = backward_input(grad_mixed_low, out_weight).astype(low)
    grad_heads = lax.all_to_all(grad_attended, "sp", split_axis=1, concat_axis=0, tiled=True)
    grad_query_local, grad_keys, grad_values = attention_backward(
        query_local,
        keys_local,
        values_local,
        mixed_heads,
        logsums,
        grad_heads.reshape(length, -1, HD),
    )
    grad_query_send = grad_query_local.astype(low).reshape(length, -1)
    grad_key_send = (
        grad_keys.reshape(length, local_kv, group, HD).sum(2).astype(low).reshape(length, -1)
    )
    grad_value_send = (
        grad_values.reshape(length, local_kv, group, HD).sum(2).astype(low).reshape(length, -1)
    )
    grad_query_low, grad_key_low, grad_value_low = (
        lax.all_to_all(grad_query_send, "sp", split_axis=0, concat_axis=1, tiled=True),
        lax.all_to_all(grad_key_send, "sp", split_axis=0, concat_axis=1, tiled=True),
        lax.all_to_all(grad_value_send, "sp", split_axis=0, concat_axis=1, tiled=True),
    )
    grad_query, query_term = rms_backward(
        query,
        query_inverse,
        query_gain,
        rotate_back(grad_query_low.astype(f32).reshape(rows, H, HD), cosine, sine),
    )
    grad_key, key_term = rms_backward(
        key,
        key_inverse,
        key_gain,
        rotate_back(grad_key_low.astype(f32).reshape(rows, KV, HD), cosine, sine),
    )
    grad_projected = jnp.concatenate(
        [
            grad_query.reshape(rows, H * HD).astype(low),
            grad_key.reshape(rows, KV * HD).astype(low),
            grad_value_low,
        ],
        1,
    )
    grad_qkv = weight_grad(grad_projected, normed1_low)
    grad_normed1 = backward_input(grad_projected, qkv_weight)
    back_one, attn_term = rms_backward(hidden, inverse1, attn_gain, grad_normed1)
    grad_input = grad_middle + back_one
    gains = lax.psum(
        (
            jnp.sum(attn_term, axis=0),
            jnp.sum(query_term, axis=(0, 1)),
            jnp.sum(key_term, axis=(0, 1)),
            jnp.sum(mlp_term, axis=0),
        ),
        ("fsdp", "sp"),
    )
    return (
        hidden_out,
        grad_input,
        gains[0],
        grad_qkv,
        gains[1],
        gains[2],
        grad_out,
        gains[3],
        grad_gate_up,
        grad_down,
    )


def solution(mesh):
    return jax.shard_map(
        on_device,
        mesh=mesh,
        in_specs=(
            P(("fsdp", "sp"), None),
            P(("fsdp", "sp")),
            P(),
            P("fsdp", None),
            P(),
            P(),
            P("fsdp", None),
            P(),
            P("fsdp", None),
            P("fsdp", None),
            P(("fsdp", "sp"), None),
        ),
        out_specs=(
            P(("fsdp", "sp"), None),
            P(("fsdp", "sp"), None),
            P(),
            P("fsdp", None),
            P(),
            P(),
            P("fsdp", None),
            P(),
            P("fsdp", None),
            P("fsdp", None),
        ),
        check_vma=False,
    )
```

profile of v0, /device:TPU:0, one launch (start us, length us, event | category | flops | bytes accessed | tf_op | source)
XLA Modules:
  0.0 1767.2 jit_solution(15282440730790111048)
XLA Ops:
  18.9 83.4 %all-gather.5.cloned.1.call-done = bf16[4096,2048]{1,0:T(8,128)(2,1)} async-done(((bf16[512,2048]{1,0:T(8,128)(2,1)}), bf16[4096,2048]{1,0:T(8,128)(2,1)}) %all-gather.5.cloned.1.call-update) | async-done | bytes 16777232 | tf_op jit(solution)/shard_map/all_gather | solution.py:125
  102.4 10.2 fusion.58
  147.9 10.5 all-to-all-done.1
  179.1 5.3 all-to-all-start
  188.6 20.7 %all-to-all-done = bf16[256,4,512]{2,0,1:T(8,128)(2,1)S(1)} async-done(((bf16[256,4,512]{2,0,1:T(8,128)(2,1)}), bf16[256,4,512]{2,0,1:T(8,128)(2,1)S(1)}, u32[]{:S(2)}, u32[]{:S(2)}) %all-to-all-start) | async-done | bytes 1048608 | tf_op jit(solution)/shard_map/all_to_all | solution.py:181
  209.7 26.5 %while.28 = (s32[]{:T(128)}, bf16[2,512,4,128]{3,1,2,0:T(8,128)(2,1)}, f32[2,4,512]{2,1,0:T(4,128)S(1)}, s32[2]{0:T(128)S(1)}, bf16[1024,4,128]{2,0,1:T(8,128)(2...) while((s32[]{:T(128)}, ...), condition=%wide.region_6.7_spmd.clone, body=%wide.region_3.6_spmd.clone.sunk | while | flops 1097595392 | bytes 46207252 | solution.py:78
  239.1 29.0 %all_to_all.119 = bf16[4,256,512]{2,1,0:T(8,128)(2,1)} all-to-all(bf16[4,256,512]{2,1,0:T(8,128)(2,1)S(1)} %all_to_all.99), channel_id=1, replica_groups=mesh['fsdp'=8,'sp'=4] {'sp'}, dimensions={0} | all-to-all | bytes 2097152 | tf_op jit(solution)/shard_map/all_to_all | solution.py:191
  270.4 6.5 multiply_reduce_fusion.5
  276.9 115.6 %all-gather.9.cloned.1.call-done = bf16[12288,2048]{1,0:T(8,128)(2,1)} async-done(((bf16[1536,2048]{1,0:T(8,128)(2,1)}), bf16[12288,2048]{1,0:T(8,128)(2,1)}) %all-gather.9.cloned.1.call-update) | async-done | bytes 50331664 | tf_op jit(solution)/shard_map/all_gather | solution.py:125
  392.6 25.7 %fusion.64 = f32[256,12288]{1,0:T(8,128)} fusion(bf16[12288,2048]{1,0:T(8,128)(2,1)} %all-gather.9.cloned.1.call-done, f32[256,2048]{1,0:T(8,128)S(1)} %get-tuple-element.437, f32[2048]{0:T(1024)S(1)} %copy-done.55, f32[256]{0:T(256)S(1)} %get-tuple-element.435), kind=kOutput, calls=%fused_computation.155 | convolution fusion | flops 12886474752 | bytes 65020928 | tf_op jit(solution)/shard_map/dot_general | solution.py:123
  418.3 101.2 %all-gather.11.cloned.1.call-done = bf16[2048,6144]{1,0:T(8,128)(2,1)} async-done(((bf16[256,6144]{1,0:T(8,128)(2,1)}), bf16[2048,6144]{1,0:T(8,128)(2,1)}) %all-gather.11.cloned.1.call-update) | async-done | bytes 25165840 | tf_op jit(solution)/shard_map/all_gather | solution.py:125
  519.5 18.5 %multiply_convert_fusion.2 = (bf16[256,6144]{1,0:T(8,128)(2,1)}, bf16[256,6144]{1,0:T(8,128)(2,1)}, bf16[256,6144]{1,0:T(8,128)(2,1)}) fusion(f32[256,12288]{1,0:T(8,128)} %fusion.64, bf16[256,2048]{1,0:T(8,128)(2,1)S(1)} %copy-done.27, bf16[2048,6144]{1,0:T(8,128)(2,1)} %all-gather.11.cloned.1.call-done), kind=kOutput, calls=%fused_computation.55 | convolution fusion | flops 6467616768 | bytes 48234496 | tf_op jit(solution)/shard_map/dot_general | solution.py:132
  538.0 22.7 %multiply_reduce_fusion.1 = (f32[2048]{0:T(1024)}, f32[256]{0:T(256)S(1)}, f32[256,2048]{1,0:T(8,128)S(1)}) fusion(f32[256,2048]{1,0:T(8,128)S(1)} %get-tuple-element.437, f32[256]{0:T(256)S(1)} %get-tuple-element.435, f32[2048]{0:T(1024)S(1)} %copy-done.55, bf16[12288,2048]{1,0:T(8,128)(2,1)} %all-gather.9.cloned.1.call-done, ...), kind=kOutput, calls=%fused_computation.88 | convolution fusion | flops 12900628480 | bytes 60835840 | tf_op jit(solution)/shard_map/dot_general | solution.py:132
  561.4 6.5 convolution_convert_fusion.3
  576.0 7.0 convolution_convert_fusion.2
  583.0 16.6 all-to-all-done.4
  600.7 49.3 %while.29 = (s32[]{:T(128)}, f32[1024,4,128]{0,2,1:T(8,128)S(1)}, f32[1024,4,128]{0,2,1:T(8,128)}, bf16[2,512,4,128]{3,1,2,0:T(8,128)(2,1)}, s32[2]{0:T(128)S(1)...) while((s32[]{:T(128)}, f32[1024,4,128]{0,2,1:T(8,128)S(1)}, ...), condition=%wide.region_11.12_spmd.clone, body=%wide.region_9.11_spmd.clone.sunk | while | flops 2709780992 | bytes 185127568 | solution.py:118
  658.6 12.0 all-to-all-done.7
  677.5 11.0 all-to-all-done.6
  709.0 8.4 all-to-all-done.5
  734.1 7.0 multiply_reduce_fusion.2
  741.1 9.9 convolution_convert_fusion.1
  752.9 17.7 %convert_bitcast_fusion = bf16[2048,6144]{0,1:T(8,128)(2,1)} fusion(bf16[256,6144]{1,0:T(8,128)(2,1)S(1)} %copy-done.26, bf16[256,2048]{1,0:T(8,128)(2,1)} %param.25), kind=kOutput, calls=%fused_computation.50 | convolution fusion | flops 6455033856 | bytes 29360128 | tf_op jit(solution)/shard_map/dot_general | solution.py:141
  772.6 24.0 %convolution_convert_fusion = bf16[12288,2048]{1,0:T(8,128)(2,1)} fusion(bf16[256,6144]{1,0:T(8,128)(2,1)} %get-tuple-element.404, bf16[256,6144]{1,0:T(8,128)(2,1)} %get-tuple-element.403, f32[256,2048]{1,0:T(8,128)S(1)} %copy-done.24, f32[2048]{0:T(1024)S(1)} %copy-done.56, f32[256]{0:T(256)S(1)} %copy-done.59), kind=kOutput, calls=%fused_computation.49 | convolution fusion | flops 12924223488 | bytes 58729472 | tf_op jit(solution)/shard_map/dot_general | solution.py:141
  796.7 68.8 %reduce-scatter.5.cloned.1.call-done = bf16[512,2048]{1,0:T(8,128)(2,1)} async-done(((bf16[4096,2048]{1,0:T(8,128)(2,1)}), bf16[512,2048]{1,0:T(8,128)(2,1)}) %reduce-scatter.5.cloned.1.call-update) | async-done | bytes 2097168 | tf_op jit(solution)/shard_map/reduce_scatter | solution.py:140
  865.5 159.6 %reduce-scatter.11.cloned.1.call-done = bf16[256,6144]{0,1:T(8,128)(2,1)} async-done(((bf16[2048,6144]{0,1:T(8,128)(2,1)}), bf16[256,6144]{0,1:T(8,128)(2,1)}) %reduce-scatter.11.cloned.1.call-update) | async-done | bytes 3145744 | tf_op jit(solution)/shard_map/reduce_scatter | solution.py:140
  1025.1 288.0 %reduce-scatter.9.cloned.1.call-done = bf16[1536,2048]{1,0:T(8,128)(2,1)} async-done(((bf16[12288,2048]{1,0:T(8,128)(2,1)}), bf16[1536,2048]{1,0:T(8,128)(2,1)}) %reduce-scatter.9.cloned.1.call-update) | async-done | bytes 6291472 | tf_op jit(solution)/shard_map/reduce_scatter | solution.py:140
  1313.2 14.4 fusion.40
  1327.6 12.6 fusion.49
  1340.2 47.4 %all-reduce = (f32[2048]{0:T(1024)}, f32[128]{0:T(128)}, f32[128]{0:T(128)}, f32[2048]{0:T(1024)}) all-reduce(f32[2048]{0:T(1024)S(1)} %get-tuple-element.353, f32[128]{0:T(128)S(1)} %bitcast_reduce_fusion.2, f32[128]{0:T(128)S(1)} %bitcast_reduce_fusion.3, f32[2048]{0:T(1024)S(1)} %copy-done.62), channel_id=1, replica_groups=mesh['fsdp'=8,'sp'=4] {'fsdp','sp'}, use_global_device_ids=true, to_apply=%region_18.19 | all-reduce | flops 4352 | bytes 34816 | tf_op jit(solution)/shard_map/psum | solution.py:261
  1391.1 352.1 %all-reduce.4.cloned.1.call-done = (bf16[256,6144]{0,1:T(8,128)(2,1)}, bf16[512,2048]{1,0:T(8,128)(2,1)}, bf16[256,2048]{1,0:T(8,128)(2,1)}, bf16[1536,2048]{1,0:T(8,128)(2,1)}) async-done(((bf16[256,6144]{0,1:T(8,128)(2,1)}, bf16[512,2048]{1,0:T(8,128)(2,1)}, bf16[256,2048]{1,0:T(8,128)(2,1)}, bf16[1536,2048]{1,0:T(8,128)(2,1)}), (bf16[256,6144]{0,1:T(8,128)(2,1)}, bf16[512,2048]{1,0:T(8,128)(2,1)}, ...) | async-done | bytes 12582928 | tf_op jit(solution)/shard_map/psum | solution.py:148
  1750.3 6.3 convert_element_type.185
  (350 shorter events, 230.4 us)
Async XLA Ops:
  7.2 95.2 %all-gather.5.cloned.1.call-start = ((), (), s32[]{:S(2)}) async-start(), calls=%async_computation.12 | async-start | bytes 18874368 | tf_op jit(solution)/shard_map/all_gather | solution.py:125
  7.9 262.5 %all-gather.7.cloned.1.call-start = ((), (), s32[]{:S(2)}) async-start(), calls=%async_computation.13 | async-start | bytes 9437184 | tf_op jit(solution)/shard_map/all_gather | solution.py:125
  8.7 383.9 %all-gather.9.cloned.1.call-start = ((), (), s32[]{:S(2)}) async-start(), calls=%async_computation.14 | async-start | bytes 56623104 | tf_op jit(solution)/shard_map/all_gather | solution.py:125
  9.4 510.1 %all-gather.11.cloned.1.call-start = ((), (), s32[]{:S(2)}) async-start(), calls=%async_computation.15 | async-start | bytes 28311552 | tf_op jit(solution)/shard_map/all_gather | solution.py:125
  10.4 152.2 %copy-start.38 = (f32[256,128]{0,1:T(8,128)}, f32[256,128]{0,1:T(8,128)S(1)}, u32[]{:S(2)}) copy-start(f32[256,128]{0,1:T(8,128)S(1)} %get-tuple-element.441) | copy-start | bytes 393220
  13.9 159.7 %copy-start.11 = (f32[256,2048]{1,0:T(8,128)}, f32[256,2048]{1,0:T(8,128)S(1)}, u32[]{:S(2)}) copy-start(f32[256,2048]{1,0:T(8,128)S(1)} %copy.256) | copy-start | bytes 6291460
  14.0 88.4 %copy-start.60 = (f32[2048]{0:T(1024)S(1)}, f32[2048]{0:T(1024)}, u32[]{:S(2)}) copy-start(f32[2048]{0:T(1024)} %param.17) | copy-start | bytes 24580
  18.9 93.7 %copy-start.68 = (f32[256]{0:T(256)}, f32[256]{0:T(256)S(1)}, u32[]{:S(2)}) copy-start(f32[256]{0:T(256)S(1)} %get-tuple-element.433) | copy-start | bytes 3076
  18.9 116.7 %copy-start.53 = (f32[1024]{0:T(1024)}, f32[1024]{0:T(1024)S(1)}, u32[]{:S(2)}) copy-start(f32[1024]{0:T(1024)S(1)} %broadcast_bitcast_fusion.1) | copy-start | bytes 12292
  18.9 154.6 %copy-start.50 = (f32[2048]{0:T(1024)}, f32[2048]{0:T(1024)S(1)}, u32[]{:S(2)}) copy-start(f32[2048]{0:T(1024)S(1)} %broadcast_bitcast_fusion) | copy-start | bytes 24580
  138.8 19.7 %all-to-all-start.1 = ((bf16[256,4,256]{2,0,1:T(8,128)(2,1)}), bf16[256,4,256]{2,0,1:T(8,128)(2,1)}, u32[]{:S(2)}, u32[]{:S(2)}) async-start(bf16[256,4,256]{2,0,1:T(8,128)(2,1)} %bitcast.141), calls=%async_computation.1 | async-start | bytes 1048576 | tf_op jit(solution)/shard_map/all_to_all | solution.py:182
  158.5 20.6 %all-to-all-start.2 = ((bf16[256,4,256]{2,0,1:T(8,128)(2,1)}), bf16[256,4,256]{2,0,1:T(8,128)(2,1)}, u32[]{:S(2)}, u32[]{:S(2)}) async-start(bf16[256,4,256]{2,0,1:T(8,128)(2,1)} %bitcast.218), calls=%async_computation.2 | async-start | bytes 1048576 | tf_op jit(solution)/shard_map/all_to_all | solution.py:183
  179.1 30.2 %all-to-all-start = ((bf16[256,4,512]{2,0,1:T(8,128)(2,1)}), bf16[256,4,512]{2,0,1:T(8,128)(2,1)S(1)}, u32[]{:S(2)}, u32[]{:S(2)}) async-start(bf16[256,4,512]{2,0,1:T(8,128)(2,1)} %bitcast.139), calls=%async_computation | async-start | bytes 2097152 | tf_op jit(solution)/shard_map/all_to_all | solution.py:181
  239.1 31.2 %copy-start.29 = (bf16[256,2048]{1,0:T(8,128)(2,1)S(1)}, bf16[256,2048]{1,0:T(8,128)(2,1)}, u32[]{:S(2)}) copy-start(bf16[256,2048]{1,0:T(8,128)(2,1)} %param.15) | copy-start | bytes 3145732
  270.4 122.2 %copy-start.55 = (f32[2048]{0:T(1024)S(1)}, f32[2048]{0:T(1024)}, u32[]{:S(2)}) copy-start(f32[2048]{0:T(1024)} %param.22) | copy-start | bytes 24580
  276.9 283.8 %copy-start.23 = (f32[256,2048]{1,0:T(8,128)}, f32[256,2048]{1,0:T(8,128)S(1)}, u32[]{:S(2)}) copy-start(f32[256,2048]{1,0:T(8,128)S(1)} %get-tuple-element.437) | copy-start | bytes 6291460
  276.9 283.8 %copy-start.58 = (f32[256]{0:T(256)}, f32[256]{0:T(256)S(1)}, u32[]{:S(2)}) copy-start(f32[256]{0:T(256)S(1)} %get-tuple-element.435) | copy-start | bytes 3076
  392.6 127.0 %copy-start.27 = (bf16[256,2048]{1,0:T(8,128)(2,1)S(1)}, bf16[256,2048]{1,0:T(8,128)(2,1)}, u32[]{:S(2)}) copy-start(bf16[256,2048]{1,0:T(8,128)(2,1)} %param.25) | copy-start | bytes 3145732
  568.9 30.7 %all-to-all-start.4 = ((bf16[256,4,512]{2,0,1:T(8,128)(2,1)}), bf16[256,4,512]{2,0,1:T(8,128)(2,1)S(1)}, u32[]{:S(2)}, u32[]{:S(2)}) async-start(bf16[256,4,512]{2,0,1:T(8,128)(2,1)} %bitcast.138), calls=%async_computation.4 | async-start | bytes 2097152 | tf_op jit(solution)/shard_map/all_to_all | solution.py:216
  573.5 223.2 %reduce-scatter.7.cloned.1.call-start = ((), (), s32[]{:S(2)}) async-start(), calls=%async_computation.17 | async-start | bytes 9437184 | tf_op jit(solution)/shard_map/reduce_scatter | solution.py:140
  653.4 17.2 all-to-all-start.7
  657.1 17.4 copy-start.57
  657.1 18.3 %copy-start.52 = (f32[256,16]{0,1:T(8,128)S(1)}, f32[256,16]{0,1:T(8,128)}, u32[]{:S(2)}) copy-start(f32[256,16]{0,1:T(8,128)} %get-tuple-element.426) | copy-start | bytes 49156
  657.5 18.0 %copy-start.49 = (bf16[2,512,4,128]{3,1,2,0:T(8,128)(2,1)S(1)}, bf16[2,512,4,128]{3,1,2,0:T(8,128)(2,1)}, u32[]{:S(2)}) copy-start(bf16[2,512,4,128]{3,1,2,0:T(8,128)(2,1)} %get-tuple-element.109) | copy-start | bytes 3145732
  670.6 17.9 %all-to-all-start.6 = ((bf16[4,256,256]{2,1,0:T(8,128)(2,1)}), bf16[4,256,256]{2,1,0:T(8,128)(2,1)S(1)}, u32[]{:S(2)}, u32[]{:S(2)}) async-start(bf16[4,256,256]{2,1,0:T(8,128)(2,1)} %copy.262), calls=%async_computation.6 | async-start | bytes 1048576 | tf_op jit(solution)/shard_map/all_to_all | solution.py:234
  688.5 28.9 %all-to-all-start.5 = ((bf16[4,256,512]{2,1,0:T(8,128)(2,1)}), bf16[4,256,512]{2,1,0:T(8,128)(2,1)S(1)}, u32[]{:S(2)}, u32[]{:S(2)}) async-start(bf16[4,256,512]{2,1,0:T(8,128)(2,1)} %convert_element_type.163), calls=%async_computation.5 | async-start | bytes 2097152 | tf_op jit(solution)/shard_map/all_to_all | solution.py:233
  692.2 173.3 %reduce-scatter.5.cloned.1.call-start = ((), (), s32[]{:S(2)}) async-start(), calls=%async_computation.16 | async-start | bytes 18874368 | tf_op jit(solution)/shard_map/reduce_scatter | solution.py:140
  751.0 274.2 %reduce-scatter.11.cloned.1.call-start = ((), (), s32[]{:S(2)}) async-start(), calls=%async_computation.19 | async-start | bytes 28311552 | tf_op jit(solution)/shard_map/reduce_scatter | solution.py:140
  770.6 542.5 %reduce-scatter.9.cloned.1.call-start = ((), (), s32[]{:S(2)}) async-start(), calls=%async_computation.18 | async-start | bytes 56623104 | tf_op jit(solution)/shard_map/reduce_scatter | solution.py:140
  796.7 946.6 %all-reduce.4.cloned.1.call-start = ((), (), s32[]{:S(2)}) async-start(), calls=%async_computation.20 | async-start | bytes 25165824 | tf_op jit(solution)/shard_map/psum | solution.py:148
  1327.6 60.1 %copy-start.9 = (f32[256,2048]{1,0:T(8,128)S(1)}, f32[256,2048]{1,0:T(8,128)}, u32[]{:S(2)}) copy-start(f32[256,2048]{1,0:T(8,128)} %copy-done.7) | copy-start | bytes 6291460
  1327.6 60.0 %copy-start.67 = (f32[256]{0:T(256)S(1)}, f32[256]{0:T(256)}, u32[]{:S(2)}) copy-start(f32[256]{0:T(256)} %get-tuple-element.432) | copy-start | bytes 3076
  (71 other events, 275.3 us)
Sparse Core Ops, SparseCore 0:
  9.9 92.4 all-gather.4
  104.2 54.2 all-gather.6
  160.4 232.0 all-gather.8
  394.3 125.1 all-gather.10
  583.2 71.9 reduce-scatter.6
  751.1 114.3 reduce-scatter.4
  869.1 155.9 reduce-scatter.10
  1028.8 284.3 reduce-scatter.8
  1316.0 427.1 all-reduce.3
where the time goes:
time: 1780 us; the launch traced here: 1770 us
  waiting for transfers between devices  1250 us (70%)
  matrix products  216 us (12%)
  local copies, waits for them, and re-layouts  111 us (6%)
  blocking collectives  76.4 us (4%)
  other arithmetic  64.7 us (4%)
  starting transfers between devices  30.1 us (2%)
    reduce_scatter x4, waiting for transfers between devices, weight_grad(): lax.psum_scatter(lax.dot_general(grad_low, inputs, (((0,), (0,)), ((), ()...  516 us
    psum x1, waiting for transfers between devices, weight_grad(): return lax.psum(shard, 'sp').astype(jnp.float32)  352 us
    all_gather x4, waiting for transfers between devices, forward_project(): lax.all_gather(weight, 'fsdp', axis=0, tiled=True)  300 us
    dot_general x4, matrix products, backward_input(): jnp.dot(grad_low, lax.all_gather(weight, 'fsdp', axis=0, tiled=True), pre...  60.3 us
    dot_general x4, matrix products, weight_grad(): lax.dot_general(grad_low, inputs, (((0,), (0,)), ((), ())), preferred_ele...  58.7 us
    dot_general x4, matrix products, forward_project(): lax.dot_general(inputs, lax.all_gather(weight, 'fsdp', axis=0, tiled=True...  56.8 us
    psum x1, blocking collectives, on_device(): lax.psum((jnp.sum(attn_term, axis=0), jnp.sum(query_term, axis=(0, 1)), j...  47.4 us
  transfers between devices with their start and end apart: 16, of which 13 were waited for; matrix products, arithmetic and copies ran while one was open for 17% of the time, Pallas kernels for 0%

commit v1 on v0

v1 whole, which is shorter than its diff:
```python
import functools

import jax
import jax.numpy as jnp
from jax import lax
from jax.sharding import PartitionSpec as P


H = 16
KV = 8
HD = 128
FF = 6144


EPS = 1e-06
THETA = 1000000.0
NEGATIVE = -1e30


def rms_forward(values, gain):
    inverse = lax.rsqrt(jnp.mean(values * values, axis=-1, keepdims=True) + EPS)
    return (values * inverse * gain, inverse)


def rms_backward(values, inverse, gain, upstream):
    scaled = upstream * gain
    cubed = inverse * inverse * inverse
    gradient = inverse * scaled - values * cubed * jnp.mean(scaled * values, axis=-1, keepdims=True)
    return (gradient, upstream * values * inverse)


def rotary_tables(positions):
    half = HD // 2
    frequency = THETA ** (-(jnp.arange(half, dtype=jnp.float32) * 2.0 / HD))
    angle = positions.astype(jnp.float32)[:, None] * frequency[None, :]
    cosine = jnp.cos(angle)
    sine = jnp.sin(angle)
    return (
        jnp.concatenate([cosine, cosine], -1)[:, None, :],
        jnp.concatenate([sine, sine], -1)[:, None, :],
    )


def rotate(values, cosine, sine):
    half = HD // 2
    turned = jnp.concatenate([-values[..., half:], values[..., :half]], -1)
    return values * cosine + turned * sine


def rotate_back(gradient, cosine, sine):
    half = HD // 2
    scaled = gradient * sine
    return gradient * cosine + jnp.concatenate([scaled[..., half:], -scaled[..., :half]], -1)


def scores_block(query_block, keys, start):
    scores = jnp.einsum("qhd,khd->hqk", query_block, keys, preferred_element_type=jnp.float32)
    query_rows = start + jnp.arange(query_block.shape[0])
    key_rows = jnp.arange(keys.shape[0])
    allowed = key_rows[None, :] <= query_rows[:, None]
    return jnp.where(allowed[None], scores * HD ** (-0.5), NEGATIVE)


def blocks_of(length):
    block = min(512, length)
    return [(start, start + block) for start in range(0, length, block)]


def attention_forward(query, keys, values):
    mixed_all, logsums = [], []
    for start, stop in blocks_of(query.shape[0]):
        scores = scores_block(query[start:stop], keys[:stop], start)
        top = jnp.max(scores, axis=-1, keepdims=True)
        logsum = top + jnp.log(jnp.sum(jnp.exp(scores - top), axis=-1, keepdims=True))
        weights = jnp.exp(scores - logsum).astype(jnp.bfloat16)
        mixed = jnp.einsum(
            "hqk,khd->qhd", weights, values[:stop], preferred_element_type=jnp.float32
        )
        mixed_all.append(mixed.astype(jnp.bfloat16))
        logsums.append(logsum)
    return (jnp.concatenate(mixed_all, 0), logsums)


def attention_backward(query, keys, values, mixed_all, logsums, grad_mixed, between):
    length = query.shape[0]
    factor = HD ** (-0.5)
    grad_query, key_total, value_total = [], None, None
    for (start, stop), logsum in reversed(list(zip(blocks_of(length), logsums))):
        query_block = query[start:stop]
        grad_block = grad_mixed[start:stop]
        mixed_block = mixed_all[start:stop]
        scores = scores_block(query_block, keys[:stop], start)
        chances = jnp.exp(scores - logsum)
        weights_low = chances.astype(jnp.bfloat16)
        delta = jnp.sum(grad_block.astype(jnp.float32) * mixed_block.astype(jnp.float32), axis=-1)
        grad_weights = jnp.einsum(
            "qhd,khd->hqk", grad_block, values[:stop], preferred_element_type=jnp.float32
        )
        grad_scores = (chances * (grad_weights - delta.T[:, :, None])).astype(jnp.bfloat16)
        grad_query.append(
            jnp.einsum(
                "hqk,khd->qhd", grad_scores, keys[:stop], preferred_element_type=jnp.float32
            )
            * factor
        )
        key_part = (
            jnp.einsum(
                "hqk,qhd->khd", grad_scores, query_block, preferred_element_type=jnp.float32
            )
            * factor
        )
        value_part = jnp.einsum(
            "hqk,qhd->khd", weights_low, grad_block, preferred_element_type=jnp.float32
        )
        if key_total is None:
            key_total, value_total = key_part, value_part
            between(grad_query[0])
        else:
            key_total = key_total.at[:stop].add(key_part)
            value_total = value_total.at[:stop].add(value_part)
    return (jnp.concatenate(grad_query[::-1], 0), key_total, value_total)


def gather_rows(array):
    return lax.all_gather(array, "fsdp", axis=0, tiled=True)


def product_nt(inputs, weight):
    return lax.dot_general(
        inputs, weight, (((1,), (1,)), ((), ())), preferred_element_type=jnp.float32
    )


def product_tn(left, right):
    return lax.dot_general(
        left, right, (((0,), (0,)), ((), ())), preferred_element_type=jnp.float32
    )


def scatter_sum(partial):
    return lax.psum_scatter(
        partial.astype(jnp.bfloat16), "fsdp", scatter_dimension=0, tiled=True
    ).astype(jnp.float32)


class Chain:
    def __init__(self, partial, count):
        half = count // 2
        self.count = count
        self.value = partial.astype(jnp.bfloat16)
        self.hops = []
        if count % 2 == 0:
            for s in range(half - 1):
                self.hops.append(([(s, s + 1), (count - 1 - s, count - 2 - s)], None))
            self.hops.append(([(half - 1, half), (half, half - 1)], None))
            for s in reversed(range(half - 1)):
                self.hops.append(([(s + 1, s), (count - 2 - s, count - 1 - s)], s))
        elif count > 1:
            self.value = lax.psum(self.value, "sp")
        self.at = 0
        self.send()

    def send(self):
        if self.at < len(self.hops):
            self.flying = lax.ppermute(self.value, "sp", self.hops[self.at][0])

    def advance(self):
        if self.at >= len(self.hops):
            return
        arrived = self.flying
        depth = self.hops[self.at][1]
        if depth is None:
            total = self.value.astype(jnp.float32) + arrived.astype(jnp.float32)
            self.value = total.astype(jnp.bfloat16)
        else:
            place = lax.axis_index("sp")
            mine = jnp.minimum(place, self.count - 1 - place) == depth
            self.value = jnp.where(mine, arrived, self.value)
        self.at += 1
        self.send()

    def finish(self):
        while self.at < len(self.hops):
            self.advance()
        return self.value


def halves(array):
    middle = array.shape[0] // 2
    return (array[:middle], array[middle:])


def layer(
    ways,
    line,
    hidden_in,
    positions,
    attn_gain,
    qkv_weight,
    query_gain,
    key_gain,
    out_weight,
    mlp_gain,
    gate_up_weight,
    down_weight,
    cotangent,
):
    f32 = jnp.float32
    low = jnp.bfloat16
    rows, width = hidden_in.shape
    group = H // KV
    units = FF // ways
    pairs_of = ways // 2
    side = lax.axis_index("fsdp") // pairs_of
    swap = [(f, (f + pairs_of) % ways) for f in range(ways)]

    qkv_full = gather_rows(qkv_weight)
    qkv_full, gate_up_late, down_late, out_late, cotangent_late = lax.optimization_barrier(
        (qkv_full, gate_up_weight, down_weight, out_weight, cotangent)
    )
    out_full = gather_rows(out_late)
    cotangent_all = gather_rows(cotangent_late)
    kept = lax.dynamic_slice_in_dim(gate_up_late, side * units, units, 0)
    sent = lax.dynamic_slice_in_dim(gate_up_late, (1 - side) * units, units, 0)
    swapped = lax.ppermute(sent, "fsdp", swap)
    gate_up_own = jnp.concatenate([kept, swapped], 0)
    down_split = down_late.reshape(-1, pairs_of, 2, units).transpose(2, 1, 0, 3)
    down_turned = lax.all_to_all(
        down_split.reshape(ways, -1, units), "fsdp", split_axis=0, concat_axis=0, tiled=True
    )
    hidden = hidden_in.astype(f32)
    normed1, inverse1 = rms_forward(hidden, attn_gain)
    normed1_low = normed1.astype(low)
    projected = product_nt(normed1_low, qkv_full)
    query = projected[:, : H * HD].reshape(rows, H, HD)
    key = projected[:, H * HD : (H + KV) * HD].reshape(rows, KV, HD)
    value_low = projected[:, (H + KV) * HD :].astype(low)
    cosine, sine = rotary_tables(positions)
    query_normed, query_inverse = rms_forward(query, query_gain)
    key_normed, key_inverse = rms_forward(key, key_gain)
    query_low = rotate(query_normed, cosine, sine).astype(low).reshape(rows, H * HD)
    key_low = rotate(key_normed, cosine, sine).astype(low).reshape(rows, KV * HD)
    query_low, key_low, value_low, down_turned = lax.optimization_barrier(
        (query_low, key_low, value_low, down_turned)
    )
    down_own = down_turned.reshape(width, units)
    query_heads, key_heads, value_heads = (
        lax.all_to_all(query_low, "sp", split_axis=1, concat_axis=0, tiled=True),
        lax.all_to_all(key_low, "sp", split_axis=1, concat_axis=0, tiled=True),
        lax.all_to_all(value_low, "sp", split_axis=1, concat_axis=0, tiled=True),
    )
    length = query_heads.shape[0]
    local_kv = key_heads.shape[1] // HD
    query_local = query_heads.reshape(length, -1, HD)
    keys_local = jnp.repeat(key_heads.reshape(length, local_kv, HD), group, axis=1)
    values_local = jnp.repeat(value_heads.reshape(length, local_kv, HD), group, axis=1)
    mixed_heads, logsums = attention_forward(query_local, keys_local, values_local)
    attended = lax.all_to_all(
        mixed_heads.reshape(length, -1), "sp", split_axis=0, concat_axis=1, tiled=True
    )
    middle = hidden + product_nt(attended, out_full)
    normed2, inverse2 = rms_forward(middle, mlp_gain)
    normed2_all = gather_rows(normed2.astype(low))
    normed1_late, middle = lax.optimization_barrier((normed1_low, middle))
    normed1_all = gather_rows(normed1_late)

    grad_act = jnp.dot(cotangent_all, down_own, preferred_element_type=f32)
    both = product_nt(normed2_all, gate_up_own)
    first, second = both[:, :units], both[:, units:]
    gate = jnp.where(side == 0, first, second)
    upper = jnp.where(side == 0, second, first)
    sigmoid = jax.nn.sigmoid(gate)
    activation = (gate * sigmoid * upper).astype(low)
    grad_gate = grad_act * upper * sigmoid * (1.0 + gate * (1.0 - sigmoid))
    grad_upper = grad_act * gate * sigmoid
    grad_first = jnp.where(side == 0, grad_gate, grad_upper).astype(low)
    grad_second = jnp.where(side == 0, grad_upper, grad_gate).astype(low)
    grad_both = jnp.concatenate([grad_first, grad_second], 1)
    grad_normed2 = scatter_sum(jnp.dot(grad_both, gate_up_own, preferred_element_type=f32))
    grad_kept = product_tn(grad_first, normed2_all).astype(low)
    grad_sent = product_tn(grad_second, normed2_all).astype(low)
    grad_down_own = product_tn(cotangent_all, activation).astype(low)
    kept_chains = [Chain(part, line) for part in halves(grad_kept)]
    grad_down_sum = lax.psum(grad_down_own, "sp")

    back_two, mlp_term = rms_backward(middle, inverse2, mlp_gain, grad_normed2)
    grad_middle = cotangent.astype(f32) + back_two
    grad_mixed_low = grad_middle.astype(low)
    grad_attended = jnp.dot(grad_mixed_low, out_full, preferred_element_type=f32).astype(low)
    grad_heads = lax.all_to_all(grad_attended, "sp", split_axis=1, concat_axis=0, tiled=True)
    grad_sent, grad_mixed_low = lax.optimization_barrier((grad_sent, grad_mixed_low))
    grad_out = scatter_sum(product_tn(grad_mixed_low, attended))
    sent_chains = [Chain(part, line) for part in halves(grad_sent)]
    for chain in kept_chains:
        chain.advance()

    def between(value):
        for chain in kept_chains:
            chain.advance()

    activation_late, grad_heads = lax.optimization_barrier((activation, grad_heads))
    hidden_out = (middle + scatter_sum(product_nt(activation_late, down_own))).astype(low)

    grad_query_local, grad_keys, grad_values = attention_backward(
        query_local,
        keys_local,
        values_local,
        mixed_heads,
        logsums,
        grad_heads.reshape(length, -1, HD),
        between,
    )
    grad_query_send = grad_query_local.astype(low).reshape(length, -1)
    grad_key_send = (
        grad_keys.reshape(length, local_kv, group, HD).sum(2).astype(low).reshape(length, -1)
    )
    grad_value_send = (
        grad_values.reshape(length, local_kv, group, HD).sum(2).astype(low).reshape(length, -1)
    )
    for chain in sent_chains:
        chain.advance()
    grad_query_low, grad_key_low, grad_value_low = (
        lax.all_to_all(grad_query_send, "sp", split_axis=0, concat_axis=1, tiled=True),
        lax.all_to_all(grad_key_send, "sp", split_axis=0, concat_axis=1, tiled=True),
        lax.all_to_all(grad_value_send, "sp", split_axis=0, concat_axis=1, tiled=True),
    )
    grad_query, query_term = rms_backward(
        query,
        query_inverse,
        query_gain,
        rotate_back(grad_query_low.astype(f32).reshape(rows, H, HD), cosine, sine),
    )
    grad_key, key_term = rms_backward(
        key,
        key_inverse,
        key_gain,
        rotate_back(grad_key_low.astype(f32).reshape(rows, KV, HD), cosine, sine),
    )
    grad_projected = jnp.concatenate(
        [
            grad_query.reshape(rows, H * HD).astype(low),
            grad_key.reshape(rows, KV * HD).astype(low),
            grad_value_low,
        ],
        1,
    )
    grad_columns = lax.all_to_all(grad_projected, "fsdp", split_axis=1, concat_axis=0, tiled=True)
    for chain in sent_chains:
        chain.advance()
    grad_qkv_own = product_tn(grad_columns, normed1_all)
    qkv_chains = [Chain(part, line) for part in halves(grad_qkv_own)]
    out_chain = Chain(grad_out, line)
    grad_normed1 = jnp.dot(grad_projected, qkv_full, preferred_element_type=f32)
    back_one, attn_term = rms_backward(hidden, inverse1, attn_gain, grad_normed1)
    grad_input = grad_middle + back_one
    grad_kept = jnp.concatenate([chain.finish() for chain in kept_chains], 0)
    grad_sent = jnp.concatenate([chain.finish() for chain in sent_chains], 0)
    grad_swapped = lax.ppermute(grad_sent, "fsdp", swap)
    grad_gate_up = jnp.concatenate(
        [
            jnp.where(side == 0, grad_kept, grad_swapped),
            jnp.where(side == 0, grad_swapped, grad_kept),
        ],
        0,
    ).astype(f32)
    grad_down_sum, grad_projected = lax.optimization_barrier((grad_down_sum, grad_projected))
    down_back = lax.all_to_all(
        grad_down_sum.reshape(ways, -1, units),
        "fsdp",
        split_axis=0,
        concat_axis=0,
        tiled=True,
    )
    grad_down = (
        down_back.reshape(2, pairs_of, -1, units)
        .transpose(2, 1, 0, 3)
        .reshape(down_weight.shape)
        .astype(f32)
    )
    grad_out = out_chain.finish().astype(f32)
    grad_qkv = jnp.concatenate([chain.finish() for chain in qkv_chains], 0).astype(f32)
    terms = jnp.concatenate(
        [
            jnp.sum(attn_term, axis=0),
            jnp.sum(mlp_term, axis=0),
            jnp.sum(query_term, axis=(0, 1)),
            jnp.sum(key_term, axis=(0, 1)),
        ]
    )
    all_terms = lax.all_gather(terms.reshape(1, -1), ("fsdp", "sp"), axis=0, tiled=True)
    sums = jnp.sum(all_terms, axis=0)
    gains = (
        sums[:width],
        sums[2 * width : 2 * width + HD],
        sums[2 * width + HD :],
        sums[width : 2 * width],
    )
    return (
        hidden_out,
        grad_input,
        gains[0],
        grad_qkv,
        gains[1],
        gains[2],
        grad_out,
        gains[3],
        grad_gate_up,
        grad_down,
    )


def solution(mesh):
    return jax.shard_map(
        functools.partial(layer, mesh.shape["fsdp"], mesh.shape["sp"]),
        mesh=mesh,
        in_specs=(
            P(("fsdp", "sp"), None),
            P(("fsdp", "sp")),
            P(),
            P("fsdp", None),
            P(),
            P(),
            P("fsdp", None),
            P(),
            P("fsdp", None),
            P("fsdp", None),
            P(("fsdp", "sp"), None),
        ),
        out_specs=(
            P(("fsdp", "sp"), None),
            P(("fsdp", "sp"), None),
            P(),
            P("fsdp", None),
            P(),
            P(),
            P("fsdp", None),
            P(),
            P("fsdp", None),
            P("fsdp", None),
        ),
        check_vma=False,
    )
```

time: 1780 us -> 1370 us (0.77)
  waiting for transfers between devices: 1250 us -> 557 us
  starting transfers between devices: 30.1 us -> 189 us
  other arithmetic: 64.7 us -> 139 us
  blocking collectives: 76.4 us -> 123 us
  matrix products: 216 us -> 181 us
  local copies, waits for them, and re-layouts: 111 us -> 143 us
    reduce_scatter x4 -> x3, waiting for transfers between devices: 516 us -> 19.9 us  [scatter_sum(): lax.psum_scatter(partial.astype(jnp.bfloat16), 'fsdp', scatter_dimension=...]
    psum x1, waiting for transfers between devices: 352 us -> 0.01 us  [layer(): grad_down_sum = lax.psum(grad_down_own, 'sp')]
    ppermute x0 -> x23, waiting for transfers between devices: none -> 324 us  [the longest x21 216 us: send(): self.flying = lax.ppermute(self.value, 'sp', self.hops[self.at][0])]
    all_gather x4 -> x5, waiting for transfers between devices: 300 us -> 108 us  [gather_rows(): return lax.all_gather(array, 'fsdp', axis=0, tiled=True)]
    all_to_all x7 -> x10, starting transfers between devices: 29.8 us -> 133 us  [the longest x1 92.5 us: layer(): lax.all_to_all(grad_attended, 'sp', split_axis=1, concat_axis=0, tiled=True)]
    all_gather x0 -> x1, blocking collectives: none -> 94.8 us  [layer(): lax.all_gather(terms.reshape(1, -1), ('fsdp', 'sp'), axis=0, tiled=True)]
    ppermute x0 -> x23, starting transfers between devices: none -> 55.6 us  [the longest x21 53 us: send(): self.flying = lax.ppermute(self.value, 'sp', self.hops[self.at][0])]
    convert_element_type x5 -> x21, other arithmetic: 20.1 us -> 70.6 us  [the longest x11 34.4 us: advance(): self.value = total.astype(jnp.bfloat16)]
  transfers between devices with their start and end apart: 16 -> 42, of which waited for: 13 -> 20; matrix products, arithmetic and copies ran while one was open for 17% -> 29% of each run, Pallas kernels for 0% -> 0%
where the time goes in v1:
time: 1370 us; the launch traced here: 1350 us
  waiting for transfers between devices  557 us (41%)
  starting transfers between devices  189 us (14%)
  matrix products  181 us (13%)
  local copies, waits for them, and re-layouts  143 us (10%)
  other arithmetic  139 us (10%)
  blocking collectives  123 us (9%)
  between operations  16.1 us (1%)
    ppermute x21, waiting for transfers between devices, send(): self.flying = lax.ppermute(self.value, 'sp', self.hops[self.at][0])  216 us
    ppermute x1, waiting for transfers between devices, layer(): swapped = lax.ppermute(sent, 'fsdp', swap)  109 us
    all_gather x5, waiting for transfers between devices, gather_rows(): return lax.all_gather(array, 'fsdp', axis=0, tiled=True)  108 us
    all_gather x1, blocking collectives, layer(): lax.all_gather(terms.reshape(1, -1), ('fsdp', 'sp'), axis=0, tiled=True)  94.8 us
    all_to_all x1, starting transfers between devices, layer(): lax.all_to_all(grad_attended, 'sp', split_axis=1, concat_axis=0, tiled=True)  92.5 us
    all_to_all x1, waiting for transfers between devices, layer(): lax.all_to_all(grad_value_send, 'sp', split_axis=0, concat_axis=1, tiled=...  56.9 us
    ppermute x21, starting transfers between devices, send(): self.flying = lax.ppermute(self.value, 'sp', self.hops[self.at][0])  53 us
    dot_general x4, matrix products, product_nt(): lax.dot_general(inputs, weight, (((1,), (1,)), ((), ())), preferred_eleme...  50.1 us
  transfers between devices with their start and end apart: 42, of which 20 were waited for; matrix products, arithmetic and copies ran while one was open for 29% of the time, Pallas kernels for 0%

profile of v1, /device:TPU:0, one launch (start us, length us, event | category | flops | bytes accessed | tf_op | source)
XLA Modules:
  0.0 1347.9 jit_solution(5316229457291615094)
XLA Ops:
  14.3 88.1 %all-gather.8.cloned.1.call-done = bf16[4096,2048]{1,0:T(8,128)(2,1)} async-done(((bf16[512,2048]{1,0:T(8,128)(2,1)}), bf16[4096,2048]{1,0:T(8,128)(2,1)}) %all-gather.8.cloned.1.call-update) | async-done | bytes 16777232 | tf_op jit(solution)/shard_map/all_gather | solution.py:125
  104.3 12.6 fusion.55
  176.9 14.4 %all-to-all-done = bf16[8,256,768]{2,1,0:T(8,128)(2,1)} async-done(((bf16[8,256,768]{2,1,0:T(8,128)(2,1)}), bf16[8,256,768]{2,1,0:T(8,128)(2,1)}, u32[]{:S(2)}, u32[]{:S(2)}) %all-to-all-start) | async-done | bytes 3145760 | tf_op jit(solution)/shard_map/all_to_all | solution.py:228
  199.6 10.1 all-to-all-done.3
  214.3 11.2 all-to-all-done.1
  269.8 28.6 %all_to_all.151 = bf16[4,256,512]{1,2,0:T(8,128)(2,1)} all-to-all(bf16[4,256,512]{1,2,0:T(8,128)(2,1)S(1)} %copy.311), channel_id=1, replica_groups=mesh['fsdp'=8,'sp'=4] {'sp'}, dimensions={0} | all-to-all | bytes 2097152 | tf_op jit(solution)/shard_map/all_to_all | solution.py:258
  314.7 108.9 %collective-permute-done = bf16[768,2048]{1,0:T(8,128)(2,1)} collective-permute-done((bf16[768,2048]{1,0:T(8,128)(2,1)}, bf16[768,2048]{1,0:T(8,128)(2,1)}, u32[]{:S(2)}, u32[]{:S(2)}) %collective-permute-start) | collective-permute-done | bytes 3145760 | tf_op jit(solution)/shard_map/ppermute | solution.py:225
  423.6 19.8 %fusion.5 = f32[2048,1536]{0,1:T(8,128)} fusion(bf16[2048,2048]{1,0:T(8,128)(2,1)} %all-gather.12.cloned.1.call-done, bf16[768,2048]{1,0:T(8,128)(2,1)} %collective-permute-done, bf16[768,2048]{1,0:T(8,128)(2,1)} %get-tuple-element.81), kind=kOutput, calls=%fused_computation.33 | convolution fusion | flops 12897484800 | bytes 27262976 | tf_op jit(solution)/shard_map/dot_general | solution.py:129
  443.3 20.0 %all-gather.14.cloned.1.call-done = bf16[2048,2048]{1,0:T(8,128)(2,1)} async-done(((bf16[256,2048]{1,0:T(8,128)(2,1)}), bf16[2048,2048]{1,0:T(8,128)(2,1)}) %all-gather.14.cloned.1.call-update) | async-done | bytes 8388624 | tf_op jit(solution)/shard_map/all_gather | solution.py:125
  463.3 19.2 %select_convert_fusion.1 = (bf16[2048,768]{0,1:T(8,128)(2,1)}, bf16[2048,768]{0,1:T(8,128)(2,1)}, f32[2048,768]{0,1:T(8,128)}, f32[2048,768]{0,1:T(8,128)}) fusion(pred[]{:T(512)S(6)} %eq.4, f32[2048,1536]{0,1:T(8,128)} %fusion.5, bf16[2048,2048]{1,0:T(8,128)(2,1)} %all-gather.14.cloned.1.call-done, bf16[2048,768]{1,0:T(8,128)(2,1)} %bitcast.22), kind=kOutput, calls=%fused_computation.15 | convolution fusion | flops 6466043904 | bytes 42991616 | tf_op jit(solution)/shard_map/dot_general | solution.py:267
  490.0 18.7 %convolution_convert_fusion.2 = bf16[2048,2048]{1,0:T(8,128)(2,1)} fusion(bf16[2048,768]{0,1:T(8,128)(2,1)S(1)} %select_convert_fusion, bf16[2048,768]{0,1:T(8,128)(2,1)} %get-tuple-element.72, bf16[768,2048]{1,0:T(8,128)(2,1)} %collective-permute-done, bf16[768,2048]{1,0:T(8,128)(2,1)S(1)} %copy-done.47), kind=kOutput, calls=%fused_computation.6 | convolution fusion | flops 12914262016 | bytes 20971520 | tf_op jit(solution)/shard_map/dot_general | solution.py:279
  518.6 11.2 convolution_convert_fusion.5
  530.6 10.2 convolution_convert_fusion.3
  551.1 10.4 convolution_convert_fusion.4
  561.5 19.9 %reduce-scatter.4.cloned.1.call-done = bf16[256,2048]{1,0:T(8,128)(2,1)} async-done(((bf16[2048,2048]{1,0:T(8,128)(2,1)}), bf16[256,2048]{1,0:T(8,128)(2,1)}) %reduce-scatter.4.cloned.1.call-update) | async-done | bytes 1048592 | tf_op jit(solution)/shard_map/reduce_scatter | solution.py:141
  591.5 51.4 %collective-permute-done.13 = bf16[384,2048]{1,0:T(8,128)(2,1)} collective-permute-done((bf16[384,2048]{1,0:T(8,128)(2,1)}, bf16[384,2048]{1,0:T(8,128)(2,1)}, u32[]{:S(2)}, u32[]{:S(2)}) %collective-permute-start.13) | collective-permute-done | bytes 1572896 | tf_op jit(solution)/shard_map/ppermute | solution.py:165
  662.0 92.5 %all-to-all-start.5 = ((bf16[256,4,512]{2,0,1:T(8,128)(2,1)}), bf16[256,4,512]{2,0,1:T(8,128)(2,1)S(1)}, u32[]{:S(2)}, u32[]{:S(2)}) async-start(bf16[256,4,512]{2,0,1:T(8,128)(2,1)} %bitcast.220), calls=%async_computation.6 | async-start | bytes 2097152 | tf_op jit(solution)/shard_map/all_to_all | solution.py:290
  759.8 29.7 %collective-permute-done.12 = bf16[384,2048]{1,0:T(8,128)(2,1)} collective-permute-done((bf16[384,2048]{1,0:T(8,128)(2,1)}, bf16[384,2048]{1,0:T(8,128)(2,1)}, u32[]{:S(2)}, u32[]{:S(2)}) %collective-permute-start.12) | collective-permute-done | bytes 1572896 | tf_op jit(solution)/shard_map/ppermute | solution.py:165
  794.3 13.3 collective-permute-start.16
  855.0 20.2 %collective-permute-done.19 = bf16[384,2048]{1,0:T(8,128)(2,1)} collective-permute-done((bf16[384,2048]{1,0:T(8,128)(2,1)}, bf16[384,2048]{1,0:T(8,128)(2,1)}, u32[]{:S(2)}, u32[]{:S(2)}) %collective-permute-start.19) | collective-permute-done | bytes 1572896 | tf_op jit(solution)/shard_map/ppermute | solution.py:165
  891.0 11.5 convolution_convert_fusion.1
  905.7 56.9 %all-to-all-done.8 = bf16[4,256,256]{2,1,0:T(8,128)(2,1)} async-done(((bf16[4,256,256]{2,1,0:T(8,128)(2,1)}), bf16[4,256,256]{2,1,0:T(8,128)(2,1)}, u32[]{:S(2)}, u32[]{:S(2)}) %all-to-all-start.8) | async-done | bytes 524320 | tf_op jit(solution)/shard_map/all_to_all | solution.py:325
  1029.5 19.4 %collective-permute-done.18 = bf16[384,2048]{1,0:T(8,128)(2,1)} collective-permute-done((bf16[384,2048]{1,0:T(8,128)(2,1)}, bf16[384,2048]{1,0:T(8,128)(2,1)}, u32[]{:S(2)}, u32[]{:S(2)}) %collective-permute-start.18) | collective-permute-done | bytes 1572896 | tf_op jit(solution)/shard_map/ppermute | solution.py:165
  1050.5 27.6 %collective-permute-done.21 = bf16[384,2048]{1,0:T(8,128)(2,1)} collective-permute-done((bf16[384,2048]{1,0:T(8,128)(2,1)}, bf16[384,2048]{1,0:T(8,128)(2,1)}, u32[]{:S(2)}, u32[]{:S(2)}) %collective-permute-start.21) | collective-permute-done | bytes 1572896 | tf_op jit(solution)/shard_map/ppermute | solution.py:165
  1087.9 8.6 convolution_convert_fusion.6
  1099.8 11.8 fusion.23
  1111.7 10.2 collective-permute-done.1
  1121.9 22.1 %collective-permute-done.4 = bf16[256,2048]{1,0:T(8,128)(2,1)S(1)} collective-permute-done((bf16[256,2048]{1,0:T(8,128)(2,1)S(1)}, bf16[256,2048]{1,0:T(8,128)(2,1)S(1)}, u32[]{:S(2)}, u32[]{:S(2)}) %collective-permute-start.4) | collective-permute-done | bytes 1048608 | tf_op jit(solution)/shard_map/ppermute | solution.py:165
  1147.8 94.8 %all-gather.1 = f32[32,1,4352]{2,1,0:T(1,128)} all-gather(f32[1,1,4352]{2,1,0:T(1,128)S(1)} %reshape.394), channel_id=2, replica_groups=mesh['fsdp'=8,'sp'=4] {'fsdp','sp'}, dimensions={0}, use_global_device_ids=true | all-gather | bytes 574464 | tf_op jit(solution)/shard_map/all_gather | solution.py:390
  1254.7 8.7 reshape.391
  1298.2 12.6 collective-permute-done.6
  1322.8 15.4 %collective-permute-done.9 = bf16[256,2048]{1,0:T(8,128)(2,1)} collective-permute-done((bf16[256,2048]{1,0:T(8,128)(2,1)}, bf16[256,2048]{1,0:T(8,128)(2,1)}, u32[]{:S(2)}, u32[]{:S(2)}) %collective-permute-start.9) | collective-permute-done | bytes 1048608 | tf_op jit(solution)/shard_map/ppermute | solution.py:165
  (451 shorter events, 421.9 us)
Async XLA Ops:
  7.2 95.2 %all-gather.8.cloned.1.call-start = ((), (), s32[]{:S(2)}) async-start(), calls=%async_computation.14 | async-start | bytes 18874368 | tf_op jit(solution)/shard_map/all_gather | solution.py:125
  7.9 290.5 %all-gather.10.cloned.1.call-start = ((), (), s32[]{:S(2)}) async-start(), calls=%async_computation.15 | async-start | bytes 9437184 | tf_op jit(solution)/shard_map/all_gather | solution.py:125
  132.9 58.4 %all-to-all-start = ((bf16[8,256,768]{2,1,0:T(8,128)(2,1)}), bf16[8,256,768]{2,1,0:T(8,128)(2,1)}, u32[]{:S(2)}, u32[]{:S(2)}) async-start(bf16[8,256,768]{2,1,0:T(8,128)(2,1)} %bitcast.195), calls=%async_computation | async-start | bytes 6291456 | tf_op jit(solution)/shard_map/all_to_all | solution.py:228
  229.0 194.6 %all-gather.12.cloned.1.call-start = ((), (), s32[]{:S(2)}) async-start(), calls=%async_computation.16 | async-start | bytes 9437184 | tf_op jit(solution)/shard_map/all_gather | solution.py:125
  306.0 157.4 %all-gather.14.cloned.1.call-start = ((), (), s32[]{:S(2)}) async-start(), calls=%async_computation.17 | async-start | bytes 9437184 | tf_op jit(solution)/shard_map/all_gather | solution.py:125
  306.6 274.8 %reduce-scatter.4.cloned.1.call-start = ((), (), s32[]{:S(2)}) async-start(), calls=%async_computation.18 | async-start | bytes 9437184 | tf_op jit(solution)/shard_map/reduce_scatter | solution.py:141
  313.3 110.3 %collective-permute-start = (bf16[768,2048]{1,0:T(8,128)(2,1)}, bf16[768,2048]{1,0:T(8,128)(2,1)}, u32[]{:S(2)}, u32[]{:S(2)}) collective-permute-start(bf16[768,2048]{1,0:T(8,128)(2,1)} %get-tuple-element.82), channel_id=1, source_target_pairs={{0,16},{4,20},{8,24},{12,28},{16,0},{20,4},{24,8},{28,12},{1,17},{... | collective-permute-start | bytes 9437192 | tf_op jit(solution)/shard_map/ppermute | solution.py:225
  508.8 520.7 %all-reduce.2.cloned.1.call-start = ((), (), s32[]{:S(2)}) async-start(), calls=%async_computation.22 | async-start | bytes 6291456 | tf_op jit(solution)/shard_map/psum | solution.py:284
  529.8 558.0 %all-gather.16.cloned.1.call-start = ((), (), s32[]{:S(2)}) async-start(), calls=%async_computation.20 | async-start | bytes 9437184 | tf_op jit(solution)/shard_map/all_gather | solution.py:125
  530.6 741.3 %reduce-scatter.8.cloned.1.call-start = ((), (), s32[]{:S(2)}) async-start(), calls=%async_computation.21 | async-start | bytes 9437184 | tf_op jit(solution)/shard_map/reduce_scatter | solution.py:141
  544.1 47.4 %collective-permute-start.10 = (bf16[384,2048]{1,0:T(8,128)(2,1)}, bf16[384,2048]{1,0:T(8,128)(2,1)}, u32[]{:S(2)}, u32[]{:S(2)}) collective-permute-start(bf16[384,2048]{1,0:T(8,128)(2,1)} %get-tuple-element.85), channel_id=1, source_target_pairs={{0,1},{3,2},{4,5},{7,6},{8,9},{11,10},{12,13},{15,14},{16,17},{19,... | collective-permute-start | bytes 4718600 | tf_op jit(solution)/shard_map/ppermute | solution.py:165
  548.6 94.2 %collective-permute-start.13 = (bf16[384,2048]{1,0:T(8,128)(2,1)}, bf16[384,2048]{1,0:T(8,128)(2,1)}, u32[]{:S(2)}, u32[]{:S(2)}) collective-permute-start(bf16[384,2048]{1,0:T(8,128)(2,1)} %get-tuple-element.86), channel_id=1, source_target_pairs={{0,1},{3,2},{4,5},{7,6},{8,9},{11,10},{12,13},{15,14},{16,17},{19,... | collective-permute-start | bytes 4718600 | tf_op jit(solution)/shard_map/ppermute | solution.py:165
  649.1 105.4 %collective-permute-start.14 = (bf16[384,2048]{1,0:T(8,128)(2,1)}, bf16[384,2048]{1,0:T(8,128)(2,1)}, u32[]{:S(2)}, u32[]{:S(2)}) collective-permute-start(bf16[384,2048]{1,0:T(8,128)(2,1)} %get-tuple-element.84), channel_id=1, source_target_pairs={{1,2},{2,1},{5,6},{6,5},{9,10},{10,9},{13,14},{14,13},{17,18},{18,... | collective-permute-start | bytes 4718600 | tf_op jit(solution)/shard_map/ppermute | solution.py:165
  652.8 136.7 %collective-permute-start.12 = (bf16[384,2048]{1,0:T(8,128)(2,1)}, bf16[384,2048]{1,0:T(8,128)(2,1)}, u32[]{:S(2)}, u32[]{:S(2)}) collective-permute-start(bf16[384,2048]{1,0:T(8,128)(2,1)} %add_convert_fusion.6), channel_id=1, source_target_pairs={{1,0},{2,3},{5,4},{6,7},{9,8},{10,11},{13,12},{14,15},{17,16},{18,... | collective-permute-start | bytes 4718600 | tf_op jit(solution)/shard_map/ppermute | solution.py:165
  662.0 148.0 %all-to-all-start.5 = ((bf16[256,4,512]{2,0,1:T(8,128)(2,1)}), bf16[256,4,512]{2,0,1:T(8,128)(2,1)S(1)}, u32[]{:S(2)}, u32[]{:S(2)}) async-start(bf16[256,4,512]{2,0,1:T(8,128)(2,1)} %bitcast.220), calls=%async_computation.6 | async-start | bytes 2097152 | tf_op jit(solution)/shard_map/all_to_all | solution.py:290
  758.3 268.4 %collective-permute-start.15 = (bf16[384,2048]{1,0:T(8,128)(2,1)}, bf16[384,2048]{1,0:T(8,128)(2,1)}, u32[]{:S(2)}, u32[]{:S(2)}) collective-permute-start(bf16[384,2048]{1,0:T(8,128)(2,1)} %add_convert_fusion.4), channel_id=1, source_target_pairs={{1,0},{2,3},{5,4},{6,7},{9,8},{10,11},{13,12},{14,15},{17,16},{18,... | collective-permute-start | bytes 4718600 | tf_op jit(solution)/shard_map/ppermute | solution.py:165
  794.3 60.7 %collective-permute-start.16 = (bf16[384,2048]{1,0:T(8,128)(2,1)}, bf16[384,2048]{1,0:T(8,128)(2,1)}, u32[]{:S(2)}, u32[]{:S(2)}) collective-permute-start(bf16[384,2048]{1,0:T(8,128)(2,1)} %get-tuple-element.89), channel_id=1, source_target_pairs={{0,1},{3,2},{4,5},{7,6},{8,9},{11,10},{12,13},{15,14},{16,17},{19,... | collective-permute-start | bytes 4718600 | tf_op jit(solution)/shard_map/ppermute | solution.py:165
  807.5 67.6 %collective-permute-start.19 = (bf16[384,2048]{1,0:T(8,128)(2,1)}, bf16[384,2048]{1,0:T(8,128)(2,1)}, u32[]{:S(2)}, u32[]{:S(2)}) collective-permute-start(bf16[384,2048]{1,0:T(8,128)(2,1)} %get-tuple-element.90), channel_id=1, source_target_pairs={{0,1},{3,2},{4,5},{7,6},{8,9},{11,10},{12,13},{15,14},{16,17},{19,... | collective-permute-start | bytes 4718600 | tf_op jit(solution)/shard_map/ppermute | solution.py:165
  837.8 47.2 %all-to-all-start.7 = ((bf16[4,256,256]{2,1,0:T(8,128)(2,1)}), bf16[4,256,256]{2,1,0:T(8,128)(2,1)S(1)}, u32[]{:S(2)}, u32[]{:S(2)}) async-start(bf16[4,256,256]{2,1,0:T(8,128)(2,1)} %copy.360), calls=%async_computation.9 | async-start | bytes 1048576 | tf_op jit(solution)/shard_map/all_to_all | solution.py:324
  881.3 124.3 %collective-permute-start.17 = (bf16[384,2048]{1,0:T(8,128)(2,1)}, bf16[384,2048]{1,0:T(8,128)(2,1)}, u32[]{:S(2)}, u32[]{:S(2)}) collective-permute-start(bf16[384,2048]{1,0:T(8,128)(2,1)} %get-tuple-element.87), channel_id=1, source_target_pairs={{1,2},{2,1},{5,6},{6,5},{9,10},{10,9},{13,14},{14,13},{17,18},{18,... | collective-permute-start | bytes 4718600 | tf_op jit(solution)/shard_map/ppermute | solution.py:165
  883.1 127.6 %collective-permute-start.20 = (bf16[384,2048]{1,0:T(8,128)(2,1)}, bf16[384,2048]{1,0:T(8,128)(2,1)}, u32[]{:S(2)}, u32[]{:S(2)}) collective-permute-start(bf16[384,2048]{1,0:T(8,128)(2,1)} %get-tuple-element.88), channel_id=1, source_target_pairs={{1,2},{2,1},{5,6},{6,5},{9,10},{10,9},{13,14},{14,13},{17,18},{18,... | collective-permute-start | bytes 4718600 | tf_op jit(solution)/shard_map/ppermute | solution.py:165
  885.0 77.6 %all-to-all-start.8 = ((bf16[4,256,256]{2,1,0:T(8,128)(2,1)}), bf16[4,256,256]{2,1,0:T(8,128)(2,1)}, u32[]{:S(2)}, u32[]{:S(2)}) async-start(bf16[4,256,256]{2,1,0:T(8,128)(2,1)} %copy.362), calls=%async_computation.10 | async-start | bytes 1048576 | tf_op jit(solution)/shard_map/all_to_all | solution.py:325
  891.0 426.6 %reduce-scatter.6.cloned.1.call-start = ((), (), s32[]{:S(2)}) async-start(), calls=%async_computation.19 | async-start | bytes 9437184 | tf_op jit(solution)/shard_map/reduce_scatter | solution.py:141
  1009.4 39.5 %collective-permute-start.18 = (bf16[384,2048]{1,0:T(8,128)(2,1)}, bf16[384,2048]{1,0:T(8,128)(2,1)}, u32[]{:S(2)}, u32[]{:S(2)}) collective-permute-start(bf16[384,2048]{1,0:T(8,128)(2,1)} %add_convert_fusion.2), channel_id=1, source_target_pairs={{1,0},{2,3},{5,4},{6,7},{9,8},{10,11},{13,12},{14,15},{17,16},{18,... | collective-permute-start | bytes 4718600 | tf_op jit(solution)/shard_map/ppermute | solution.py:165
  1014.6 63.4 %collective-permute-start.21 = (bf16[384,2048]{1,0:T(8,128)(2,1)}, bf16[384,2048]{1,0:T(8,128)(2,1)}, u32[]{:S(2)}, u32[]{:S(2)}) collective-permute-start(bf16[384,2048]{1,0:T(8,128)(2,1)} %add_convert_fusion), channel_id=1, source_target_pairs={{1,0},{2,3},{5,4},{6,7},{9,8},{10,11},{13,12},{14,15},{17,16},{18,... | collective-permute-start | bytes 4718600 | tf_op jit(solution)/shard_map/ppermute | solution.py:165
  1022.0 60.9 %all-to-all-start.9 = ((bf16[256,8,512]{2,0,1:T(8,128)(2,1)}), bf16[256,8,512]{2,0,1:T(8,128)(2,1)}, u32[]{:S(2)}, u32[]{:S(2)}) async-start(bf16[256,8,512]{2,0,1:T(8,128)(2,1)} %bitcast.206), calls=%async_computation.11 | async-start | bytes 4194304 | tf_op jit(solution)/shard_map/all_to_all | solution.py:347
  1081.7 196.7 %collective-permute-start.22 = (bf16[768,2048]{1,0:T(8,128)(2,1)}, bf16[768,2048]{1,0:T(8,128)(2,1)}, u32[]{:S(2)}, u32[]{:S(2)}) collective-permute-start(bf16[768,2048]{1,0:T(8,128)(2,1)} %pad_maximum_fusion.4), channel_id=1, source_target_pairs={{0,16},{4,20},{8,24},{12,28},{16,0},{20,4},{24,8},{28,12},{1,17},{... | collective-permute-start | bytes 9437192 | tf_op jit(solution)/shard_map/ppermute | solution.py:358
  1082.9 164.1 %all-to-all-start.10 = ((bf16[8,256,768]{2,1,0:T(8,128)(2,1)}), bf16[8,256,768]{2,1,0:T(8,128)(2,1)}, u32[]{:S(2)}, u32[]{:S(2)}) async-start(bf16[8,256,768]{2,1,0:T(8,128)(2,1)} %bitcast.231), calls=%async_computation.13 | async-start | bytes 6291456 | tf_op jit(solution)/shard_map/all_to_all | solution.py:367
  1098.4 45.6 %collective-permute-start.4 = (bf16[256,2048]{1,0:T(8,128)(2,1)S(1)}, bf16[256,2048]{1,0:T(8,128)(2,1)S(1)}, u32[]{:S(2)}, u32[]{:S(2)}) collective-permute-start(bf16[256,2048]{1,0:T(8,128)(2,1)S(1)} %get-tuple-element.94), channel_id=1, source_target_pairs={{0,1},{3,2},{4,5},{7,6},{8,9},{11,10},{12,13},{15,14},{16,17},{19,... | collective-permute-start | bytes 3145736 | tf_op jit(solution)/shard_map/ppermute | solution.py:165
  1146.1 117.3 %collective-permute-start.2 = (bf16[256,2048]{1,0:T(8,128)(2,1)}, bf16[256,2048]{1,0:T(8,128)(2,1)}, u32[]{:S(2)}, u32[]{:S(2)}) collective-permute-start(bf16[256,2048]{1,0:T(8,128)(2,1)} %get-tuple-element.91), channel_id=1, source_target_pairs={{1,2},{2,1},{5,6},{6,5},{9,10},{10,9},{13,14},{14,13},{17,18},{18,... | collective-permute-start | bytes 3145736 | tf_op jit(solution)/shard_map/ppermute | solution.py:165
  1266.3 30.5 %collective-permute-start.3 = (bf16[256,2048]{1,0:T(8,128)(2,1)}, bf16[256,2048]{1,0:T(8,128)(2,1)}, u32[]{:S(2)}, u32[]{:S(2)}) collective-permute-start(bf16[256,2048]{1,0:T(8,128)(2,1)} %add_convert_fusion.12), channel_id=1, source_target_pairs={{1,0},{2,3},{5,4},{6,7},{9,8},{10,11},{13,12},{14,15},{17,16},{18,... | collective-permute-start | bytes 3145736 | tf_op jit(solution)/shard_map/ppermute | solution.py:165
  1270.5 40.3 %collective-permute-start.6 = (bf16[256,2048]{1,0:T(8,128)(2,1)}, bf16[256,2048]{1,0:T(8,128)(2,1)}, u32[]{:S(2)}, u32[]{:S(2)}) collective-permute-start(bf16[256,2048]{1,0:T(8,128)(2,1)} %add_convert_fusion.10), channel_id=1, source_target_pairs={{1,0},{2,3},{5,4},{6,7},{9,8},{10,11},{13,12},{14,15},{17,16},{18,... | collective-permute-start | bytes 3145736 | tf_op jit(solution)/shard_map/ppermute | solution.py:165
  (111 other events, 1863.2 us)
Sparse Core Ops, SparseCore 0:
  9.9 92.4 all-gather.7
  104.2 78.6 all-gather.9
  306.1 91.5 all-gather.11
  399.5 63.8 all-gather.13
  508.9 72.3 reduce-scatter.3
  583.6 171.0 all-reduce.1
  757.1 53.1 all-gather.15
  814.3 71.4 reduce-scatter.7
  902.6 72.9 reduce-scatter.5

commit v2 on v1

--- a/solution.py
+++ b/solution.py
@@ -114,7 +114,7 @@
         )
         if key_total is None:
             key_total, value_total = key_part, value_part
-            between(grad_query[0])
+            grad_mixed, key_total = between((grad_mixed, key_total))
         else:
             key_total = key_total.at[:stop].add(key_part)
             value_total = value_total.at[:stop].add(value_part)
@@ -148,6 +148,7 @@
         half = count // 2
         self.count = count
         self.value = partial.astype(jnp.bfloat16)
+        self.flying = None
         self.hops = []
         if count % 2 == 0:
             for s in range(half - 1):
@@ -158,31 +159,69 @@
         elif count > 1:
             self.value = lax.psum(self.value, "sp")
         self.at = 0
-        self.send()
 
     def send(self):
         if self.at < len(self.hops):
             self.flying = lax.ppermute(self.value, "sp", self.hops[self.at][0])
 
-    def advance(self):
-        if self.at >= len(self.hops):
-            return
-        arrived = self.flying
+    def take(self):
         depth = self.hops[self.at][1]
         if depth is None:
-            total = self.value.astype(jnp.float32) + arrived.astype(jnp.float32)
+            total = self.value.astype(jnp.float32) + self.flying.astype(jnp.float32)
             self.value = total.astype(jnp.bfloat16)
         else:
             place = lax.axis_index("sp")
             mine = jnp.minimum(place, self.count - 1 - place) == depth
-            self.value = jnp.where(mine, arrived, self.value)
+            self.value = jnp.where(mine, self.flying, self.value)
         self.at += 1
-        self.send()
+        self.flying = None
 
     def finish(self):
         while self.at < len(self.hops):
-            self.advance()
+            if self.flying is None:
+                self.send()
+            self.take()
         return self.value
+
+
+def meet(values, moving, starting=()):
+    moving = [c for c in moving if c.flying is not None]
+    tied = lax.optimization_barrier(
+        (values, [c.flying for c in moving], [c.value for c in starting])
+    )
+    for chain, arrived in zip(moving, tied[1]):
+        chain.flying = arrived
+        chain.take()
+        chain.send()
+    for chain, value in zip(starting, tied[2]):
+        chain.value = value
+        chain.send()
+    return tied[0]
+
+
+def turn(blocks, ways):
+    me = lax.axis_index("fsdp")
+    result = lax.dynamic_update_slice_in_dim(
+        jnp.zeros_like(blocks), lax.dynamic_slice_in_dim(blocks, me, 1, 0), me, 0
+    )
+    for shift in range(1, ways):
+        block = lax.dynamic_slice_in_dim(blocks, (me + shift) % ways, 1, 0)
+        pairs = [(f, (f + shift) % ways) for f in range(ways)]
+        arrived = lax.ppermute(block, "fsdp", pairs)
+        result = lax.dynamic_update_slice_in_dim(result, arrived, (me - shift) % ways, 0)
+    return result
+
+
+def sum_all(values, sizes):
+    for axis, size in sizes:
+        if size & (size - 1):
+            values = lax.psum(values, axis)
+            continue
+        step = 1
+        while step < size:
+            values = values + lax.ppermute(values, axis, [(d, d ^ step) for d in range(size)])
+            step *= 2
+    return values
 
 
 def halves(array):
@@ -225,9 +264,7 @@
     swapped = lax.ppermute(sent, "fsdp", swap)
     gate_up_own = jnp.concatenate([kept, swapped], 0)
     down_split = down_late.reshape(-1, pairs_of, 2, units).transpose(2, 1, 0, 3)
-    down_turned = lax.all_to_all(
-        down_split.reshape(ways, -1, units), "fsdp", split_axis=0, concat_axis=0, tiled=True
-    )
+    down_own = turn(down_split.reshape(ways, -1, units), ways).reshape(width, units)
     hidden = hidden_in.astype(f32)
     normed1, inverse1 = rms_forward(hidden, attn_gain)
     normed1_low = normed1.astype(low)
@@ -240,10 +277,6 @@
     key_normed, key_inverse = rms_forward(key, key_gain)
     query_low = rotate(query_normed, cosine, sine).astype(low).reshape(rows, H * HD)
     key_low = rotate(key_normed, cosine, sine).astype(low).reshape(rows, KV * HD)
-    query_low, key_low, value_low, down_turned = lax.optimization_barrier(
-        (query_low, key_low, value_low, down_turned)
-    )
-    down_own = down_turned.reshape(width, units)
     query_heads, key_heads, value_heads = (
         lax.all_to_all(query_low, "sp", split_axis=1, concat_axis=0, tiled=True),
         lax.all_to_all(key_low, "sp", split_axis=1, concat_axis=0, tiled=True),
@@ -277,30 +310,23 @@
     grad_second = jnp.where(side == 0, grad_upper, grad_gate).astype(low)
     grad_both = jnp.concatenate([grad_first, grad_second], 1)
     grad_normed2 = scatter_sum(jnp.dot(grad_both, gate_up_own, preferred_element_type=f32))
+    grad_sent = product_tn(grad_second, normed2_all).astype(low)
+    s0, s1 = (Chain(part, line) for part in halves(grad_sent))
+    s0.send()
+    s1.send()
+    grad_down_own = product_tn(cotangent_all, activation).astype(low)
     grad_kept = product_tn(grad_first, normed2_all).astype(low)
-    grad_sent = product_tn(grad_second, normed2_all).astype(low)
-    grad_down_own = product_tn(cotangent_all, activation).astype(low)
-    kept_chains = [Chain(part, line) for part in halves(grad_kept)]
-    grad_down_sum = lax.psum(grad_down_own, "sp")
+    grad_kept, grad_down_own = meet((grad_kept, grad_down_own), [s0])
+    d0, d1 = (Chain(part, line) for part in halves(grad_down_own))
+    k0, k1 = (Chain(part, line) for part in halves(grad_kept))
 
     back_two, mlp_term = rms_backward(middle, inverse2, mlp_gain, grad_normed2)
     grad_middle = cotangent.astype(f32) + back_two
     grad_mixed_low = grad_middle.astype(low)
     grad_attended = jnp.dot(grad_mixed_low, out_full, preferred_element_type=f32).astype(low)
     grad_heads = lax.all_to_all(grad_attended, "sp", split_axis=1, concat_axis=0, tiled=True)
-    grad_sent, grad_mixed_low = lax.optimization_barrier((grad_sent, grad_mixed_low))
+    grad_mixed_low = meet(grad_mixed_low, [s1], [d0])
     grad_out = scatter_sum(product_tn(grad_mixed_low, attended))
-    sent_chains = [Chain(part, line) for part in halves(grad_sent)]
-    for chain in kept_chains:
-        chain.advance()
-
-    def between(value):
-        for chain in kept_chains:
-            chain.advance()
-
-    activation_late, grad_heads = lax.optimization_barrier((activation, grad_heads))
-    hidden_out = (middle + scatter_sum(product_nt(activation_late, down_own))).astype(low)
-
     grad_query_local, grad_keys, grad_values = attention_backward(
         query_local,
         keys_local,
@@ -308,7 +334,7 @@
         mixed_heads,
         logsums,
         grad_heads.reshape(length, -1, HD),
-        between,
+        lambda values: meet(values, [s0], [d1]),
     )
     grad_query_send = grad_query_local.astype(low).reshape(length, -1)
     grad_key_send = (
@@ -317,13 +343,16 @@
     grad_value_send = (
         grad_values.reshape(length, local_kv, group, HD).sum(2).astype(low).reshape(length, -1)
     )
-    for chain in sent_chains:
-        chain.advance()
-    grad_query_low, grad_key_low, grad_value_low = (
-        lax.all_to_all(grad_query_send, "sp", split_axis=0, concat_axis=1, tiled=True),
-        lax.all_to_all(grad_key_send, "sp", split_axis=0, concat_axis=1, tiled=True),
-        lax.all_to_all(grad_value_send, "sp", split_axis=0, concat_axis=1, tiled=True),
-    )
+    grads_send = jnp.concatenate([grad_query_send, grad_key_send, grad_value_send], 1)
+    grads_send, activation = meet((grads_send, activation), [s1, d0], [k0])
+    grads_low = lax.all_to_all(grads_send, "sp", split_axis=0, concat_axis=1, tiled=True)
+    hidden_out = (middle + scatter_sum(product_nt(activation, down_own))).astype(low)
+    grads_low = meet(grads_low, [s0, d1], [k1])
+    grads_low = grads_low.reshape(rows, line, -1)
+    cuts = (grad_query_send.shape[1], grad_query_send.shape[1] + grad_key_send.shape[1])
+    grad_query_low = grads_low[:, :, : cuts[0]]
+    grad_key_low = grads_low[:, :, cuts[0] : cuts[1]]
+    grad_value_low = grads_low[:, :, cuts[1] :].reshape(rows, KV * HD)
     grad_query, query_term = rms_backward(
         query,
         query_inverse,
@@ -345,17 +374,44 @@
         1,
     )
     grad_columns = lax.all_to_all(grad_projected, "fsdp", split_axis=1, concat_axis=0, tiled=True)
-    for chain in sent_chains:
-        chain.advance()
-    grad_qkv_own = product_tn(grad_columns, normed1_all)
-    qkv_chains = [Chain(part, line) for part in halves(grad_qkv_own)]
     out_chain = Chain(grad_out, line)
+    grad_columns = meet(grad_columns, [d0, k0, s1], [out_chain])
     grad_normed1 = jnp.dot(grad_projected, qkv_full, preferred_element_type=f32)
+    grad_qkv_own = product_tn(grad_columns, normed1_all).astype(low)
     back_one, attn_term = rms_backward(hidden, inverse1, attn_gain, grad_normed1)
     grad_input = grad_middle + back_one
-    grad_kept = jnp.concatenate([chain.finish() for chain in kept_chains], 0)
-    grad_sent = jnp.concatenate([chain.finish() for chain in sent_chains], 0)
-    grad_swapped = lax.ppermute(grad_sent, "fsdp", swap)
+    terms = jnp.concatenate(
+        [
+            jnp.sum(attn_term, axis=0),
+            jnp.sum(mlp_term, axis=0),
+            jnp.sum(query_term, axis=(0, 1)),
+            jnp.sum(key_term, axis=(0, 1)),
+        ]
+    )
+    grad_qkv_own, terms = meet((grad_qkv_own, terms), [d1, k1])
+    q0, q1 = (Chain(part, line) for part in halves(grad_qkv_own))
+    q0.send()
+    q1.send()
+    sums = sum_all(terms, (("fsdp", ways), ("sp", line)))
+    grad_swapped = []
+    for chain in (s0, s1):
+        grad_swapped.append(lax.ppermute(chain.finish(), "fsdp", swap))
+    grad_swapped = jnp.concatenate(grad_swapped, 0)
+    grad_down_sum = jnp.concatenate([d0.finish(), d1.finish()], 0)
+    down_back = lax.all_to_all(
+        grad_down_sum.reshape(ways, -1, units),
+        "fsdp",
+        split_axis=0,
+        concat_axis=0,
+        tiled=True,
+    )
+    grad_down = (
+        down_back.reshape(2, pairs_of, -1, units)
+        .transpose(2, 1, 0, 3)
+        .reshape(down_weight.shape)
+        .astype(f32)
+    )
+    grad_kept = jnp.concatenate([k0.finish(), k1.finish()], 0)
     grad_gate_up = jnp.concatenate(
         [
             jnp.where(side == 0, grad_kept, grad_swapped),
@@ -363,32 +419,8 @@
         ],
         0,
     ).astype(f32)
-    grad_down_sum, grad_projected = lax.optimization_barrier((grad_down_sum, grad_projected))
-    down_back = lax.all_to_all(
-        grad_down_sum.reshape(ways, -1, units),
-        "fsdp",
-        split_axis=0,
-        concat_axis=0,
-        tiled=True,
-    )
-    grad_down = (
-        down_back.reshape(2, pairs_of, -1, units)
-        .transpose(2, 1, 0, 3)
-        .reshape(down_weight.shape)
-        .astype(f32)
-    )
     grad_out = out_chain.finish().astype(f32)
-    grad_qkv = jnp.concatenate([chain.finish() for chain in qkv_chains], 0).astype(f32)
-    terms = jnp.concatenate(
-        [
-            jnp.sum(attn_term, axis=0),
-            jnp.sum(mlp_term, axis=0),
-            jnp.sum(query_term, axis=(0, 1)),
-            jnp.sum(key_term, axis=(0, 1)),
-        ]
-    )
-    all_terms = lax.all_gather(terms.reshape(1, -1), ("fsdp", "sp"), axis=0, tiled=True)
-    sums = jnp.sum(all_terms, axis=0)
+    grad_qkv = jnp.concatenate([q0.finish(), q1.finish()], 0).astype(f32)
     gains = (
         sums[:width],
         sums[2 * width : 2 * width + HD],

time: 1370 us -> 1280 us (0.934)
  blocking collectives: 123 us -> 28.8 us
  waiting for transfers between devices: 557 us -> 629 us
  starting transfers between devices: 189 us -> 134 us
    ppermute x1 -> x14, waiting for transfers between devices: 0.01 us -> 224 us  [the longest x7 132 us: turn(): arrived = lax.ppermute(block, 'fsdp', pairs)]
    ppermute x1, waiting for transfers between devices: 109 us -> 0.01 us  [layer(): swapped = lax.ppermute(sent, 'fsdp', swap)]
    all_gather x1 -> x0, blocking collectives: 94.8 us -> none  [layer(): lax.all_gather(terms.reshape(1, -1), ('fsdp', 'sp'), axis=0, tiled=True)]
    all_to_all x1, starting transfers between devices: 92.5 us -> 4.56 us  [layer(): lax.all_to_all(grad_attended, 'sp', split_axis=1, concat_axis=0, tiled=True)]
    all_to_all x4 -> x1, waiting for transfers between devices: 73.9 us -> 0.01 us  [layer(): lax.all_to_all(grads_send, 'sp', split_axis=0, concat_axis=1, tiled=True)]
    ppermute x21 -> x27, waiting for transfers between devices: 216 us -> 263 us  [send(): self.flying = lax.ppermute(self.value, 'sp', self.hops[self.at][0])]
    convert_element_type x12 -> x19, other arithmetic: 37 us -> 58.8 us  [the longest x16 51.1 us: take(): self.value = total.astype(jnp.bfloat16)]
    unnamed x208 -> x230, local copies, waits for them, and re-layouts: 21.3 us -> 38.6 us
  transfers between devices with their start and end apart: 42 -> 57, of which waited for: 20 -> 21; matrix products, arithmetic and copies ran while one was open for 29% -> 29% of each run, Pallas kernels for 0% -> 0%
where the time goes in v2:
time: 1280 us; the launch traced here: 1270 us
  waiting for transfers between devices  629 us (49%)
  matrix products  169 us (13%)
  local copies, waits for them, and re-layouts  146 us (11%)
  other arithmetic  146 us (11%)
  starting transfers between devices  134 us (10%)
  blocking collectives  28.8 us (2%)
  between operations  16.5 us (1%)
    ppermute x27, waiting for transfers between devices, send(): self.flying = lax.ppermute(self.value, 'sp', self.hops[self.at][0])  263 us
    ppermute x7, waiting for transfers between devices, turn(): arrived = lax.ppermute(block, 'fsdp', pairs)  132 us
    all_gather x5, waiting for transfers between devices, gather_rows(): return lax.all_gather(array, 'fsdp', axis=0, tiled=True)  94.4 us
    ppermute x27, starting transfers between devices, send(): self.flying = lax.ppermute(self.value, 'sp', self.hops[self.at][0])  66 us
    ppermute x5, waiting for transfers between devices, sum_all(): lax.ppermute(values, axis, [(d, d ^ step) for d in range(size)])  54.3 us
    convert_element_type x16, other arithmetic, take(): self.value = total.astype(jnp.bfloat16)  51.1 us
    dot_general x4, matrix products, product_nt(): lax.dot_general(inputs, weight, (((1,), (1,)), ((), ())), preferred_eleme...  43.8 us
    dot_general x5, matrix products, product_tn(): lax.dot_general(left, right, (((0,), (0,)), ((), ())), preferred_element_...  42.3 us
  transfers between devices with their start and end apart: 57, of which 21 were waited for; matrix products, arithmetic and copies ran while one was open for 29% of the time, Pallas kernels for 0%

profile of v2, /device:TPU:0, one launch (start us, length us, event | category | flops | bytes accessed | tf_op | source)
XLA Modules:
  0.0 1270.3 jit_solution(6840795871755168363)
XLA Ops:
  8.0 94.4 %all-gather.6.cloned.1.call-done = bf16[4096,2048]{1,0:T(8,128)(2,1)} async-done(((bf16[512,2048]{1,0:T(8,128)(2,1)}), bf16[4096,2048]{1,0:T(8,128)(2,1)}) %all-gather.6.cloned.1.call-update) | async-done | bytes 16777232 | tf_op jit(solution)/shard_map/all_gather | solution.py:125
  104.4 10.5 fusion.61
  181.9 8.1 all-to-all-done.1
  207.3 28.8 %all_to_all.126 = bf16[4,256,512]{1,2,0:T(8,128)(2,1)} all-to-all(bf16[4,256,512]{1,2,0:T(8,128)(2,1)S(1)} %copy.285), channel_id=1, replica_groups=mesh['fsdp'=8,'sp'=4] {'sp'}, dimensions={0} | all-to-all | bytes 2097152 | tf_op jit(solution)/shard_map/all_to_all | solution.py:291
  270.4 8.0 collective-permute-done
  282.2 106.6 %collective-permute-done.2 = bf16[1,256,768]{2,1,0:T(8,128)(2,1)S(1)} collective-permute-done((bf16[1,256,768]{2,1,0:T(8,128)(2,1)}, bf16[1,256,768]{2,1,0:T(8,128)(2,1)S(1)}, u32[]{:S(2)}, u32[]{:S(2)}) %collective-permute-start.2) | collective-permute-done | bytes 393248 | tf_op jit(solution)/shard_map/ppermute | solution.py:210
  394.4 13.3 %collective-permute-done.4 = bf16[1,256,768]{2,1,0:T(8,128)(2,1)S(1)} collective-permute-done((bf16[1,256,768]{2,1,0:T(8,128)(2,1)}, bf16[1,256,768]{2,1,0:T(8,128)(2,1)S(1)}, u32[]{:S(2)}, u32[]{:S(2)}) %collective-permute-start.4) | collective-permute-done | bytes 393248 | tf_op jit(solution)/shard_map/ppermute | solution.py:210
  410.0 17.9 %fusion.5 = f32[2048,1536]{0,1:T(8,128)S(1)} fusion(bf16[2048,2048]{1,0:T(8,128)(2,1)} %all-gather.12.cloned.1.call-done, bf16[768,2048]{1,0:T(8,128)(2,1)} %collective-permute-done.7, bf16[768,2048]{1,0:T(8,128)(2,1)} %get-tuple-element.122), kind=kOutput, calls=%fused_computation.33 | convolution fusion | flops 12897484800 | bytes 27262976 | tf_op jit(solution)/shard_map/dot_general | solution.py:129
  437.4 19.1 %select_convert_fusion.1 = (bf16[2048,768]{0,1:T(8,128)(2,1)}, bf16[2048,768]{0,1:T(8,128)(2,1)}, f32[2048,768]{0,1:T(8,128)}) fusion(pred[]{:T(512)S(6)} %eq.34, f32[2048,768]{0,1:T(8,128)} %get-tuple-element.113, f32[2048,1536]{0,1:T(8,128)} %copy-done.16, bf16[2048,2048]{1,0:T(8,128)(2,1)} %all-gather.10.cloned.1.call-done, bf16[2048,768]{1,0:T(8,128)(2,1)} %bitcast.283), kind=kOutput, calls=%fused_computation.16 | convolution fusion | flops 6464471040 | bytes 42991616 | tf_op jit(solution)/shard_map/dot_general | solution.py:300
  464.0 18.5 %convolution_convert_fusion.2 = bf16[2048,2048]{1,0:T(8,128)(2,1)} fusion(bf16[2048,768]{0,1:T(8,128)(2,1)S(1)} %select_convert_fusion, bf16[2048,768]{0,1:T(8,128)(2,1)} %get-tuple-element.114, bf16[768,2048]{1,0:T(8,128)(2,1)} %collective-permute-done.7, bf16[768,2048]{1,0:T(8,128)(2,1)S(1)} %copy-done.56), kind=kOutput, calls=%fused_computation.6 | convolution fusion | flops 12914262016 | bytes 20971520 | tf_op jit(solution)/shard_map/dot_general | solution.py:312
  482.5 10.0 convolution_convert_fusion.4
  499.6 9.9 convolution_convert_fusion.5
  509.6 8.1 convolution_convert_fusion.3
  517.6 13.0 %collective-permute-done.8 = bf16[384,2048]{1,0:T(8,128)(2,1)S(1)} collective-permute-done((bf16[384,2048]{1,0:T(8,128)(2,1)S(1)}, bf16[384,2048]{1,0:T(8,128)(2,1)S(1)}, u32[]{:S(2)}, u32[]{:S(2)}) %collective-permute-start.8) | collective-permute-done | bytes 1572896 | tf_op jit(solution)/shard_map/ppermute | solution.py:165
  533.7 20.2 %reduce-scatter.4.cloned.1.call-done = bf16[256,2048]{1,0:T(8,128)(2,1)} async-done(((bf16[2048,2048]{1,0:T(8,128)(2,1)}), bf16[256,2048]{1,0:T(8,128)(2,1)}) %reduce-scatter.4.cloned.1.call-update) | async-done | bytes 1048592 | tf_op jit(solution)/shard_map/reduce_scatter | solution.py:141
  604.9 7.3 all-to-all-done.4
  659.3 25.7 %all-to-all-start.5 = ((bf16[4,256,1024]{1,2,0:T(8,128)(2,1)}), bf16[4,256,1024]{1,2,0:T(8,128)(2,1)}, u32[]{:S(2)}, u32[]{:S(2)}) async-start(bf16[4,256,1024]{1,2,0:T(8,128)(2,1)} %copy.303), calls=%async_computation.7 | async-start | bytes 4194304 | tf_op jit(solution)/shard_map/all_to_all | solution.py:348
  701.4 11.0 collective-permute-start.14
  714.8 9.1 convolution_convert_fusion.1
  723.9 65.3 %collective-permute-done.13 = bf16[384,2048]{1,0:T(8,128)(2,1)} collective-permute-done((bf16[384,2048]{1,0:T(8,128)(2,1)}, bf16[384,2048]{1,0:T(8,128)(2,1)}, u32[]{:S(2)}, u32[]{:S(2)}) %collective-permute-start.13) | collective-permute-done | bytes 1572896 | tf_op jit(solution)/shard_map/ppermute | solution.py:165
  849.3 11.9 fusion.23
  861.2 38.1 %collective-permute-done.38 = bf16[384,2048]{1,0:T(8,128)(2,1)S(1)} collective-permute-done((bf16[384,2048]{1,0:T(8,128)(2,1)S(1)}, bf16[384,2048]{1,0:T(8,128)(2,1)S(1)}, u32[]{:S(2)}, u32[]{:S(2)}) %collective-permute-start.38) | collective-permute-done | bytes 1572896 | tf_op jit(solution)/shard_map/ppermute | solution.py:398
  908.1 8.6 convolution_convert_fusion.6
  916.7 17.5 %collective-permute-done.19 = bf16[384,2048]{1,0:T(8,128)(2,1)} collective-permute-done((bf16[384,2048]{1,0:T(8,128)(2,1)}, bf16[384,2048]{1,0:T(8,128)(2,1)}, u32[]{:S(2)}, u32[]{:S(2)}) %collective-permute-start.19) | collective-permute-done | bytes 1572896 | tf_op jit(solution)/shard_map/ppermute | solution.py:165
  957.4 38.2 %collective-permute-done.23 = f32[4352]{0:T(1024)S(1)} collective-permute-done((f32[4352]{0:T(1024)S(1)}, f32[4352]{0:T(1024)S(1)}, u32[]{:S(2)}, u32[]{:S(2)}) %collective-permute-start.23) | collective-permute-done | bytes 17440 | tf_op jit(solution)/shard_map/ppermute | solution.py:222
  1001.4 16.1 %collective-permute-done.24 = f32[4352]{0:T(1024)S(1)} collective-permute-done((f32[4352]{0:T(1024)S(1)}, f32[4352]{0:T(1024)S(1)}, u32[]{:S(2)}, u32[]{:S(2)}) %collective-permute-start.24) | collective-permute-done | bytes 17440 | tf_op jit(solution)/shard_map/ppermute | solution.py:222
  1032.1 23.5 %collective-permute-done.41 = bf16[1024,768]{1,0:T(8,128)(2,1)S(1)} collective-permute-done((bf16[1024,768]{1,0:T(8,128)(2,1)S(1)}, bf16[1024,768]{1,0:T(8,128)(2,1)S(1)}, u32[]{:S(2)}, u32[]{:S(2)}) %collective-permute-start.41) | collective-permute-done | bytes 1572896 | tf_op jit(solution)/shard_map/ppermute | solution.py:165
  1093.4 96.2 %collective-permute-done.27 = bf16[256,2048]{1,0:T(8,128)(2,1)S(1)} collective-permute-done((bf16[256,2048]{1,0:T(8,128)(2,1)S(1)}, bf16[256,2048]{1,0:T(8,128)(2,1)S(1)}, u32[]{:S(2)}, u32[]{:S(2)}) %collective-permute-start.27) | collective-permute-done | bytes 1048608 | tf_op jit(solution)/shard_map/ppermute | solution.py:165
  1189.7 22.3 %collective-permute-done.30 = bf16[256,2048]{1,0:T(8,128)(2,1)S(1)} collective-permute-done((bf16[256,2048]{1,0:T(8,128)(2,1)S(1)}, bf16[256,2048]{1,0:T(8,128)(2,1)S(1)}, u32[]{:S(2)}, u32[]{:S(2)}) %collective-permute-start.30) | collective-permute-done | bytes 1048608 | tf_op jit(solution)/shard_map/ppermute | solution.py:165
  1212.2 17.4 %collective-permute-done.33 = bf16[256,2048]{1,0:T(8,128)(2,1)S(1)} collective-permute-done((bf16[256,2048]{1,0:T(8,128)(2,1)S(1)}, bf16[256,2048]{1,0:T(8,128)(2,1)S(1)}, u32[]{:S(2)}, u32[]{:S(2)}) %collective-permute-start.33) | collective-permute-done | bytes 1048608 | tf_op jit(solution)/shard_map/ppermute | solution.py:165
  1246.5 7.7 copy.388
  1254.3 8.7 reshape.386
  (514 shorter events, 442.4 us)
Async XLA Ops:
  7.2 95.2 %all-gather.6.cloned.1.call-start = ((), (), s32[]{:S(2)}) async-start(), calls=%async_computation.11 | async-start | bytes 18874368 | tf_op jit(solution)/shard_map/all_gather | solution.py:125
  8.0 228.2 %all-gather.8.cloned.1.call-start = ((), (), s32[]{:S(2)}) async-start(), calls=%async_computation.12 | async-start | bytes 9437184 | tf_op jit(solution)/shard_map/all_gather | solution.py:125
  164.7 245.3 %all-gather.12.cloned.1.call-start = ((), (), s32[]{:S(2)}) async-start(), calls=%async_computation.14 | async-start | bytes 9437184 | tf_op jit(solution)/shard_map/all_gather | solution.py:125
  243.7 193.6 %all-gather.10.cloned.1.call-start = ((), (), s32[]{:S(2)}) async-start(), calls=%async_computation.13 | async-start | bytes 9437184 | tf_op jit(solution)/shard_map/all_gather | solution.py:125
  244.3 309.6 %reduce-scatter.4.cloned.1.call-start = ((), (), s32[]{:S(2)}) async-start(), calls=%async_computation.15 | async-start | bytes 9437184 | tf_op jit(solution)/shard_map/reduce_scatter | solution.py:141
  251.2 158.8 %collective-permute-start.7 = (bf16[768,2048]{1,0:T(8,128)(2,1)}, bf16[768,2048]{1,0:T(8,128)(2,1)}, u32[]{:S(2)}, u32[]{:S(2)}) collective-permute-start(bf16[768,2048]{1,0:T(8,128)(2,1)} %get-tuple-element.123), channel_id=1, source_target_pairs={{0,16},{4,20},{8,24},{12,28},{16,0},{20,4},{24,8},{28,12},{1,17},{... | collective-permute-start | bytes 9437192 | tf_op jit(solution)/shard_map/ppermute | solution.py:264
  267.5 121.3 %collective-permute-start.2 = (bf16[1,256,768]{2,1,0:T(8,128)(2,1)}, bf16[1,256,768]{2,1,0:T(8,128)(2,1)S(1)}, u32[]{:S(2)}, u32[]{:S(2)}) collective-permute-start(bf16[1,256,768]{2,1,0:T(8,128)(2,1)} %get-tuple-element.136), channel_id=1, source_target_pairs={{0,12},{4,16},{8,20},{12,24},{16,28},{20,0},{24,4},{28,8},{1,13},{... | collective-permute-start | bytes 1179656 | tf_op jit(solution)/shard_map/ppermute | solution.py:210
  269.9 123.7 %collective-permute-start.3 = (bf16[1,256,768]{2,1,0:T(8,128)(2,1)}, bf16[1,256,768]{2,1,0:T(8,128)(2,1)S(1)}, u32[]{:S(2)}, u32[]{:S(2)}) collective-permute-start(bf16[1,256,768]{2,1,0:T(8,128)(2,1)} %get-tuple-element.135), channel_id=1, source_target_pairs={{0,16},{4,20},{8,24},{12,28},{16,0},{20,4},{24,8},{28,12},{1,17},{... | collective-permute-start | bytes 1179656 | tf_op jit(solution)/shard_map/ppermute | solution.py:210
  278.4 129.3 %collective-permute-start.4 = (bf16[1,256,768]{2,1,0:T(8,128)(2,1)}, bf16[1,256,768]{2,1,0:T(8,128)(2,1)S(1)}, u32[]{:S(2)}, u32[]{:S(2)}) collective-permute-start(bf16[1,256,768]{2,1,0:T(8,128)(2,1)} %get-tuple-element.134), channel_id=1, source_target_pairs={{0,20},{4,24},{8,28},{12,0},{16,4},{20,8},{24,12},{28,16},{1,21},{... | collective-permute-start | bytes 1179656 | tf_op jit(solution)/shard_map/ppermute | solution.py:210
  280.2 128.2 %collective-permute-start.5 = (bf16[1,256,768]{2,1,0:T(8,128)(2,1)}, bf16[1,256,768]{2,1,0:T(8,128)(2,1)S(1)}, u32[]{:S(2)}, u32[]{:S(2)}) collective-permute-start(bf16[1,256,768]{2,1,0:T(8,128)(2,1)} %get-tuple-element.133), channel_id=1, source_target_pairs={{0,24},{4,28},{8,0},{12,4},{16,8},{20,12},{24,16},{28,20},{1,25},{... | collective-permute-start | bytes 1179656 | tf_op jit(solution)/shard_map/ppermute | solution.py:210
  482.5 420.6 %reduce-scatter.8.cloned.1.call-start = ((), (), s32[]{:S(2)}) async-start(), calls=%async_computation.17 | async-start | bytes 9437184 | tf_op jit(solution)/shard_map/reduce_scatter | solution.py:141
  496.9 67.6 %collective-permute-start.10 = (bf16[384,2048]{1,0:T(8,128)(2,1)}, bf16[384,2048]{1,0:T(8,128)(2,1)}, u32[]{:S(2)}, u32[]{:S(2)}) collective-permute-start(bf16[384,2048]{1,0:T(8,128)(2,1)} %get-tuple-element.130), channel_id=1, source_target_pairs={{0,1},{3,2},{4,5},{7,6},{8,9},{11,10},{12,13},{15,14},{16,17},{19,... | collective-permute-start | bytes 4718600 | tf_op jit(solution)/shard_map/ppermute | solution.py:165
  570.3 337.8 %all-gather.14.cloned.1.call-start = ((), (), s32[]{:S(2)}) async-start(), calls=%async_computation.18 | async-start | bytes 9437184 | tf_op jit(solution)/shard_map/all_gather | solution.py:125
  659.3 129.9 %all-to-all-start.5 = ((bf16[4,256,1024]{1,2,0:T(8,128)(2,1)}), bf16[4,256,1024]{1,2,0:T(8,128)(2,1)}, u32[]{:S(2)}, u32[]{:S(2)}) async-start(bf16[4,256,1024]{1,2,0:T(8,128)(2,1)} %copy.303), calls=%async_computation.7 | async-start | bytes 4194304 | tf_op jit(solution)/shard_map/all_to_all | solution.py:348
  685.1 393.5 %reduce-scatter.6.cloned.1.call-start = ((), (), s32[]{:S(2)}) async-start(), calls=%async_computation.16 | async-start | bytes 9437184 | tf_op jit(solution)/shard_map/reduce_scatter | solution.py:141
  689.4 213.7 %collective-permute-start.17 = (bf16[384,2048]{1,0:T(8,128)(2,1)}, bf16[384,2048]{1,0:T(8,128)(2,1)}, u32[]{:S(2)}, u32[]{:S(2)}) collective-permute-start(bf16[384,2048]{1,0:T(8,128)(2,1)} %add_convert_fusion.7), channel_id=1, source_target_pairs={{1,0},{2,3},{5,4},{6,7},{9,8},{10,11},{13,12},{14,15},{17,16},{18,... | collective-permute-start | bytes 4718600 | tf_op jit(solution)/shard_map/ppermute | solution.py:165
  694.3 208.8 %collective-permute-start.15 = (bf16[1024,768]{1,0:T(8,128)(2,1)}, bf16[1024,768]{1,0:T(8,128)(2,1)}, u32[]{:S(2)}, u32[]{:S(2)}) collective-permute-start(bf16[1024,768]{1,0:T(8,128)(2,1)} %add_convert_fusion.8), channel_id=1, source_target_pairs={{1,2},{2,1},{5,6},{6,5},{9,10},{10,9},{13,14},{14,13},{17,18},{18,... | collective-permute-start | bytes 4718600 | tf_op jit(solution)/shard_map/ppermute | solution.py:165
  700.1 89.2 %collective-permute-start.13 = (bf16[384,2048]{1,0:T(8,128)(2,1)}, bf16[384,2048]{1,0:T(8,128)(2,1)}, u32[]{:S(2)}, u32[]{:S(2)}) collective-permute-start(bf16[384,2048]{1,0:T(8,128)(2,1)} %add_convert_fusion.9), channel_id=1, source_target_pairs={{1,0},{2,3},{5,4},{6,7},{9,8},{10,11},{13,12},{14,15},{17,16},{18,... | collective-permute-start | bytes 4718600 | tf_op jit(solution)/shard_map/ppermute | solution.py:165
  701.4 87.9 %collective-permute-start.14 = (bf16[1024,768]{1,0:T(8,128)(2,1)}, bf16[1024,768]{1,0:T(8,128)(2,1)}, u32[]{:S(2)}, u32[]{:S(2)}) collective-permute-start(bf16[1024,768]{1,0:T(8,128)(2,1)} %get-tuple-element.85), channel_id=1, source_target_pairs={{0,1},{3,2},{4,5},{7,6},{8,9},{11,10},{12,13},{15,14},{16,17},{19,... | collective-permute-start | bytes 4718600 | tf_op jit(solution)/shard_map/ppermute | solution.py:165
  712.3 190.8 %collective-permute-start.16 = (bf16[384,2048]{1,0:T(8,128)(2,1)}, bf16[384,2048]{1,0:T(8,128)(2,1)}, u32[]{:S(2)}, u32[]{:S(2)}) collective-permute-start(bf16[384,2048]{1,0:T(8,128)(2,1)} %get-tuple-element.88), channel_id=1, source_target_pairs={{0,1},{3,2},{4,5},{7,6},{8,9},{11,10},{12,13},{15,14},{16,17},{19,... | collective-permute-start | bytes 4718600 | tf_op jit(solution)/shard_map/ppermute | solution.py:165
  835.6 67.5 %all-to-all-start.6 = ((bf16[256,8,512]{2,0,1:T(8,128)(2,1)}), bf16[256,8,512]{2,0,1:T(8,128)(2,1)}, u32[]{:S(2)}, u32[]{:S(2)}) async-start(bf16[256,8,512]{2,0,1:T(8,128)(2,1)} %bitcast.265), calls=%async_computation.8 | async-start | bytes 4194304 | tf_op jit(solution)/shard_map/all_to_all | solution.py:376
  843.4 73.3 %collective-permute-start.18 = (bf16[1024,768]{1,0:T(8,128)(2,1)}, bf16[1024,768]{1,0:T(8,128)(2,1)}, u32[]{:S(2)}, u32[]{:S(2)}) collective-permute-start(bf16[1024,768]{1,0:T(8,128)(2,1)} %add_convert_fusion.6), channel_id=1, source_target_pairs={{1,2},{2,1},{5,6},{6,5},{9,10},{10,9},{13,14},{14,13},{17,18},{18,... | collective-permute-start | bytes 4718600 | tf_op jit(solution)/shard_map/ppermute | solution.py:165
  906.6 122.3 %collective-permute-start.40 = (bf16[1024,768]{1,0:T(8,128)(2,1)}, bf16[1024,768]{1,0:T(8,128)(2,1)}, u32[]{:S(2)}, u32[]{:S(2)}) collective-permute-start(bf16[1024,768]{1,0:T(8,128)(2,1)} %add_convert_fusion.1), channel_id=1, source_target_pairs={{1,0},{2,3},{5,4},{6,7},{9,8},{10,11},{13,12},{14,15},{17,16},{18,... | collective-permute-start | bytes 4718600 | tf_op jit(solution)/shard_map/ppermute | solution.py:165
  944.6 75.3 %collective-permute-start.25 = (bf16[256,2048]{1,0:T(8,128)(2,1)S(1)}, bf16[256,2048]{1,0:T(8,128)(2,1)S(1)}, u32[]{:S(2)}, u32[]{:S(2)}) collective-permute-start(bf16[256,2048]{1,0:T(8,128)(2,1)S(1)} %get-tuple-element.142), channel_id=1, source_target_pairs={{0,1},{3,2},{4,5},{7,6},{8,9},{11,10},{12,13},{15,14},{16,17},{19,... | collective-permute-start | bytes 3145736 | tf_op jit(solution)/shard_map/ppermute | solution.py:165
  949.2 72.6 %collective-permute-start.28 = (bf16[256,2048]{1,0:T(8,128)(2,1)S(1)}, bf16[256,2048]{1,0:T(8,128)(2,1)S(1)}, u32[]{:S(2)}, u32[]{:S(2)}) collective-permute-start(bf16[256,2048]{1,0:T(8,128)(2,1)S(1)} %get-tuple-element.143), channel_id=1, source_target_pairs={{0,1},{3,2},{4,5},{7,6},{8,9},{11,10},{12,13},{15,14},{16,17},{19,... | collective-permute-start | bytes 3145736 | tf_op jit(solution)/shard_map/ppermute | solution.py:165
  953.4 72.4 %collective-permute-start.31 = (bf16[256,2048]{1,0:T(8,128)(2,1)S(1)}, bf16[256,2048]{1,0:T(8,128)(2,1)S(1)}, u32[]{:S(2)}, u32[]{:S(2)}) collective-permute-start(bf16[256,2048]{1,0:T(8,128)(2,1)S(1)} %copy-done.74), channel_id=1, source_target_pairs={{0,1},{3,2},{4,5},{7,6},{8,9},{11,10},{12,13},{15,14},{16,17},{19,... | collective-permute-start | bytes 3145736 | tf_op jit(solution)/shard_map/ppermute | solution.py:165
  1059.4 187.2 %all-to-all-start.7 = ((bf16[8,256,768]{2,1,0:T(8,128)(2,1)}), bf16[8,256,768]{2,1,0:T(8,128)(2,1)}, u32[]{:S(2)}, u32[]{:S(2)}) async-start(bf16[8,256,768]{2,1,0:T(8,128)(2,1)} %bitcast.251), calls=%async_computation.10 | async-start | bytes 6291456 | tf_op jit(solution)/shard_map/all_to_all | solution.py:401
  1069.2 164.4 %collective-permute-start.35 = (bf16[384,2048]{1,0:T(8,128)(2,1)}, bf16[384,2048]{1,0:T(8,128)(2,1)}, u32[]{:S(2)}, u32[]{:S(2)}) collective-permute-start(bf16[384,2048]{1,0:T(8,128)(2,1)} %add_convert_fusion.4), channel_id=1, source_target_pairs={{1,0},{2,3},{5,4},{6,7},{9,8},{10,11},{13,12},{14,15},{17,16},{18,... | collective-permute-start | bytes 4718600 | tf_op jit(solution)/shard_map/ppermute | solution.py:165
  1074.3 160.9 %collective-permute-start.37 = (bf16[384,2048]{1,0:T(8,128)(2,1)}, bf16[384,2048]{1,0:T(8,128)(2,1)}, u32[]{:S(2)}, u32[]{:S(2)}) collective-permute-start(bf16[384,2048]{1,0:T(8,128)(2,1)} %add_convert_fusion.2), channel_id=1, source_target_pairs={{1,0},{2,3},{5,4},{6,7},{9,8},{10,11},{13,12},{14,15},{17,16},{18,... | collective-permute-start | bytes 4718600 | tf_op jit(solution)/shard_map/ppermute | solution.py:165
  1085.9 103.7 %collective-permute-start.27 = (bf16[256,2048]{1,0:T(8,128)(2,1)S(1)}, bf16[256,2048]{1,0:T(8,128)(2,1)S(1)}, u32[]{:S(2)}, u32[]{:S(2)}) collective-permute-start(bf16[256,2048]{1,0:T(8,128)(2,1)S(1)} %add_convert_fusion.16), channel_id=1, source_target_pairs={{1,0},{2,3},{5,4},{6,7},{9,8},{10,11},{13,12},{14,15},{17,16},{18,... | collective-permute-start | bytes 3145736 | tf_op jit(solution)/shard_map/ppermute | solution.py:165
  1088.8 123.2 %collective-permute-start.30 = (bf16[256,2048]{1,0:T(8,128)(2,1)S(1)}, bf16[256,2048]{1,0:T(8,128)(2,1)S(1)}, u32[]{:S(2)}, u32[]{:S(2)}) collective-permute-start(bf16[256,2048]{1,0:T(8,128)(2,1)S(1)} %add_convert_fusion.14), channel_id=1, source_target_pairs={{1,0},{2,3},{5,4},{6,7},{9,8},{10,11},{13,12},{14,15},{17,16},{18,... | collective-permute-start | bytes 3145736 | tf_op jit(solution)/shard_map/ppermute | solution.py:165
  1092.1 137.5 %collective-permute-start.33 = (bf16[256,2048]{1,0:T(8,128)(2,1)S(1)}, bf16[256,2048]{1,0:T(8,128)(2,1)S(1)}, u32[]{:S(2)}, u32[]{:S(2)}) collective-permute-start(bf16[256,2048]{1,0:T(8,128)(2,1)S(1)} %add_convert_fusion.12), channel_id=1, source_target_pairs={{1,0},{2,3},{5,4},{6,7},{9,8},{10,11},{13,12},{14,15},{17,16},{18,... | collective-permute-start | bytes 3145736 | tf_op jit(solution)/shard_map/ppermute | solution.py:165
  (135 other events, 2328.4 us)
Sparse Core Ops, SparseCore 0:
  9.9 92.4 all-gather.5
  104.3 54.2 all-gather.7
  243.8 102.2 all-gather.11
  347.8 75.0 all-gather.9
  482.6 71.2 reduce-scatter.3
  570.4 72.0 reduce-scatter.7
  644.3 54.2 all-gather.13
  724.0 69.9 reduce-scatter.5

commit v3 on v2

--- a/solution.py
+++ b/solution.py
@@ -104,9 +104,7 @@
             * factor
         )
         key_part = (
-            jnp.einsum(
-                "hqk,qhd->khd", grad_scores, query_block, preferred_element_type=jnp.float32
-            )
+            jnp.einsum("hqk,qhd->khd", grad_scores, query_block, preferred_element_type=jnp.float32)
             * factor
         )
         value_part = jnp.einsum(
@@ -325,7 +323,7 @@
     grad_mixed_low = grad_middle.astype(low)
     grad_attended = jnp.dot(grad_mixed_low, out_full, preferred_element_type=f32).astype(low)
     grad_heads = lax.all_to_all(grad_attended, "sp", split_axis=1, concat_axis=0, tiled=True)
-    grad_mixed_low = meet(grad_mixed_low, [s1], [d0])
+    grad_mixed_low = meet(grad_mixed_low, [s1], [d0, d1])
     grad_out = scatter_sum(product_tn(grad_mixed_low, attended))
     grad_query_local, grad_keys, grad_values = attention_backward(
         query_local,
@@ -334,7 +332,7 @@
         mixed_heads,
         logsums,
         grad_heads.reshape(length, -1, HD),
-        lambda values: meet(values, [s0], [d1]),
+        lambda values: meet(values, [s0]),
     )
     grad_query_send = grad_query_local.astype(low).reshape(length, -1)
     grad_key_send = (
@@ -344,10 +342,10 @@
         grad_values.reshape(length, local_kv, group, HD).sum(2).astype(low).reshape(length, -1)
     )
     grads_send = jnp.concatenate([grad_query_send, grad_key_send, grad_value_send], 1)
-    grads_send, activation = meet((grads_send, activation), [s1, d0], [k0])
+    grads_send, activation = meet((grads_send, activation), [s1, d0])
     grads_low = lax.all_to_all(grads_send, "sp", split_axis=0, concat_axis=1, tiled=True)
     hidden_out = (middle + scatter_sum(product_nt(activation, down_own))).astype(low)
-    grads_low = meet(grads_low, [s0, d1], [k1])
+    grads_low = meet(grads_low, [d1], [k0, k1])
     grads_low = grads_low.reshape(rows, line, -1)
     cuts = (grad_query_send.shape[1], grad_query_send.shape[1] + grad_key_send.shape[1])
     grad_query_low = grads_low[:, :, : cuts[0]]
@@ -359,6 +357,7 @@
         query_gain,
         rotate_back(grad_query_low.astype(f32).reshape(rows, H, HD), cosine, sine),
     )
+    grad_query, query_term = meet((grad_query, query_term), [d0, k0])
     grad_key, key_term = rms_backward(
         key,
         key_inverse,
@@ -375,7 +374,7 @@
     )
     grad_columns = lax.all_to_all(grad_projected, "fsdp", split_axis=1, concat_axis=0, tiled=True)
     out_chain = Chain(grad_out, line)
-    grad_columns = meet(grad_columns, [d0, k0, s1], [out_chain])
+    grad_columns = meet(grad_columns, [d1, k1], [out_chain])
     grad_normed1 = jnp.dot(grad_projected, qkv_full, preferred_element_type=f32)
     grad_qkv_own = product_tn(grad_columns, normed1_all).astype(low)
     back_one, attn_term = rms_backward(hidden, inverse1, attn_gain, grad_normed1)
@@ -388,7 +387,7 @@
             jnp.sum(key_term, axis=(0, 1)),
         ]
     )
-    grad_qkv_own, terms = meet((grad_qkv_own, terms), [d1, k1])
+    grad_qkv_own, terms = meet((grad_qkv_own, terms), [k0])
     q0, q1 = (Chain(part, line) for part in halves(grad_qkv_own))
     q0.send()
     q1.send()

time: 1280 us -> 1220 us (0.953)
  waiting for transfers between devices: 629 us -> 572 us
  local copies, waits for them, and re-layouts: 146 us -> 127 us
    ppermute x27, waiting for transfers between devices: 263 us -> 214 us  [send(): self.flying = lax.ppermute(self.value, 'sp', self.hops[self.at][0])]
    ppermute x2, waiting for transfers between devices: 38.1 us -> 6.06 us  [layer(): grad_swapped.append(lax.ppermute(chain.finish(), 'fsdp', swap))]
    unnamed x230 -> x220, local copies, waits for them, and re-layouts: 38.6 us -> 31.6 us
  transfers between devices with their start and end apart: 57 -> 57, of which waited for: 21 -> 22; matrix products, arithmetic and copies ran while one was open for 29% -> 28% of each run, Pallas kernels for 0% -> 0%
where the time goes in v3:
time: 1220 us; the launch traced here: 1210 us
  waiting for transfers between devices  572 us (47%)
  matrix products  168 us (14%)
  other arithmetic  143 us (12%)
  starting transfers between devices  141 us (12%)
  local copies, waits for them, and re-layouts  127 us (10%)
  blocking collectives  39.6 us (3%)
  between operations  16.9 us (1%)
    ppermute x27, waiting for transfers between devices, send(): self.flying = lax.ppermute(self.value, 'sp', self.hops[self.at][0])  214 us
    ppermute x7, waiting for transfers between devices, turn(): arrived = lax.ppermute(block, 'fsdp', pairs)  132 us
    all_gather x5, waiting for transfers between devices, gather_rows(): return lax.all_gather(array, 'fsdp', axis=0, tiled=True)  94.4 us
    ppermute x27, starting transfers between devices, send(): self.flying = lax.ppermute(self.value, 'sp', self.hops[self.at][0])  67.6 us
    ppermute x5, waiting for transfers between devices, sum_all(): lax.ppermute(values, axis, [(d, d ^ step) for d in range(size)])  58.4 us
    convert_element_type x16, other arithmetic, take(): self.value = total.astype(jnp.bfloat16)  50.7 us
    dot_general x4, matrix products, product_nt(): lax.dot_general(inputs, weight, (((1,), (1,)), ((), ())), preferred_eleme...  44 us
    dot_general x5, matrix products, product_tn(): lax.dot_general(left, right, (((0,), (0,)), ((), ())), preferred_element_...  41.6 us
  transfers between devices with their start and end apart: 57, of which 22 were waited for; matrix products, arithmetic and copies ran while one was open for 28% of the time, Pallas kernels for 0%

profile of v3, /device:TPU:0, one launch (start us, length us, event | category | flops | bytes accessed | tf_op | source)
XLA Modules:
  0.0 1207.9 jit_solution(17582877050732693302)
XLA Ops:
  8.0 94.4 %all-gather.6.cloned.1.call-done = bf16[4096,2048]{1,0:T(8,128)(2,1)} async-done(((bf16[512,2048]{1,0:T(8,128)(2,1)}), bf16[4096,2048]{1,0:T(8,128)(2,1)}) %all-gather.6.cloned.1.call-update) | async-done | bytes 16777232 | tf_op jit(solution)/shard_map/all_gather | solution.py:123
  105.0 10.7 fusion.58
  138.8 8.6 all-to-all-done.2
  176.4 18.3 %all-to-all-done.1 = bf16[256,4,512]{2,0,1:T(8,128)(2,1)S(1)} async-done(((bf16[256,4,512]{2,0,1:T(8,128)(2,1)}), bf16[256,4,512]{2,0,1:T(8,128)(2,1)S(1)}, u32[]{:S(2)}, u32[]{:S(2)}) %all-to-all-start.1) | async-done | bytes 1048608 | tf_op jit(solution)/shard_map/all_to_all | solution.py:279
  214.8 39.6 %all_to_all.126 = bf16[4,256,512]{1,2,0:T(8,128)(2,1)} all-to-all(bf16[4,256,512]{1,2,0:T(8,128)(2,1)S(1)} %copy.302), channel_id=1, replica_groups=mesh['fsdp'=8,'sp'=4] {'sp'}, dimensions={0} | all-to-all | bytes 2097152 | tf_op jit(solution)/shard_map/all_to_all | solution.py:289
  288.9 7.9 collective-permute-done
  300.7 106.6 %collective-permute-done.2 = bf16[1,256,768]{2,1,0:T(8,128)(2,1)S(1)} collective-permute-done((bf16[1,256,768]{2,1,0:T(8,128)(2,1)}, bf16[1,256,768]{2,1,0:T(8,128)(2,1)S(1)}, u32[]{:S(2)}, u32[]{:S(2)}) %collective-permute-start.2) | collective-permute-done | bytes 393248 | tf_op jit(solution)/shard_map/ppermute | solution.py:208
  412.9 13.2 %collective-permute-done.4 = bf16[1,256,768]{2,1,0:T(8,128)(2,1)S(1)} collective-permute-done((bf16[1,256,768]{2,1,0:T(8,128)(2,1)}, bf16[1,256,768]{2,1,0:T(8,128)(2,1)S(1)}, u32[]{:S(2)}, u32[]{:S(2)}) %collective-permute-start.4) | collective-permute-done | bytes 393248 | tf_op jit(solution)/shard_map/ppermute | solution.py:208
  428.4 17.9 %fusion.5 = f32[2048,1536]{0,1:T(8,128)S(1)} fusion(bf16[2048,2048]{1,0:T(8,128)(2,1)} %all-gather.12.cloned.1.call-done, bf16[768,2048]{1,0:T(8,128)(2,1)} %collective-permute-done.7, bf16[768,2048]{1,0:T(8,128)(2,1)} %get-tuple-element.122), kind=kOutput, calls=%fused_computation.33 | convolution fusion | flops 12897484800 | bytes 27262976 | tf_op jit(solution)/shard_map/dot_general | solution.py:127
  455.7 18.9 %select_convert_fusion.1 = (bf16[2048,768]{0,1:T(8,128)(2,1)}, bf16[2048,768]{0,1:T(8,128)(2,1)}, f32[2048,768]{0,1:T(8,128)}) fusion(pred[]{:T(512)S(6)} %eq.34, f32[2048,768]{0,1:T(8,128)} %get-tuple-element.115, f32[2048,1536]{0,1:T(8,128)} %copy-done.14, bf16[2048,2048]{1,0:T(8,128)(2,1)} %all-gather.10.cloned.1.call-done, bf16[2048,768]{1,0:T(8,128)(2,1)} %bitcast.242), kind=kOutput, calls=%fused_computation.16 | convolution fusion | flops 6464471040 | bytes 42991616 | tf_op jit(solution)/shard_map/dot_general | solution.py:298
  482.0 18.7 %convolution_convert_fusion.2 = bf16[2048,2048]{1,0:T(8,128)(2,1)} fusion(bf16[2048,768]{0,1:T(8,128)(2,1)S(1)} %select_convert_fusion, bf16[2048,768]{0,1:T(8,128)(2,1)} %get-tuple-element.116, bf16[768,2048]{1,0:T(8,128)(2,1)} %collective-permute-done.7, bf16[768,2048]{1,0:T(8,128)(2,1)S(1)} %copy-done.58), kind=kOutput, calls=%fused_computation.6 | convolution fusion | flops 12914262016 | bytes 20971520 | tf_op jit(solution)/shard_map/dot_general | solution.py:310
  500.8 10.0 convolution_convert_fusion.4
  517.8 9.6 convolution_convert_fusion.5
  527.5 8.1 convolution_convert_fusion.3
  535.5 13.3 %collective-permute-done.8 = bf16[384,2048]{1,0:T(8,128)(2,1)S(1)} collective-permute-done((bf16[384,2048]{1,0:T(8,128)(2,1)S(1)}, bf16[384,2048]{1,0:T(8,128)(2,1)S(1)}, u32[]{:S(2)}, u32[]{:S(2)}) %collective-permute-start.8) | collective-permute-done | bytes 1572896 | tf_op jit(solution)/shard_map/ppermute | solution.py:163
  551.9 20.2 %reduce-scatter.4.cloned.1.call-done = bf16[256,2048]{1,0:T(8,128)(2,1)} async-done(((bf16[2048,2048]{1,0:T(8,128)(2,1)}), bf16[256,2048]{1,0:T(8,128)(2,1)}) %reduce-scatter.4.cloned.1.call-update) | async-done | bytes 1048592 | tf_op jit(solution)/shard_map/reduce_scatter | solution.py:139
  574.8 7.8 collective-permute-done.10
  675.6 33.3 %all-to-all-start.5 = ((bf16[4,256,1024]{1,2,0:T(8,128)(2,1)}), bf16[4,256,1024]{1,2,0:T(8,128)(2,1)S(1)}, u32[]{:S(2)}, u32[]{:S(2)}) async-start(bf16[4,256,1024]{1,2,0:T(8,128)(2,1)} %copy.320), calls=%async_computation.7 | async-start | bytes 4194304 | tf_op jit(solution)/shard_map/all_to_all | solution.py:346
  720.0 9.1 convolution_convert_fusion.1
  729.1 39.8 %collective-permute-done.38 = bf16[384,2048]{1,0:T(8,128)(2,1)} collective-permute-done((bf16[384,2048]{1,0:T(8,128)(2,1)}, bf16[384,2048]{1,0:T(8,128)(2,1)}, u32[]{:S(2)}, u32[]{:S(2)}) %collective-permute-start.38) | collective-permute-done | bytes 1572896 | tf_op jit(solution)/shard_map/ppermute | solution.py:163
  774.4 38.6 %collective-permute-done.36 = bf16[384,2048]{1,0:T(8,128)(2,1)} collective-permute-done((bf16[384,2048]{1,0:T(8,128)(2,1)}, bf16[384,2048]{1,0:T(8,128)(2,1)}, u32[]{:S(2)}, u32[]{:S(2)}) %collective-permute-start.36) | collective-permute-done | bytes 1572896 | tf_op jit(solution)/shard_map/ppermute | solution.py:163
  890.8 12.4 %fusion.23 = (f32[2048]{0:T(1024)S(1)}, f32[256]{0:T(256)S(1)}, f32[256,2048]{1,0:T(8,128)}) fusion(bf16[256,2048]{1,0:T(8,128)(2,1)S(1)} %copy-done.20, f32[256]{0:T(256)S(1)} %copy-done.88, f32[2048]{0:T(1024)S(1)} %copy-done.83, bf16[4096,2048]{1,0:T(8,128)(2,1)} %all-gather.6.cloned.1.call-done, bf16[256,1024]{0,1:T(8,128)(2,1)} %bitcast.252, ...), kind=kOutput, calls=%fused_computation.74 | convolution fusion | flops 4304926720 | bytes 22038528 | tf_op jit(solution)/shard_map/dot_general | solution.py:378
  913.9 8.2 convolution_convert_fusion.6
  932.5 12.7 %collective-permute-start.30 = (bf16[256,2048]{1,0:T(8,128)(2,1)S(1)}, bf16[256,2048]{1,0:T(8,128)(2,1)S(1)}, u32[]{:S(2)}, u32[]{:S(2)}) collective-permute-start(bf16[256,2048]{1,0:T(8,128)(2,1)S(1)} %copy-done.70), channel_id=1, source_target_pairs={{0,1},{3,2},{4,5},{7,6},{8,9},{11,10},{12,13},{15,14},{16,17},{19,... | collective-permute-start | bytes 3145736 | tf_op jit(solution)/shard_map/ppermute | solution.py:163
  950.9 22.2 %collective-permute-done.22 = f32[4352]{0:T(1024)S(1)} collective-permute-done((f32[4352]{0:T(1024)S(1)}, f32[4352]{0:T(1024)S(1)}, u32[]{:S(2)}, u32[]{:S(2)}) %collective-permute-start.22) | collective-permute-done | bytes 17440 | tf_op jit(solution)/shard_map/ppermute | solution.py:220
  977.2 36.2 %collective-permute-done.23 = f32[4352]{0:T(1024)S(1)} collective-permute-done((f32[4352]{0:T(1024)S(1)}, f32[4352]{0:T(1024)S(1)}, u32[]{:S(2)}, u32[]{:S(2)}) %collective-permute-start.23) | collective-permute-done | bytes 17440 | tf_op jit(solution)/shard_map/ppermute | solution.py:220
  1043.7 8.1 collective-permute-done.33
  1063.4 63.9 %collective-permute-done.26 = bf16[256,2048]{1,0:T(8,128)(2,1)S(1)} collective-permute-done((bf16[256,2048]{1,0:T(8,128)(2,1)S(1)}, bf16[256,2048]{1,0:T(8,128)(2,1)S(1)}, u32[]{:S(2)}, u32[]{:S(2)}) %collective-permute-start.26) | collective-permute-done | bytes 1048608 | tf_op jit(solution)/shard_map/ppermute | solution.py:163
  1127.4 25.1 %collective-permute-done.29 = bf16[256,2048]{1,0:T(8,128)(2,1)S(1)} collective-permute-done((bf16[256,2048]{1,0:T(8,128)(2,1)S(1)}, bf16[256,2048]{1,0:T(8,128)(2,1)S(1)}, u32[]{:S(2)}, u32[]{:S(2)}) %collective-permute-start.29) | collective-permute-done | bytes 1048608 | tf_op jit(solution)/shard_map/ppermute | solution.py:163
  1155.2 17.0 %collective-permute-done.32 = bf16[256,2048]{1,0:T(8,128)(2,1)S(1)} collective-permute-done((bf16[256,2048]{1,0:T(8,128)(2,1)S(1)}, bf16[256,2048]{1,0:T(8,128)(2,1)S(1)}, u32[]{:S(2)}, u32[]{:S(2)}) %collective-permute-start.32) | collective-permute-done | bytes 1048608 | tf_op jit(solution)/shard_map/ppermute | solution.py:163
  1184.2 7.8 copy.388
  1191.9 8.7 reshape.378
  (504 shorter events, 424.0 us)
Async XLA Ops:
  7.2 95.2 %all-gather.6.cloned.1.call-start = ((), (), s32[]{:S(2)}) async-start(), calls=%async_computation.11 | async-start | bytes 18874368 | tf_op jit(solution)/shard_map/all_gather | solution.py:123
  8.0 246.4 %all-gather.8.cloned.1.call-start = ((), (), s32[]{:S(2)}) async-start(), calls=%async_computation.12 | async-start | bytes 9437184 | tf_op jit(solution)/shard_map/all_gather | solution.py:123
  169.5 258.9 %all-gather.12.cloned.1.call-start = ((), (), s32[]{:S(2)}) async-start(), calls=%async_computation.14 | async-start | bytes 9437184 | tf_op jit(solution)/shard_map/all_gather | solution.py:123
  262.2 193.5 %all-gather.10.cloned.1.call-start = ((), (), s32[]{:S(2)}) async-start(), calls=%async_computation.13 | async-start | bytes 9437184 | tf_op jit(solution)/shard_map/all_gather | solution.py:123
  262.8 309.3 %reduce-scatter.4.cloned.1.call-start = ((), (), s32[]{:S(2)}) async-start(), calls=%async_computation.15 | async-start | bytes 9437184 | tf_op jit(solution)/shard_map/reduce_scatter | solution.py:139
  269.7 158.6 %collective-permute-start.7 = (bf16[768,2048]{1,0:T(8,128)(2,1)}, bf16[768,2048]{1,0:T(8,128)(2,1)}, u32[]{:S(2)}, u32[]{:S(2)}) collective-permute-start(bf16[768,2048]{1,0:T(8,128)(2,1)} %get-tuple-element.123), channel_id=1, source_target_pairs={{0,16},{4,20},{8,24},{12,28},{16,0},{20,4},{24,8},{28,12},{1,17},{... | collective-permute-start | bytes 9437192 | tf_op jit(solution)/shard_map/ppermute | solution.py:262
  286.0 121.3 %collective-permute-start.2 = (bf16[1,256,768]{2,1,0:T(8,128)(2,1)}, bf16[1,256,768]{2,1,0:T(8,128)(2,1)S(1)}, u32[]{:S(2)}, u32[]{:S(2)}) collective-permute-start(bf16[1,256,768]{2,1,0:T(8,128)(2,1)} %get-tuple-element.136), channel_id=1, source_target_pairs={{0,12},{4,16},{8,20},{12,24},{16,28},{20,0},{24,4},{28,8},{1,13},{... | collective-permute-start | bytes 1179656 | tf_op jit(solution)/shard_map/ppermute | solution.py:208
  288.4 123.7 %collective-permute-start.3 = (bf16[1,256,768]{2,1,0:T(8,128)(2,1)}, bf16[1,256,768]{2,1,0:T(8,128)(2,1)S(1)}, u32[]{:S(2)}, u32[]{:S(2)}) collective-permute-start(bf16[1,256,768]{2,1,0:T(8,128)(2,1)} %get-tuple-element.135), channel_id=1, source_target_pairs={{0,16},{4,20},{8,24},{12,28},{16,0},{20,4},{24,8},{28,12},{1,17},{... | collective-permute-start | bytes 1179656 | tf_op jit(solution)/shard_map/ppermute | solution.py:208
  296.8 129.2 %collective-permute-start.4 = (bf16[1,256,768]{2,1,0:T(8,128)(2,1)}, bf16[1,256,768]{2,1,0:T(8,128)(2,1)S(1)}, u32[]{:S(2)}, u32[]{:S(2)}) collective-permute-start(bf16[1,256,768]{2,1,0:T(8,128)(2,1)} %get-tuple-element.134), channel_id=1, source_target_pairs={{0,20},{4,24},{8,28},{12,0},{16,4},{20,8},{24,12},{28,16},{1,21},{... | collective-permute-start | bytes 1179656 | tf_op jit(solution)/shard_map/ppermute | solution.py:208
  298.6 128.2 %collective-permute-start.5 = (bf16[1,256,768]{2,1,0:T(8,128)(2,1)}, bf16[1,256,768]{2,1,0:T(8,128)(2,1)S(1)}, u32[]{:S(2)}, u32[]{:S(2)}) collective-permute-start(bf16[1,256,768]{2,1,0:T(8,128)(2,1)} %get-tuple-element.133), channel_id=1, source_target_pairs={{0,24},{4,28},{8,0},{12,4},{16,8},{20,12},{24,16},{28,20},{1,25},{... | collective-permute-start | bytes 1179656 | tf_op jit(solution)/shard_map/ppermute | solution.py:208
  500.8 413.1 %reduce-scatter.8.cloned.1.call-start = ((), (), s32[]{:S(2)}) async-start(), calls=%async_computation.17 | async-start | bytes 9437184 | tf_op jit(solution)/shard_map/reduce_scatter | solution.py:139
  515.2 67.4 %collective-permute-start.10 = (bf16[384,2048]{1,0:T(8,128)(2,1)}, bf16[384,2048]{1,0:T(8,128)(2,1)}, u32[]{:S(2)}, u32[]{:S(2)}) collective-permute-start(bf16[384,2048]{1,0:T(8,128)(2,1)} %get-tuple-element.130), channel_id=1, source_target_pairs={{0,1},{3,2},{4,5},{7,6},{8,9},{11,10},{12,13},{15,14},{16,17},{19,... | collective-permute-start | bytes 4718600 | tf_op jit(solution)/shard_map/ppermute | solution.py:163
  588.4 325.5 %all-gather.14.cloned.1.call-start = ((), (), s32[]{:S(2)}) async-start(), calls=%async_computation.18 | async-start | bytes 9437184 | tf_op jit(solution)/shard_map/all_gather | solution.py:123
  612.7 54.9 %collective-permute-start.11 = (bf16[384,2048]{1,0:T(8,128)(2,1)}, bf16[384,2048]{1,0:T(8,128)(2,1)}, u32[]{:S(2)}, u32[]{:S(2)}) collective-permute-start(bf16[384,2048]{1,0:T(8,128)(2,1)} %get-tuple-element.126), channel_id=1, source_target_pairs={{1,2},{2,1},{5,6},{6,5},{9,10},{10,9},{13,14},{14,13},{17,18},{18,... | collective-permute-start | bytes 4718600 | tf_op jit(solution)/shard_map/ppermute | solution.py:163
  614.6 53.1 %collective-permute-start.12 = (bf16[1024,768]{1,0:T(8,128)(2,1)}, bf16[1024,768]{1,0:T(8,128)(2,1)}, u32[]{:S(2)}, u32[]{:S(2)}) collective-permute-start(bf16[1024,768]{1,0:T(8,128)(2,1)} %get-tuple-element.81), channel_id=1, source_target_pairs={{0,1},{3,2},{4,5},{7,6},{8,9},{11,10},{12,13},{15,14},{16,17},{19,... | collective-permute-start | bytes 4718600 | tf_op jit(solution)/shard_map/ppermute | solution.py:163
  622.1 196.4 %collective-permute-start.13 = (bf16[1024,768]{1,0:T(8,128)(2,1)}, bf16[1024,768]{1,0:T(8,128)(2,1)}, u32[]{:S(2)}, u32[]{:S(2)}) collective-permute-start(bf16[1024,768]{1,0:T(8,128)(2,1)} %get-tuple-element.84), channel_id=1, source_target_pairs={{0,1},{3,2},{4,5},{7,6},{8,9},{11,10},{12,13},{15,14},{16,17},{19,... | collective-permute-start | bytes 4718600 | tf_op jit(solution)/shard_map/ppermute | solution.py:163
  671.3 201.4 %collective-permute-start.14 = (bf16[1024,768]{1,0:T(8,128)(2,1)}, bf16[1024,768]{1,0:T(8,128)(2,1)}, u32[]{:S(2)}, u32[]{:S(2)}) collective-permute-start(bf16[1024,768]{1,0:T(8,128)(2,1)} %add_convert_fusion.9), channel_id=1, source_target_pairs={{1,2},{2,1},{5,6},{6,5},{9,10},{10,9},{13,14},{14,13},{17,18},{18,... | collective-permute-start | bytes 4718600 | tf_op jit(solution)/shard_map/ppermute | solution.py:163
  675.6 142.9 %all-to-all-start.5 = ((bf16[4,256,1024]{1,2,0:T(8,128)(2,1)}), bf16[4,256,1024]{1,2,0:T(8,128)(2,1)S(1)}, u32[]{:S(2)}, u32[]{:S(2)}) async-start(bf16[4,256,1024]{1,2,0:T(8,128)(2,1)} %copy.320), calls=%async_computation.7 | async-start | bytes 4194304 | tf_op jit(solution)/shard_map/all_to_all | solution.py:346
  708.9 329.4 %reduce-scatter.6.cloned.1.call-start = ((), (), s32[]{:S(2)}) async-start(), calls=%async_computation.16 | async-start | bytes 9437184 | tf_op jit(solution)/shard_map/reduce_scatter | solution.py:139
  713.3 55.7 %collective-permute-start.38 = (bf16[384,2048]{1,0:T(8,128)(2,1)}, bf16[384,2048]{1,0:T(8,128)(2,1)}, u32[]{:S(2)}, u32[]{:S(2)}) collective-permute-start(bf16[384,2048]{1,0:T(8,128)(2,1)} %add_convert_fusion.2), channel_id=1, source_target_pairs={{1,0},{2,3},{5,4},{6,7},{9,8},{10,11},{13,12},{14,15},{17,16},{18,... | collective-permute-start | bytes 4718600 | tf_op jit(solution)/shard_map/ppermute | solution.py:163
  718.7 94.3 %collective-permute-start.36 = (bf16[384,2048]{1,0:T(8,128)(2,1)}, bf16[384,2048]{1,0:T(8,128)(2,1)}, u32[]{:S(2)}, u32[]{:S(2)}) collective-permute-start(bf16[384,2048]{1,0:T(8,128)(2,1)} %add_convert_fusion.3), channel_id=1, source_target_pairs={{1,0},{2,3},{5,4},{6,7},{9,8},{10,11},{13,12},{14,15},{17,16},{18,... | collective-permute-start | bytes 4718600 | tf_op jit(solution)/shard_map/ppermute | solution.py:163
  771.7 97.2 %collective-permute-start.39 = (bf16[384,2048]{1,0:T(8,128)(2,1)}, bf16[384,2048]{1,0:T(8,128)(2,1)}, u32[]{:S(2)}, u32[]{:S(2)}) collective-permute-start(bf16[384,2048]{1,0:T(8,128)(2,1)} %broadcast_select_fusion.4), channel_id=1, source_target_pairs={{0,16},{4,20},{8,24},{12,28},{16,0},{20,4},{24,8},{28,12},{1,17},{... | collective-permute-start | bytes 4718600 | tf_op jit(solution)/shard_map/ppermute | solution.py:397
  831.2 82.6 %collective-permute-start.16 = (bf16[1024,768]{1,0:T(8,128)(2,1)}, bf16[1024,768]{1,0:T(8,128)(2,1)}, u32[]{:S(2)}, u32[]{:S(2)}) collective-permute-start(bf16[1024,768]{1,0:T(8,128)(2,1)} %add_convert_fusion.8), channel_id=1, source_target_pairs={{1,2},{2,1},{5,6},{6,5},{9,10},{10,9},{13,14},{14,13},{17,18},{18,... | collective-permute-start | bytes 4718600 | tf_op jit(solution)/shard_map/ppermute | solution.py:163
  926.6 98.0 %collective-permute-start.41 = (bf16[1024,768]{1,0:T(8,128)(2,1)S(1)}, bf16[1024,768]{1,0:T(8,128)(2,1)S(1)}, u32[]{:S(2)}, u32[]{:S(2)}) collective-permute-start(bf16[1024,768]{1,0:T(8,128)(2,1)S(1)} %add_convert_fusion), channel_id=1, source_target_pairs={{1,0},{2,3},{5,4},{6,7},{9,8},{10,11},{13,12},{14,15},{17,16},{18,... | collective-permute-start | bytes 4718600 | tf_op jit(solution)/shard_map/ppermute | solution.py:163
  932.5 83.4 %collective-permute-start.30 = (bf16[256,2048]{1,0:T(8,128)(2,1)S(1)}, bf16[256,2048]{1,0:T(8,128)(2,1)S(1)}, u32[]{:S(2)}, u32[]{:S(2)}) collective-permute-start(bf16[256,2048]{1,0:T(8,128)(2,1)S(1)} %copy-done.70), channel_id=1, source_target_pairs={{0,1},{3,2},{4,5},{7,6},{8,9},{11,10},{12,13},{15,14},{16,17},{19,... | collective-permute-start | bytes 3145736 | tf_op jit(solution)/shard_map/ppermute | solution.py:163
  945.6 73.6 %collective-permute-start.24 = (bf16[256,2048]{1,0:T(8,128)(2,1)S(1)}, bf16[256,2048]{1,0:T(8,128)(2,1)S(1)}, u32[]{:S(2)}, u32[]{:S(2)}) collective-permute-start(bf16[256,2048]{1,0:T(8,128)(2,1)S(1)} %get-tuple-element.142), channel_id=1, source_target_pairs={{0,1},{3,2},{4,5},{7,6},{8,9},{11,10},{12,13},{15,14},{16,17},{19,... | collective-permute-start | bytes 3145736 | tf_op jit(solution)/shard_map/ppermute | solution.py:163
  949.6 71.3 %collective-permute-start.27 = (bf16[256,2048]{1,0:T(8,128)(2,1)S(1)}, bf16[256,2048]{1,0:T(8,128)(2,1)S(1)}, u32[]{:S(2)}, u32[]{:S(2)}) collective-permute-start(bf16[256,2048]{1,0:T(8,128)(2,1)S(1)} %get-tuple-element.143), channel_id=1, source_target_pairs={{0,1},{3,2},{4,5},{7,6},{8,9},{11,10},{12,13},{15,14},{16,17},{19,... | collective-permute-start | bytes 3145736 | tf_op jit(solution)/shard_map/ppermute | solution.py:163
  1028.4 155.8 %all-to-all-start.7 = ((bf16[8,256,768]{2,1,0:T(8,128)(2,1)}), bf16[8,256,768]{2,1,0:T(8,128)(2,1)}, u32[]{:S(2)}, u32[]{:S(2)}) async-start(bf16[8,256,768]{2,1,0:T(8,128)(2,1)} %bitcast.44), calls=%async_computation.10 | async-start | bytes 6291456 | tf_op jit(solution)/shard_map/all_to_all | solution.py:400
  1037.1 136.6 %collective-permute-start.35 = (bf16[384,2048]{1,0:T(8,128)(2,1)}, bf16[384,2048]{1,0:T(8,128)(2,1)}, u32[]{:S(2)}, u32[]{:S(2)}) collective-permute-start(bf16[384,2048]{1,0:T(8,128)(2,1)} %add_convert_fusion.4), channel_id=1, source_target_pairs={{1,0},{2,3},{5,4},{6,7},{9,8},{10,11},{13,12},{14,15},{17,16},{18,... | collective-permute-start | bytes 4718600 | tf_op jit(solution)/shard_map/ppermute | solution.py:163
  1055.4 71.8 %collective-permute-start.26 = (bf16[256,2048]{1,0:T(8,128)(2,1)S(1)}, bf16[256,2048]{1,0:T(8,128)(2,1)S(1)}, u32[]{:S(2)}, u32[]{:S(2)}) collective-permute-start(bf16[256,2048]{1,0:T(8,128)(2,1)S(1)} %add_convert_fusion.16), channel_id=1, source_target_pairs={{1,0},{2,3},{5,4},{6,7},{9,8},{10,11},{13,12},{14,15},{17,16},{18,... | collective-permute-start | bytes 3145736 | tf_op jit(solution)/shard_map/ppermute | solution.py:163
  1058.7 93.7 %collective-permute-start.29 = (bf16[256,2048]{1,0:T(8,128)(2,1)S(1)}, bf16[256,2048]{1,0:T(8,128)(2,1)S(1)}, u32[]{:S(2)}, u32[]{:S(2)}) collective-permute-start(bf16[256,2048]{1,0:T(8,128)(2,1)S(1)} %add_convert_fusion.14), channel_id=1, source_target_pairs={{1,0},{2,3},{5,4},{6,7},{9,8},{10,11},{13,12},{14,15},{17,16},{18,... | collective-permute-start | bytes 3145736 | tf_op jit(solution)/shard_map/ppermute | solution.py:163
  1062.1 110.1 %collective-permute-start.32 = (bf16[256,2048]{1,0:T(8,128)(2,1)S(1)}, bf16[256,2048]{1,0:T(8,128)(2,1)S(1)}, u32[]{:S(2)}, u32[]{:S(2)}) collective-permute-start(bf16[256,2048]{1,0:T(8,128)(2,1)S(1)} %add_convert_fusion.12), channel_id=1, source_target_pairs={{1,0},{2,3},{5,4},{6,7},{9,8},{10,11},{13,12},{14,15},{17,16},{18,... | collective-permute-start | bytes 3145736 | tf_op jit(solution)/shard_map/ppermute | solution.py:163
  (131 other events, 2853.1 us)
Sparse Core Ops, SparseCore 0:
  9.9 92.4 all-gather.5
  104.3 54.2 all-gather.7
  262.3 102.2 all-gather.11
  366.3 75.0 all-gather.9
  500.9 71.1 reduce-scatter.3
  588.5 72.3 reduce-scatter.7
  662.8 54.2 all-gather.13
  729.3 104.0 reduce-scatter.5

commit v4 on v3

--- a/solution.py
+++ b/solution.py
@@ -374,7 +374,10 @@
     )
     grad_columns = lax.all_to_all(grad_projected, "fsdp", split_axis=1, concat_axis=0, tiled=True)
     out_chain = Chain(grad_out, line)
-    grad_columns = meet(grad_columns, [d1, k1], [out_chain])
+    grad_columns = meet(grad_columns, [d1, k1, s0, s1], [out_chain])
+    swapped_back = []
+    for chain in (s0, s1):
+        swapped_back.append(lax.ppermute(chain.finish(), "fsdp", swap))
     grad_normed1 = jnp.dot(grad_projected, qkv_full, preferred_element_type=f32)
     grad_qkv_own = product_tn(grad_columns, normed1_all).astype(low)
     back_one, attn_term = rms_backward(hidden, inverse1, attn_gain, grad_normed1)
@@ -391,11 +394,10 @@
     q0, q1 = (Chain(part, line) for part in halves(grad_qkv_own))
     q0.send()
     q1.send()
+    meet((), [out_chain])
+    swapped_back = [meet(swapped_back[0], [q0]), meet(swapped_back[1], [q1])]
     sums = sum_all(terms, (("fsdp", ways), ("sp", line)))
-    grad_swapped = []
-    for chain in (s0, s1):
-        grad_swapped.append(lax.ppermute(chain.finish(), "fsdp", swap))
-    grad_swapped = jnp.concatenate(grad_swapped, 0)
+    grad_swapped = jnp.concatenate(swapped_back, 0)
     grad_down_sum = jnp.concatenate([d0.finish(), d1.finish()], 0)
     down_back = lax.all_to_all(
         grad_down_sum.reshape(ways, -1, units),

time: 1220 us -> 1110 us (0.910)
  waiting for transfers between devices: 572 us -> 454 us
  other arithmetic: 143 us -> 159 us
    ppermute x27, waiting for transfers between devices: 214 us -> 110 us  [send(): self.flying = lax.ppermute(self.value, 'sp', self.hops[self.at][0])]
    ppermute x5, waiting for transfers between devices: 58.4 us -> 21.8 us  [sum_all(): lax.ppermute(values, axis, [(d, d ^ step) for d in range(size)])]
    all_to_all x1, waiting for transfers between devices: 0.01 us -> 24.4 us  [layer(): lax.all_to_all(grads_send, 'sp', split_axis=0, concat_axis=1, tiled=True)]
    unnamed x220 -> x208, local copies, waits for them, and re-layouts: 31.6 us -> 31.2 us
  transfers between devices with their start and end apart: 57 -> 57, of which waited for: 22 -> 23; matrix products, arithmetic and copies ran while one was open for 28% -> 33% of each run, Pallas kernels for 0% -> 0%
where the time goes in v4:
time: 1110 us; the launch traced here: 1100 us
  waiting for transfers between devices  454 us (41%)
  matrix products  170 us (15%)
  other arithmetic  159 us (14%)
  starting transfers between devices  135 us (12%)
  local copies, waits for them, and re-layouts  134 us (12%)
  blocking collectives  28.6 us (3%)
  between operations  16.2 us (1%)
    ppermute x7, waiting for transfers between devices, turn(): arrived = lax.ppermute(block, 'fsdp', pairs)  132 us
    ppermute x27, waiting for transfers between devices, send(): self.flying = lax.ppermute(self.value, 'sp', self.hops[self.at][0])  110 us
    all_gather x5, waiting for transfers between devices, gather_rows(): return lax.all_gather(array, 'fsdp', axis=0, tiled=True)  94.4 us
    ppermute x27, starting transfers between devices, send(): self.flying = lax.ppermute(self.value, 'sp', self.hops[self.at][0])  69.6 us
    convert_element_type x16, other arithmetic, take(): self.value = total.astype(jnp.bfloat16)  54.9 us
    dot_general x4, matrix products, product_nt(): lax.dot_general(inputs, weight, (((1,), (1,)), ((), ())), preferred_eleme...  44 us
    dot_general x5, matrix products, product_tn(): lax.dot_general(left, right, (((0,), (0,)), ((), ())), preferred_element_...  42 us
    unnamed x208, local copies, waits for them, and re-layouts  31.2 us
  transfers between devices with their start and end apart: 57, of which 23 were waited for; matrix products, arithmetic and copies ran while one was open for 33% of the time, Pallas kernels for 0%

profile of v4, /device:TPU:0, one launch (start us, length us, event | category | flops | bytes accessed | tf_op | source)
XLA Modules:
  0.0 1097.9 jit_solution(1134857628948280559)
XLA Ops:
  8.0 94.4 %all-gather.6.cloned.1.call-done = bf16[4096,2048]{1,0:T(8,128)(2,1)} async-done(((bf16[512,2048]{1,0:T(8,128)(2,1)}), bf16[4096,2048]{1,0:T(8,128)(2,1)}) %all-gather.6.cloned.1.call-update) | async-done | bytes 16777232 | tf_op jit(solution)/shard_map/all_gather | solution.py:123
  105.0 10.7 fusion.58
  138.8 8.6 all-to-all-done.2
  176.6 18.3 %all-to-all-done.1 = bf16[256,4,512]{2,0,1:T(8,128)(2,1)S(1)} async-done(((bf16[256,4,512]{2,0,1:T(8,128)(2,1)}), bf16[256,4,512]{2,0,1:T(8,128)(2,1)S(1)}, u32[]{:S(2)}, u32[]{:S(2)}) %all-to-all-start.1) | async-done | bytes 1048608 | tf_op jit(solution)/shard_map/all_to_all | solution.py:279
  211.8 28.6 %all_to_all.126 = bf16[4,256,512]{1,2,0:T(8,128)(2,1)} all-to-all(bf16[4,256,512]{1,2,0:T(8,128)(2,1)S(1)} %copy.302), channel_id=1, replica_groups=mesh['fsdp'=8,'sp'=4] {'sp'}, dimensions={0} | all-to-all | bytes 2097152 | tf_op jit(solution)/shard_map/all_to_all | solution.py:289
  274.6 8.0 collective-permute-done
  286.4 106.6 %collective-permute-done.2 = bf16[1,256,768]{2,1,0:T(8,128)(2,1)S(1)} collective-permute-done((bf16[1,256,768]{2,1,0:T(8,128)(2,1)}, bf16[1,256,768]{2,1,0:T(8,128)(2,1)S(1)}, u32[]{:S(2)}, u32[]{:S(2)}) %collective-permute-start.2) | collective-permute-done | bytes 393248 | tf_op jit(solution)/shard_map/ppermute | solution.py:208
  398.6 13.2 %collective-permute-done.4 = bf16[1,256,768]{2,1,0:T(8,128)(2,1)S(1)} collective-permute-done((bf16[1,256,768]{2,1,0:T(8,128)(2,1)}, bf16[1,256,768]{2,1,0:T(8,128)(2,1)S(1)}, u32[]{:S(2)}, u32[]{:S(2)}) %collective-permute-start.4) | collective-permute-done | bytes 393248 | tf_op jit(solution)/shard_map/ppermute | solution.py:208
  414.1 17.9 %fusion.5 = f32[2048,1536]{0,1:T(8,128)S(1)} fusion(bf16[2048,2048]{1,0:T(8,128)(2,1)} %all-gather.12.cloned.1.call-done, bf16[768,2048]{1,0:T(8,128)(2,1)} %collective-permute-done.7, bf16[768,2048]{1,0:T(8,128)(2,1)} %get-tuple-element.134), kind=kOutput, calls=%fused_computation.33 | convolution fusion | flops 12897484800 | bytes 27262976 | tf_op jit(solution)/shard_map/dot_general | solution.py:127
  441.5 19.1 %select_convert_fusion.1 = (bf16[2048,768]{0,1:T(8,128)(2,1)}, bf16[2048,768]{0,1:T(8,128)(2,1)}, f32[2048,768]{0,1:T(8,128)}) fusion(pred[]{:T(512)S(6)} %eq.34, f32[2048,768]{0,1:T(8,128)} %get-tuple-element.127, f32[2048,1536]{0,1:T(8,128)} %copy-done.10, bf16[2048,2048]{1,0:T(8,128)(2,1)} %all-gather.10.cloned.1.call-done, bf16[2048,768]{1,0:T(8,128)(2,1)} %bitcast.244), kind=kOutput, calls=%fused_computation.16 | convolution fusion | flops 6464471040 | bytes 42991616 | tf_op jit(solution)/shard_map/dot_general | solution.py:298
  468.0 18.7 %convolution_convert_fusion.2 = bf16[2048,2048]{1,0:T(8,128)(2,1)} fusion(bf16[2048,768]{0,1:T(8,128)(2,1)S(1)} %select_convert_fusion, bf16[2048,768]{0,1:T(8,128)(2,1)} %get-tuple-element.128, bf16[768,2048]{1,0:T(8,128)(2,1)} %collective-permute-done.7, bf16[768,2048]{1,0:T(8,128)(2,1)S(1)} %copy-done.54), kind=kOutput, calls=%fused_computation.6 | convolution fusion | flops 12914262016 | bytes 20971520 | tf_op jit(solution)/shard_map/dot_general | solution.py:310
  486.9 10.0 convolution_convert_fusion.4
  503.9 9.6 convolution_convert_fusion.5
  513.5 8.1 convolution_convert_fusion.3
  521.6 13.3 %collective-permute-done.8 = bf16[384,2048]{1,0:T(8,128)(2,1)S(1)} collective-permute-done((bf16[384,2048]{1,0:T(8,128)(2,1)S(1)}, bf16[384,2048]{1,0:T(8,128)(2,1)S(1)}, u32[]{:S(2)}, u32[]{:S(2)}) %collective-permute-start.8) | collective-permute-done | bytes 1572896 | tf_op jit(solution)/shard_map/ppermute | solution.py:163
  537.9 20.3 %reduce-scatter.4.cloned.1.call-done = bf16[256,2048]{1,0:T(8,128)(2,1)} async-done(((bf16[2048,2048]{1,0:T(8,128)(2,1)}), bf16[256,2048]{1,0:T(8,128)(2,1)}) %reduce-scatter.4.cloned.1.call-update) | async-done | bytes 1048592 | tf_op jit(solution)/shard_map/reduce_scatter | solution.py:139
  601.8 7.3 collective-permute-start.12
  663.8 25.6 %all-to-all-start.5 = ((bf16[4,256,1024]{1,2,0:T(8,128)(2,1)}), bf16[4,256,1024]{1,2,0:T(8,128)(2,1)}, u32[]{:S(2)}, u32[]{:S(2)}) async-start(bf16[4,256,1024]{1,2,0:T(8,128)(2,1)} %copy.320), calls=%async_computation.7 | async-start | bytes 4194304 | tf_op jit(solution)/shard_map/all_to_all | solution.py:346
  705.2 9.1 convolution_convert_fusion.1
  714.4 24.4 %all-to-all-done.5 = bf16[4,256,1024]{1,2,0:T(8,128)(2,1)} async-done(((bf16[4,256,1024]{1,2,0:T(8,128)(2,1)}), bf16[4,256,1024]{1,2,0:T(8,128)(2,1)}, u32[]{:S(2)}, u32[]{:S(2)}) %all-to-all-start.5) | async-done | bytes 2097184 | tf_op jit(solution)/shard_map/all_to_all | solution.py:346
  801.5 12.5 %fusion.23 = (f32[2048]{0:T(1024)S(1)}, f32[256]{0:T(256)S(1)}, f32[256,2048]{1,0:T(8,128)}) fusion(bf16[256,2048]{1,0:T(8,128)(2,1)S(1)} %copy-done.15, f32[256]{0:T(256)S(1)} %copy-done.81, f32[2048]{0:T(1024)S(1)} %copy-done.78, bf16[4096,2048]{1,0:T(8,128)(2,1)} %all-gather.6.cloned.1.call-done, bf16[256,1024]{0,1:T(8,128)(2,1)} %bitcast.255, ...), kind=kOutput, calls=%fused_computation.74 | convolution fusion | flops 4304926720 | bytes 22038528 | tf_op jit(solution)/shard_map/dot_general | solution.py:381
  819.8 9.2 collective-permute-done.40
  842.4 8.6 convolution_convert_fusion.6
  866.1 17.1 %collective-permute-start.34 = (bf16[256,2048]{1,0:T(8,128)(2,1)S(1)}, bf16[256,2048]{1,0:T(8,128)(2,1)S(1)}, u32[]{:S(2)}, u32[]{:S(2)}) collective-permute-start(bf16[256,2048]{1,0:T(8,128)(2,1)S(1)} %copy-done.66), channel_id=1, source_target_pairs={{0,1},{3,2},{4,5},{7,6},{8,9},{11,10},{12,13},{15,14},{16,17},{19,... | collective-permute-start | bytes 3145736 | tf_op jit(solution)/shard_map/ppermute | solution.py:163
  886.1 19.6 %collective-permute-done.24 = f32[4352]{0:T(1024)S(1)} collective-permute-done((f32[4352]{0:T(1024)S(1)}, f32[4352]{0:T(1024)S(1)}, u32[]{:S(2)}, u32[]{:S(2)}) %collective-permute-start.24) | collective-permute-done | bytes 17440 | tf_op jit(solution)/shard_map/ppermute | solution.py:220
  941.6 17.6 %collective-permute-done.27 = bf16[256,2048]{1,0:T(8,128)(2,1)} collective-permute-done((bf16[256,2048]{1,0:T(8,128)(2,1)}, bf16[256,2048]{1,0:T(8,128)(2,1)}, u32[]{:S(2)}, u32[]{:S(2)}) %collective-permute-start.27) | collective-permute-done | bytes 1048608 | tf_op jit(solution)/shard_map/ppermute | solution.py:163
  959.2 12.2 %collective-permute-done.26 = bf16[384,2048]{1,0:T(8,128)(2,1)} collective-permute-done((bf16[384,2048]{1,0:T(8,128)(2,1)}, bf16[384,2048]{1,0:T(8,128)(2,1)}, u32[]{:S(2)}, u32[]{:S(2)}) %collective-permute-start.26) | collective-permute-done | bytes 1572896 | tf_op jit(solution)/shard_map/ppermute | solution.py:380
  1013.6 12.5 %collective-permute-done.36 = bf16[256,2048]{1,0:T(8,128)(2,1)S(1)} collective-permute-done((bf16[256,2048]{1,0:T(8,128)(2,1)S(1)}, bf16[256,2048]{1,0:T(8,128)(2,1)S(1)}, u32[]{:S(2)}, u32[]{:S(2)}) %collective-permute-start.36) | collective-permute-done | bytes 1048608 | tf_op jit(solution)/shard_map/ppermute | solution.py:163
  1027.6 21.1 %collective-permute-done.29 = bf16[256,2048]{1,0:T(8,128)(2,1)} collective-permute-done((bf16[256,2048]{1,0:T(8,128)(2,1)S(1)}, bf16[256,2048]{1,0:T(8,128)(2,1)}, u32[]{:S(2)}, u32[]{:S(2)}) %collective-permute-start.29) | collective-permute-done | bytes 1048608 | tf_op jit(solution)/shard_map/ppermute | solution.py:163
  1050.0 20.5 %collective-permute-done.33 = bf16[256,2048]{1,0:T(8,128)(2,1)} collective-permute-done((bf16[256,2048]{1,0:T(8,128)(2,1)S(1)}, bf16[256,2048]{1,0:T(8,128)(2,1)}, u32[]{:S(2)}, u32[]{:S(2)}) %collective-permute-start.33) | collective-permute-done | bytes 1048608 | tf_op jit(solution)/shard_map/ppermute | solution.py:163
  1074.4 7.7 copy.388
  1082.2 8.7 reshape.378
  (492 shorter events, 442.3 us)
Async XLA Ops:
  7.2 95.2 %all-gather.6.cloned.1.call-start = ((), (), s32[]{:S(2)}) async-start(), calls=%async_computation.11 | async-start | bytes 18874368 | tf_op jit(solution)/shard_map/all_gather | solution.py:123
  8.0 232.4 %all-gather.8.cloned.1.call-start = ((), (), s32[]{:S(2)}) async-start(), calls=%async_computation.12 | async-start | bytes 9437184 | tf_op jit(solution)/shard_map/all_gather | solution.py:123
  169.7 244.5 %all-gather.12.cloned.1.call-start = ((), (), s32[]{:S(2)}) async-start(), calls=%async_computation.14 | async-start | bytes 9437184 | tf_op jit(solution)/shard_map/all_gather | solution.py:123
  247.9 193.6 %all-gather.10.cloned.1.call-start = ((), (), s32[]{:S(2)}) async-start(), calls=%async_computation.13 | async-start | bytes 9437184 | tf_op jit(solution)/shard_map/all_gather | solution.py:123
  248.5 309.7 %reduce-scatter.4.cloned.1.call-start = ((), (), s32[]{:S(2)}) async-start(), calls=%async_computation.15 | async-start | bytes 9437184 | tf_op jit(solution)/shard_map/reduce_scatter | solution.py:139
  255.4 158.7 %collective-permute-start.7 = (bf16[768,2048]{1,0:T(8,128)(2,1)}, bf16[768,2048]{1,0:T(8,128)(2,1)}, u32[]{:S(2)}, u32[]{:S(2)}) collective-permute-start(bf16[768,2048]{1,0:T(8,128)(2,1)} %get-tuple-element.135), channel_id=1, source_target_pairs={{0,16},{4,20},{8,24},{12,28},{16,0},{20,4},{24,8},{28,12},{1,17},{... | collective-permute-start | bytes 9437192 | tf_op jit(solution)/shard_map/ppermute | solution.py:262
  271.7 121.3 %collective-permute-start.2 = (bf16[1,256,768]{2,1,0:T(8,128)(2,1)}, bf16[1,256,768]{2,1,0:T(8,128)(2,1)S(1)}, u32[]{:S(2)}, u32[]{:S(2)}) collective-permute-start(bf16[1,256,768]{2,1,0:T(8,128)(2,1)} %get-tuple-element.148), channel_id=1, source_target_pairs={{0,12},{4,16},{8,20},{12,24},{16,28},{20,0},{24,4},{28,8},{1,13},{... | collective-permute-start | bytes 1179656 | tf_op jit(solution)/shard_map/ppermute | solution.py:208
  274.1 123.7 %collective-permute-start.3 = (bf16[1,256,768]{2,1,0:T(8,128)(2,1)}, bf16[1,256,768]{2,1,0:T(8,128)(2,1)S(1)}, u32[]{:S(2)}, u32[]{:S(2)}) collective-permute-start(bf16[1,256,768]{2,1,0:T(8,128)(2,1)} %get-tuple-element.147), channel_id=1, source_target_pairs={{0,16},{4,20},{8,24},{12,28},{16,0},{20,4},{24,8},{28,12},{1,17},{... | collective-permute-start | bytes 1179656 | tf_op jit(solution)/shard_map/ppermute | solution.py:208
  282.5 129.2 %collective-permute-start.4 = (bf16[1,256,768]{2,1,0:T(8,128)(2,1)}, bf16[1,256,768]{2,1,0:T(8,128)(2,1)S(1)}, u32[]{:S(2)}, u32[]{:S(2)}) collective-permute-start(bf16[1,256,768]{2,1,0:T(8,128)(2,1)} %get-tuple-element.146), channel_id=1, source_target_pairs={{0,20},{4,24},{8,28},{12,0},{16,4},{20,8},{24,12},{28,16},{1,21},{... | collective-permute-start | bytes 1179656 | tf_op jit(solution)/shard_map/ppermute | solution.py:208
  284.4 128.2 %collective-permute-start.5 = (bf16[1,256,768]{2,1,0:T(8,128)(2,1)}, bf16[1,256,768]{2,1,0:T(8,128)(2,1)S(1)}, u32[]{:S(2)}, u32[]{:S(2)}) collective-permute-start(bf16[1,256,768]{2,1,0:T(8,128)(2,1)} %get-tuple-element.145), channel_id=1, source_target_pairs={{0,24},{4,28},{8,0},{12,4},{16,8},{20,12},{24,16},{28,20},{1,25},{... | collective-permute-start | bytes 1179656 | tf_op jit(solution)/shard_map/ppermute | solution.py:208
  486.8 350.8 %reduce-scatter.8.cloned.1.call-start = ((), (), s32[]{:S(2)}) async-start(), calls=%async_computation.17 | async-start | bytes 9437184 | tf_op jit(solution)/shard_map/reduce_scatter | solution.py:139
  501.2 67.5 %collective-permute-start.10 = (bf16[384,2048]{1,0:T(8,128)(2,1)}, bf16[384,2048]{1,0:T(8,128)(2,1)}, u32[]{:S(2)}, u32[]{:S(2)}) collective-permute-start(bf16[384,2048]{1,0:T(8,128)(2,1)} %get-tuple-element.142), channel_id=1, source_target_pairs={{0,1},{3,2},{4,5},{7,6},{8,9},{11,10},{12,13},{15,14},{16,17},{19,... | collective-permute-start | bytes 4718600 | tf_op jit(solution)/shard_map/ppermute | solution.py:163
  574.5 267.9 %all-gather.14.cloned.1.call-start = ((), (), s32[]{:S(2)}) async-start(), calls=%async_computation.18 | async-start | bytes 9437184 | tf_op jit(solution)/shard_map/all_gather | solution.py:123
  600.0 59.8 %collective-permute-start.11 = (bf16[384,2048]{1,0:T(8,128)(2,1)}, bf16[384,2048]{1,0:T(8,128)(2,1)}, u32[]{:S(2)}, u32[]{:S(2)}) collective-permute-start(bf16[384,2048]{1,0:T(8,128)(2,1)} %get-tuple-element.138), channel_id=1, source_target_pairs={{1,2},{2,1},{5,6},{6,5},{9,10},{10,9},{13,14},{14,13},{17,18},{18,... | collective-permute-start | bytes 4718600 | tf_op jit(solution)/shard_map/ppermute | solution.py:163
  601.8 58.0 %collective-permute-start.12 = (bf16[1024,768]{1,0:T(8,128)(2,1)}, bf16[1024,768]{1,0:T(8,128)(2,1)}, u32[]{:S(2)}, u32[]{:S(2)}) collective-permute-start(bf16[1024,768]{1,0:T(8,128)(2,1)} %get-tuple-element.87), channel_id=1, source_target_pairs={{0,1},{3,2},{4,5},{7,6},{8,9},{11,10},{12,13},{15,14},{16,17},{19,... | collective-permute-start | bytes 4718600 | tf_op jit(solution)/shard_map/ppermute | solution.py:163
  609.1 105.2 %collective-permute-start.13 = (bf16[1024,768]{1,0:T(8,128)(2,1)}, bf16[1024,768]{1,0:T(8,128)(2,1)}, u32[]{:S(2)}, u32[]{:S(2)}) collective-permute-start(bf16[1024,768]{1,0:T(8,128)(2,1)} %get-tuple-element.90), channel_id=1, source_target_pairs={{0,1},{3,2},{4,5},{7,6},{8,9},{11,10},{12,13},{15,14},{16,17},{19,... | collective-permute-start | bytes 4718600 | tf_op jit(solution)/shard_map/ppermute | solution.py:163
  663.8 75.0 %all-to-all-start.5 = ((bf16[4,256,1024]{1,2,0:T(8,128)(2,1)}), bf16[4,256,1024]{1,2,0:T(8,128)(2,1)}, u32[]{:S(2)}, u32[]{:S(2)}) async-start(bf16[4,256,1024]{1,2,0:T(8,128)(2,1)} %copy.320), calls=%async_computation.7 | async-start | bytes 4194304 | tf_op jit(solution)/shard_map/all_to_all | solution.py:346
  689.4 289.0 %reduce-scatter.6.cloned.1.call-start = ((), (), s32[]{:S(2)}) async-start(), calls=%async_computation.16 | async-start | bytes 9437184 | tf_op jit(solution)/shard_map/reduce_scatter | solution.py:139
  693.0 91.9 %collective-permute-start.14 = (bf16[1024,768]{1,0:T(8,128)(2,1)}, bf16[1024,768]{1,0:T(8,128)(2,1)}, u32[]{:S(2)}, u32[]{:S(2)}) collective-permute-start(bf16[1024,768]{1,0:T(8,128)(2,1)} %add_convert_fusion.9), channel_id=1, source_target_pairs={{1,2},{2,1},{5,6},{6,5},{9,10},{10,9},{13,14},{14,13},{17,18},{18,... | collective-permute-start | bytes 4718600 | tf_op jit(solution)/shard_map/ppermute | solution.py:163
  698.7 138.9 %collective-permute-start.19 = (bf16[384,2048]{1,0:T(8,128)(2,1)}, bf16[384,2048]{1,0:T(8,128)(2,1)}, u32[]{:S(2)}, u32[]{:S(2)}) collective-permute-start(bf16[384,2048]{1,0:T(8,128)(2,1)} %add_convert_fusion.6), channel_id=1, source_target_pairs={{1,0},{2,3},{5,4},{6,7},{9,8},{10,11},{13,12},{14,15},{17,16},{18,... | collective-permute-start | bytes 4718600 | tf_op jit(solution)/shard_map/ppermute | solution.py:163
  703.9 133.6 %collective-permute-start.18 = (bf16[384,2048]{1,0:T(8,128)(2,1)}, bf16[384,2048]{1,0:T(8,128)(2,1)}, u32[]{:S(2)}, u32[]{:S(2)}) collective-permute-start(bf16[384,2048]{1,0:T(8,128)(2,1)} %add_convert_fusion.7), channel_id=1, source_target_pairs={{1,0},{2,3},{5,4},{6,7},{9,8},{10,11},{13,12},{14,15},{17,16},{18,... | collective-permute-start | bytes 4718600 | tf_op jit(solution)/shard_map/ppermute | solution.py:163
  756.8 80.8 %collective-permute-start.16 = (bf16[1024,768]{1,0:T(8,128)(2,1)}, bf16[1024,768]{1,0:T(8,128)(2,1)}, u32[]{:S(2)}, u32[]{:S(2)}) collective-permute-start(bf16[1024,768]{1,0:T(8,128)(2,1)} %add_convert_fusion.8), channel_id=1, source_target_pairs={{1,2},{2,1},{5,6},{6,5},{9,10},{10,9},{13,14},{14,13},{17,18},{18,... | collective-permute-start | bytes 4718600 | tf_op jit(solution)/shard_map/ppermute | solution.py:163
  784.8 52.7 %collective-permute-start.17 = (bf16[384,2048]{1,0:T(8,128)(2,1)}, bf16[384,2048]{1,0:T(8,128)(2,1)}, u32[]{:S(2)}, u32[]{:S(2)}) collective-permute-start(bf16[384,2048]{1,0:T(8,128)(2,1)} %get-tuple-element.97), channel_id=1, source_target_pairs={{0,1},{3,2},{4,5},{7,6},{8,9},{11,10},{12,13},{15,14},{16,17},{19,... | collective-permute-start | bytes 4718600 | tf_op jit(solution)/shard_map/ppermute | solution.py:163
  841.0 79.0 %collective-permute-start.41 = (bf16[1024,768]{1,0:T(8,128)(2,1)}, bf16[1024,768]{1,0:T(8,128)(2,1)}, u32[]{:S(2)}, u32[]{:S(2)}) collective-permute-start(bf16[1024,768]{1,0:T(8,128)(2,1)} %add_convert_fusion), channel_id=1, source_target_pairs={{1,0},{2,3},{5,4},{6,7},{9,8},{10,11},{13,12},{14,15},{17,16},{18,... | collective-permute-start | bytes 4718600 | tf_op jit(solution)/shard_map/ppermute | solution.py:163
  859.3 71.1 %collective-permute-start.38 = (bf16[384,2048]{1,0:T(8,128)(2,1)}, bf16[384,2048]{1,0:T(8,128)(2,1)}, u32[]{:S(2)}, u32[]{:S(2)}) collective-permute-start(bf16[384,2048]{1,0:T(8,128)(2,1)} %add_convert_fusion.3), channel_id=1, source_target_pairs={{1,2},{2,1},{5,6},{6,5},{9,10},{10,9},{13,14},{14,13},{17,18},{18,... | collective-permute-start | bytes 4718600 | tf_op jit(solution)/shard_map/ppermute | solution.py:163
  866.0 74.4 %collective-permute-start.30 = (bf16[384,2048]{1,0:T(8,128)(2,1)}, bf16[384,2048]{1,0:T(8,128)(2,1)}, u32[]{:S(2)}, u32[]{:S(2)}) collective-permute-start(bf16[384,2048]{1,0:T(8,128)(2,1)} %broadcast_select_fusion.6), channel_id=1, source_target_pairs={{0,16},{4,20},{8,24},{12,28},{16,0},{20,4},{24,8},{28,12},{1,17},{... | collective-permute-start | bytes 4718600 | tf_op jit(solution)/shard_map/ppermute | solution.py:380
  917.0 54.4 %collective-permute-start.26 = (bf16[384,2048]{1,0:T(8,128)(2,1)}, bf16[384,2048]{1,0:T(8,128)(2,1)}, u32[]{:S(2)}, u32[]{:S(2)}) collective-permute-start(bf16[384,2048]{1,0:T(8,128)(2,1)} %broadcast_select_fusion.7), channel_id=1, source_target_pairs={{0,16},{4,20},{8,24},{12,28},{16,0},{20,4},{24,8},{28,12},{1,17},{... | collective-permute-start | bytes 4718600 | tf_op jit(solution)/shard_map/ppermute | solution.py:380
  926.0 148.5 %all-to-all-start.7 = ((bf16[8,256,768]{2,1,0:T(8,128)(2,1)}), bf16[8,256,768]{2,1,0:T(8,128)(2,1)}, u32[]{:S(2)}, u32[]{:S(2)}) async-start(bf16[8,256,768]{2,1,0:T(8,128)(2,1)} %bitcast.210), calls=%async_computation.10 | async-start | bytes 6291456 | tf_op jit(solution)/shard_map/all_to_all | solution.py:402
  930.4 56.3 %collective-permute-start.37 = (bf16[384,2048]{1,0:T(8,128)(2,1)}, bf16[384,2048]{1,0:T(8,128)(2,1)}, u32[]{:S(2)}, u32[]{:S(2)}) collective-permute-start(bf16[384,2048]{1,0:T(8,128)(2,1)} %add_convert_fusion.4), channel_id=1, source_target_pairs={{1,0},{2,3},{5,4},{6,7},{9,8},{10,11},{13,12},{14,15},{17,16},{18,... | collective-permute-start | bytes 4718600 | tf_op jit(solution)/shard_map/ppermute | solution.py:163
  940.4 63.4 %collective-permute-start.39 = (bf16[384,2048]{1,0:T(8,128)(2,1)}, bf16[384,2048]{1,0:T(8,128)(2,1)}, u32[]{:S(2)}, u32[]{:S(2)}) collective-permute-start(bf16[384,2048]{1,0:T(8,128)(2,1)} %add_convert_fusion.2), channel_id=1, source_target_pairs={{1,0},{2,3},{5,4},{6,7},{9,8},{10,11},{13,12},{14,15},{17,16},{18,... | collective-permute-start | bytes 4718600 | tf_op jit(solution)/shard_map/ppermute | solution.py:163
  993.6 55.1 %collective-permute-start.29 = (bf16[256,2048]{1,0:T(8,128)(2,1)S(1)}, bf16[256,2048]{1,0:T(8,128)(2,1)}, u32[]{:S(2)}, u32[]{:S(2)}) collective-permute-start(bf16[256,2048]{1,0:T(8,128)(2,1)S(1)} %add_convert_fusion.16), channel_id=1, source_target_pairs={{1,0},{2,3},{5,4},{6,7},{9,8},{10,11},{13,12},{14,15},{17,16},{18,... | collective-permute-start | bytes 3145736 | tf_op jit(solution)/shard_map/ppermute | solution.py:163
  996.9 73.7 %collective-permute-start.33 = (bf16[256,2048]{1,0:T(8,128)(2,1)S(1)}, bf16[256,2048]{1,0:T(8,128)(2,1)}, u32[]{:S(2)}, u32[]{:S(2)}) collective-permute-start(bf16[256,2048]{1,0:T(8,128)(2,1)S(1)} %add_convert_fusion.14), channel_id=1, source_target_pairs={{1,0},{2,3},{5,4},{6,7},{9,8},{10,11},{13,12},{14,15},{17,16},{18,... | collective-permute-start | bytes 3145736 | tf_op jit(solution)/shard_map/ppermute | solution.py:163
  (125 other events, 2313.9 us)
Sparse Core Ops, SparseCore 0:
  9.9 92.4 all-gather.5
  104.3 54.2 all-gather.7
  248.0 102.2 all-gather.11
  352.0 75.0 all-gather.9
  486.9 71.2 reduce-scatter.3
  574.6 72.3 reduce-scatter.7
  648.9 54.2 all-gather.13
  714.5 76.3 reduce-scatter.5

commit v5 on v4

--- a/solution.py
+++ b/solution.py
@@ -342,10 +342,10 @@
         grad_values.reshape(length, local_kv, group, HD).sum(2).astype(low).reshape(length, -1)
     )
     grads_send = jnp.concatenate([grad_query_send, grad_key_send, grad_value_send], 1)
-    grads_send, activation = meet((grads_send, activation), [s1, d0])
+    grads_send, activation = meet((grads_send, activation), [s1, d0], [k0, k1])
     grads_low = lax.all_to_all(grads_send, "sp", split_axis=0, concat_axis=1, tiled=True)
     hidden_out = (middle + scatter_sum(product_nt(activation, down_own))).astype(low)
-    grads_low = meet(grads_low, [d1], [k0, k1])
+    grads_low = meet(grads_low, [d1])
     grads_low = grads_low.reshape(rows, line, -1)
     cuts = (grad_query_send.shape[1], grad_query_send.shape[1] + grad_key_send.shape[1])
     grad_query_low = grads_low[:, :, : cuts[0]]
@@ -374,7 +374,7 @@
     )
     grad_columns = lax.all_to_all(grad_projected, "fsdp", split_axis=1, concat_axis=0, tiled=True)
     out_chain = Chain(grad_out, line)
-    grad_columns = meet(grad_columns, [d1, k1, s0, s1], [out_chain])
+    grad_columns = meet(grad_columns, [d1, k0, k1, s0, s1], [out_chain])
     swapped_back = []
     for chain in (s0, s1):
         swapped_back.append(lax.ppermute(chain.finish(), "fsdp", swap))
@@ -390,13 +390,13 @@
             jnp.sum(key_term, axis=(0, 1)),
         ]
     )
-    grad_qkv_own, terms = meet((grad_qkv_own, terms), [k0])
+    grad_qkv_own, terms = meet((grad_qkv_own, terms), [])
     q0, q1 = (Chain(part, line) for part in halves(grad_qkv_own))
     q0.send()
     q1.send()
     meet((), [out_chain])
+    meet((), [k1])
     swapped_back = [meet(swapped_back[0], [q0]), meet(swapped_back[1], [q1])]
-    sums = sum_all(terms, (("fsdp", ways), ("sp", line)))
     grad_swapped = jnp.concatenate(swapped_back, 0)
     grad_down_sum = jnp.concatenate([d0.finish(), d1.finish()], 0)
     down_back = lax.all_to_all(
@@ -406,6 +406,8 @@
         concat_axis=0,
         tiled=True,
     )
+    down_back, terms = meet((down_back, terms), [])
+    sums = sum_all(terms, (("fsdp", ways), ("sp", line)))
     grad_down = (
         down_back.reshape(2, pairs_of, -1, units)
         .transpose(2, 1, 0, 3)

time: 1110 us -> 1140 us (1.027)
  waiting for transfers between devices: 454 us -> 489 us
    ppermute x27, waiting for transfers between devices: 110 us -> 193 us  [send(): self.flying = lax.ppermute(self.value, 'sp', self.hops[self.at][0])]
    ppermute x5, waiting for transfers between devices: 21.8 us -> 0.01 us  [sum_all(): lax.ppermute(values, axis, [(d, d ^ step) for d in range(size)])]
    all_to_all x1, waiting for transfers between devices: 24.4 us -> 10.9 us  [layer(): lax.all_to_all(grads_send, 'sp', split_axis=0, concat_axis=1, tiled=True)]
    ppermute x27, starting transfers between devices: 69.6 us -> 82.9 us  [send(): self.flying = lax.ppermute(self.value, 'sp', self.hops[self.at][0])]
    ppermute x2, waiting for transfers between devices: 12.2 us -> 0.01 us  [layer(): swapped_back.append(lax.ppermute(chain.finish(), 'fsdp', swap))]
    unnamed x208 -> x212, local copies, waits for them, and re-layouts: 31.2 us -> 32.4 us
where the time goes in v5:
time: 1140 us; the launch traced here: 1130 us
  waiting for transfers between devices  489 us (43%)
  matrix products  169 us (15%)
  other arithmetic  155 us (14%)
  starting transfers between devices  144 us (13%)
  local copies, waits for them, and re-layouts  132 us (12%)
  blocking collectives  28.6 us (3%)
  between operations  16.3 us (1%)
    ppermute x27, waiting for transfers between devices, send(): self.flying = lax.ppermute(self.value, 'sp', self.hops[self.at][0])  193 us
    ppermute x7, waiting for transfers between devices, turn(): arrived = lax.ppermute(block, 'fsdp', pairs)  132 us
    all_gather x5, waiting for transfers between devices, gather_rows(): return lax.all_gather(array, 'fsdp', axis=0, tiled=True)  94.4 us
    ppermute x27, starting transfers between devices, send(): self.flying = lax.ppermute(self.value, 'sp', self.hops[self.at][0])  82.9 us
    convert_element_type x16, other arithmetic, take(): self.value = total.astype(jnp.bfloat16)  53.4 us
    dot_general x4, matrix products, product_nt(): lax.dot_general(inputs, weight, (((1,), (1,)), ((), ())), preferred_eleme...  44 us
    dot_general x5, matrix products, product_tn(): lax.dot_general(left, right, (((0,), (0,)), ((), ())), preferred_element_...  42.1 us
    unnamed x212, local copies, waits for them, and re-layouts  32.4 us
  transfers between devices with their start and end apart: 57, of which 23 were waited for; matrix products, arithmetic and copies ran while one was open for 33% of the time, Pallas kernels for 0%

profile of v5, /device:TPU:0, one launch (start us, length us, event | category | flops | bytes accessed | tf_op | source)
XLA Modules:
  0.0 1134.8 jit_solution(8893480457897673199)
XLA Ops:
  8.0 94.4 %all-gather.6.cloned.1.call-done = bf16[4096,2048]{1,0:T(8,128)(2,1)} async-done(((bf16[512,2048]{1,0:T(8,128)(2,1)}), bf16[4096,2048]{1,0:T(8,128)(2,1)}) %all-gather.6.cloned.1.call-update) | async-done | bytes 16777232 | tf_op jit(solution)/shard_map/all_gather | solution.py:123
  105.0 10.7 fusion.58
  138.8 8.6 all-to-all-done.2
  176.7 18.3 %all-to-all-done.1 = bf16[256,4,512]{2,0,1:T(8,128)(2,1)S(1)} async-done(((bf16[256,4,512]{2,0,1:T(8,128)(2,1)}), bf16[256,4,512]{2,0,1:T(8,128)(2,1)S(1)}, u32[]{:S(2)}, u32[]{:S(2)}) %all-to-all-start.1) | async-done | bytes 1048608 | tf_op jit(solution)/shard_map/all_to_all | solution.py:279
  211.8 28.6 %all_to_all.126 = bf16[4,256,512]{1,2,0:T(8,128)(2,1)} all-to-all(bf16[4,256,512]{1,2,0:T(8,128)(2,1)S(1)} %copy.302), channel_id=1, replica_groups=mesh['fsdp'=8,'sp'=4] {'sp'}, dimensions={0} | all-to-all | bytes 2097152 | tf_op jit(solution)/shard_map/all_to_all | solution.py:289
  286.4 106.6 %collective-permute-done.2 = bf16[1,256,768]{2,1,0:T(8,128)(2,1)S(1)} collective-permute-done((bf16[1,256,768]{2,1,0:T(8,128)(2,1)}, bf16[1,256,768]{2,1,0:T(8,128)(2,1)S(1)}, u32[]{:S(2)}, u32[]{:S(2)}) %collective-permute-start.2) | collective-permute-done | bytes 393248 | tf_op jit(solution)/shard_map/ppermute | solution.py:208
  398.6 13.2 %collective-permute-done.4 = bf16[1,256,768]{2,1,0:T(8,128)(2,1)S(1)} collective-permute-done((bf16[1,256,768]{2,1,0:T(8,128)(2,1)}, bf16[1,256,768]{2,1,0:T(8,128)(2,1)S(1)}, u32[]{:S(2)}, u32[]{:S(2)}) %collective-permute-start.4) | collective-permute-done | bytes 393248 | tf_op jit(solution)/shard_map/ppermute | solution.py:208
  414.2 18.0 %fusion.5 = f32[2048,1536]{0,1:T(8,128)S(1)} fusion(bf16[2048,2048]{1,0:T(8,128)(2,1)} %all-gather.12.cloned.1.call-done, bf16[768,2048]{1,0:T(8,128)(2,1)} %collective-permute-done.7, bf16[768,2048]{1,0:T(8,128)(2,1)} %get-tuple-element.138), kind=kOutput, calls=%fused_computation.33 | convolution fusion | flops 12897484800 | bytes 27262976 | tf_op jit(solution)/shard_map/dot_general | solution.py:127
  441.6 19.1 %select_convert_fusion.1 = (bf16[2048,768]{0,1:T(8,128)(2,1)}, bf16[2048,768]{0,1:T(8,128)(2,1)}, f32[2048,768]{0,1:T(8,128)}) fusion(pred[]{:T(512)S(6)} %eq.34, f32[2048,768]{0,1:T(8,128)} %get-tuple-element.131, f32[2048,1536]{0,1:T(8,128)} %copy-done.10, bf16[2048,2048]{1,0:T(8,128)(2,1)} %all-gather.10.cloned.1.call-done, bf16[2048,768]{1,0:T(8,128)(2,1)} %bitcast.244), kind=kOutput, calls=%fused_computation.16 | convolution fusion | flops 6464471040 | bytes 42991616 | tf_op jit(solution)/shard_map/dot_general | solution.py:298
  468.1 18.7 %convolution_convert_fusion.2 = bf16[2048,2048]{1,0:T(8,128)(2,1)} fusion(bf16[2048,768]{0,1:T(8,128)(2,1)S(1)} %select_convert_fusion, bf16[2048,768]{0,1:T(8,128)(2,1)} %get-tuple-element.132, bf16[768,2048]{1,0:T(8,128)(2,1)} %collective-permute-done.7, bf16[768,2048]{1,0:T(8,128)(2,1)S(1)} %copy-done.52), kind=kOutput, calls=%fused_computation.6 | convolution fusion | flops 12914262016 | bytes 20971520 | tf_op jit(solution)/shard_map/dot_general | solution.py:310
  486.9 10.0 convolution_convert_fusion.4
  503.9 9.6 convolution_convert_fusion.5
  513.6 8.1 convolution_convert_fusion.3
  521.6 13.3 %collective-permute-done.8 = bf16[384,2048]{1,0:T(8,128)(2,1)S(1)} collective-permute-done((bf16[384,2048]{1,0:T(8,128)(2,1)S(1)}, bf16[384,2048]{1,0:T(8,128)(2,1)S(1)}, u32[]{:S(2)}, u32[]{:S(2)}) %collective-permute-start.8) | collective-permute-done | bytes 1572896 | tf_op jit(solution)/shard_map/ppermute | solution.py:163
  538.0 20.2 %reduce-scatter.4.cloned.1.call-done = bf16[256,2048]{1,0:T(8,128)(2,1)} async-done(((bf16[2048,2048]{1,0:T(8,128)(2,1)}), bf16[256,2048]{1,0:T(8,128)(2,1)}) %reduce-scatter.4.cloned.1.call-update) | async-done | bytes 1048592 | tf_op jit(solution)/shard_map/reduce_scatter | solution.py:139
  663.8 25.7 %all-to-all-start.5 = ((bf16[4,256,1024]{1,2,0:T(8,128)(2,1)}), bf16[4,256,1024]{1,2,0:T(8,128)(2,1)}, u32[]{:S(2)}, u32[]{:S(2)}) async-start(bf16[4,256,1024]{1,2,0:T(8,128)(2,1)} %copy.320), calls=%async_computation.7 | async-start | bytes 4194304 | tf_op jit(solution)/shard_map/all_to_all | solution.py:346
  705.3 11.2 collective-permute-start.15
  716.5 9.1 convolution_convert_fusion.1
  728.1 10.9 all-to-all-done.5
  800.3 28.8 %collective-permute-done.16 = bf16[1024,768]{1,0:T(8,128)(2,1)} collective-permute-done((bf16[1024,768]{1,0:T(8,128)(2,1)}, bf16[1024,768]{1,0:T(8,128)(2,1)}, u32[]{:S(2)}, u32[]{:S(2)}) %collective-permute-start.16) | collective-permute-done | bytes 1572896 | tf_op jit(solution)/shard_map/ppermute | solution.py:163
  830.9 11.8 %fusion.23 = (f32[2048]{0:T(1024)S(1)}, f32[256]{0:T(256)S(1)}, f32[256,2048]{1,0:T(8,128)}) fusion(bf16[256,2048]{1,0:T(8,128)(2,1)S(1)} %copy-done.15, f32[256]{0:T(256)S(1)} %copy-done.83, f32[2048]{0:T(1024)S(1)} %copy-done.78, bf16[4096,2048]{1,0:T(8,128)(2,1)} %all-gather.6.cloned.1.call-done, bf16[256,1024]{0,1:T(8,128)(2,1)S(1)} %bitcast.255, ...), kind=kOutput, calls=%fused_computation.74 | convolution fusion | flops 4304926720 | bytes 22038528 | tf_op jit(solution)/shard_map/dot_general | solution.py:381
  859.8 8.7 convolution_convert_fusion.6
  868.7 20.7 %collective-permute-start.33 = (bf16[256,2048]{1,0:T(8,128)(2,1)S(1)}, bf16[256,2048]{1,0:T(8,128)(2,1)S(1)}, u32[]{:S(2)}, u32[]{:S(2)}) collective-permute-start(bf16[256,2048]{1,0:T(8,128)(2,1)S(1)} %get-tuple-element.159), channel_id=1, source_target_pairs={{0,1},{3,2},{4,5},{7,6},{8,9},{11,10},{12,13},{15,14},{16,17},{19,... | collective-permute-start | bytes 3145736 | tf_op jit(solution)/shard_map/ppermute | solution.py:163
  898.8 33.1 %collective-permute-done.36 = bf16[256,2048]{1,0:T(8,128)(2,1)S(1)} collective-permute-done((bf16[256,2048]{1,0:T(8,128)(2,1)S(1)}, bf16[256,2048]{1,0:T(8,128)(2,1)S(1)}, u32[]{:S(2)}, u32[]{:S(2)}) %collective-permute-start.36) | collective-permute-done | bytes 1048608 | tf_op jit(solution)/shard_map/ppermute | solution.py:163
  945.7 10.0 collective-permute-done.29
  960.9 14.6 %collective-permute-done.22 = bf16[1024,768]{1,0:T(8,128)(2,1)S(1)} collective-permute-done((bf16[1024,768]{1,0:T(8,128)(2,1)S(1)}, bf16[1024,768]{1,0:T(8,128)(2,1)S(1)}, u32[]{:S(2)}, u32[]{:S(2)}) %collective-permute-start.22) | collective-permute-done | bytes 1572896 | tf_op jit(solution)/shard_map/ppermute | solution.py:163
  992.1 17.2 %collective-permute-done.39 = bf16[384,2048]{1,0:T(8,128)(2,1)} collective-permute-done((bf16[384,2048]{1,0:T(8,128)(2,1)}, bf16[384,2048]{1,0:T(8,128)(2,1)}, u32[]{:S(2)}, u32[]{:S(2)}) %collective-permute-start.39) | collective-permute-done | bytes 1572896 | tf_op jit(solution)/shard_map/ppermute | solution.py:163
  1022.8 20.2 %collective-permute-done.41 = bf16[384,2048]{1,0:T(8,128)(2,1)} collective-permute-done((bf16[384,2048]{1,0:T(8,128)(2,1)}, bf16[384,2048]{1,0:T(8,128)(2,1)}, u32[]{:S(2)}, u32[]{:S(2)}) %collective-permute-start.41) | collective-permute-done | bytes 1572896 | tf_op jit(solution)/shard_map/ppermute | solution.py:163
  1048.3 9.2 maximum_convert_fusion
  1068.8 19.1 %collective-permute-done.31 = bf16[256,2048]{1,0:T(8,128)(2,1)} collective-permute-done((bf16[256,2048]{1,0:T(8,128)(2,1)}, bf16[256,2048]{1,0:T(8,128)(2,1)}, u32[]{:S(2)}, u32[]{:S(2)}) %collective-permute-start.31) | collective-permute-done | bytes 1048608 | tf_op jit(solution)/shard_map/ppermute | solution.py:163
  1089.4 16.8 %collective-permute-done.35 = bf16[256,2048]{1,0:T(8,128)(2,1)} collective-permute-done((bf16[256,2048]{1,0:T(8,128)(2,1)}, bf16[256,2048]{1,0:T(8,128)(2,1)}, u32[]{:S(2)}, u32[]{:S(2)}) %collective-permute-start.35) | collective-permute-done | bytes 1048608 | tf_op jit(solution)/shard_map/ppermute | solution.py:163
  1118.0 8.7 reshape.378
  (496 shorter events, 445.1 us)
Async XLA Ops:
  7.2 95.2 %all-gather.6.cloned.1.call-start = ((), (), s32[]{:S(2)}) async-start(), calls=%async_computation.11 | async-start | bytes 18874368 | tf_op jit(solution)/shard_map/all_gather | solution.py:123
  8.0 232.4 %all-gather.8.cloned.1.call-start = ((), (), s32[]{:S(2)}) async-start(), calls=%async_computation.12 | async-start | bytes 9437184 | tf_op jit(solution)/shard_map/all_gather | solution.py:123
  169.7 244.5 %all-gather.12.cloned.1.call-start = ((), (), s32[]{:S(2)}) async-start(), calls=%async_computation.14 | async-start | bytes 9437184 | tf_op jit(solution)/shard_map/all_gather | solution.py:123
  248.0 193.6 %all-gather.10.cloned.1.call-start = ((), (), s32[]{:S(2)}) async-start(), calls=%async_computation.13 | async-start | bytes 9437184 | tf_op jit(solution)/shard_map/all_gather | solution.py:123
  248.6 309.7 %reduce-scatter.4.cloned.1.call-start = ((), (), s32[]{:S(2)}) async-start(), calls=%async_computation.15 | async-start | bytes 9437184 | tf_op jit(solution)/shard_map/reduce_scatter | solution.py:139
  255.5 158.7 %collective-permute-start.7 = (bf16[768,2048]{1,0:T(8,128)(2,1)}, bf16[768,2048]{1,0:T(8,128)(2,1)}, u32[]{:S(2)}, u32[]{:S(2)}) collective-permute-start(bf16[768,2048]{1,0:T(8,128)(2,1)} %get-tuple-element.139), channel_id=1, source_target_pairs={{0,16},{4,20},{8,24},{12,28},{16,0},{20,4},{24,8},{28,12},{1,17},{... | collective-permute-start | bytes 9437192 | tf_op jit(solution)/shard_map/ppermute | solution.py:262
  271.7 121.4 %collective-permute-start.2 = (bf16[1,256,768]{2,1,0:T(8,128)(2,1)}, bf16[1,256,768]{2,1,0:T(8,128)(2,1)S(1)}, u32[]{:S(2)}, u32[]{:S(2)}) collective-permute-start(bf16[1,256,768]{2,1,0:T(8,128)(2,1)} %get-tuple-element.152), channel_id=1, source_target_pairs={{0,12},{4,16},{8,20},{12,24},{16,28},{20,0},{24,4},{28,8},{1,13},{... | collective-permute-start | bytes 1179656 | tf_op jit(solution)/shard_map/ppermute | solution.py:208
  274.2 123.7 %collective-permute-start.3 = (bf16[1,256,768]{2,1,0:T(8,128)(2,1)}, bf16[1,256,768]{2,1,0:T(8,128)(2,1)S(1)}, u32[]{:S(2)}, u32[]{:S(2)}) collective-permute-start(bf16[1,256,768]{2,1,0:T(8,128)(2,1)} %get-tuple-element.151), channel_id=1, source_target_pairs={{0,16},{4,20},{8,24},{12,28},{16,0},{20,4},{24,8},{28,12},{1,17},{... | collective-permute-start | bytes 1179656 | tf_op jit(solution)/shard_map/ppermute | solution.py:208
  282.6 129.3 %collective-permute-start.4 = (bf16[1,256,768]{2,1,0:T(8,128)(2,1)}, bf16[1,256,768]{2,1,0:T(8,128)(2,1)S(1)}, u32[]{:S(2)}, u32[]{:S(2)}) collective-permute-start(bf16[1,256,768]{2,1,0:T(8,128)(2,1)} %get-tuple-element.150), channel_id=1, source_target_pairs={{0,20},{4,24},{8,28},{12,0},{16,4},{20,8},{24,12},{28,16},{1,21},{... | collective-permute-start | bytes 1179656 | tf_op jit(solution)/shard_map/ppermute | solution.py:208
  284.4 128.3 %collective-permute-start.5 = (bf16[1,256,768]{2,1,0:T(8,128)(2,1)}, bf16[1,256,768]{2,1,0:T(8,128)(2,1)S(1)}, u32[]{:S(2)}, u32[]{:S(2)}) collective-permute-start(bf16[1,256,768]{2,1,0:T(8,128)(2,1)} %get-tuple-element.149), channel_id=1, source_target_pairs={{0,24},{4,28},{8,0},{12,4},{16,8},{20,12},{24,16},{28,20},{1,25},{... | collective-permute-start | bytes 1179656 | tf_op jit(solution)/shard_map/ppermute | solution.py:208
  486.9 362.5 %reduce-scatter.8.cloned.1.call-start = ((), (), s32[]{:S(2)}) async-start(), calls=%async_computation.17 | async-start | bytes 9437184 | tf_op jit(solution)/shard_map/reduce_scatter | solution.py:139
  501.3 67.5 %collective-permute-start.10 = (bf16[384,2048]{1,0:T(8,128)(2,1)}, bf16[384,2048]{1,0:T(8,128)(2,1)}, u32[]{:S(2)}, u32[]{:S(2)}) collective-permute-start(bf16[384,2048]{1,0:T(8,128)(2,1)} %get-tuple-element.146), channel_id=1, source_target_pairs={{0,1},{3,2},{4,5},{7,6},{8,9},{11,10},{12,13},{15,14},{16,17},{19,... | collective-permute-start | bytes 4718600 | tf_op jit(solution)/shard_map/ppermute | solution.py:163
  574.5 285.2 %all-gather.14.cloned.1.call-start = ((), (), s32[]{:S(2)}) async-start(), calls=%async_computation.18 | async-start | bytes 9437184 | tf_op jit(solution)/shard_map/all_gather | solution.py:123
  600.1 59.7 %collective-permute-start.11 = (bf16[384,2048]{1,0:T(8,128)(2,1)}, bf16[384,2048]{1,0:T(8,128)(2,1)}, u32[]{:S(2)}, u32[]{:S(2)}) collective-permute-start(bf16[384,2048]{1,0:T(8,128)(2,1)} %get-tuple-element.142), channel_id=1, source_target_pairs={{1,2},{2,1},{5,6},{6,5},{9,10},{10,9},{13,14},{14,13},{17,18},{18,... | collective-permute-start | bytes 4718600 | tf_op jit(solution)/shard_map/ppermute | solution.py:163
  602.0 57.9 %collective-permute-start.12 = (bf16[1024,768]{1,0:T(8,128)(2,1)}, bf16[1024,768]{1,0:T(8,128)(2,1)}, u32[]{:S(2)}, u32[]{:S(2)}) collective-permute-start(bf16[1024,768]{1,0:T(8,128)(2,1)} %get-tuple-element.89), channel_id=1, source_target_pairs={{0,1},{3,2},{4,5},{7,6},{8,9},{11,10},{12,13},{15,14},{16,17},{19,... | collective-permute-start | bytes 4718600 | tf_op jit(solution)/shard_map/ppermute | solution.py:163
  609.1 116.5 %collective-permute-start.13 = (bf16[1024,768]{1,0:T(8,128)(2,1)}, bf16[1024,768]{1,0:T(8,128)(2,1)}, u32[]{:S(2)}, u32[]{:S(2)}) collective-permute-start(bf16[1024,768]{1,0:T(8,128)(2,1)} %get-tuple-element.93), channel_id=1, source_target_pairs={{0,1},{3,2},{4,5},{7,6},{8,9},{11,10},{12,13},{15,14},{16,17},{19,... | collective-permute-start | bytes 4718600 | tf_op jit(solution)/shard_map/ppermute | solution.py:163
  663.8 75.2 %all-to-all-start.5 = ((bf16[4,256,1024]{1,2,0:T(8,128)(2,1)}), bf16[4,256,1024]{1,2,0:T(8,128)(2,1)}, u32[]{:S(2)}, u32[]{:S(2)}) async-start(bf16[4,256,1024]{1,2,0:T(8,128)(2,1)} %copy.320), calls=%async_computation.7 | async-start | bytes 4194304 | tf_op jit(solution)/shard_map/all_to_all | solution.py:346
  689.5 294.3 %reduce-scatter.6.cloned.1.call-start = ((), (), s32[]{:S(2)}) async-start(), calls=%async_computation.16 | async-start | bytes 9437184 | tf_op jit(solution)/shard_map/reduce_scatter | solution.py:139
  693.4 156.0 %collective-permute-start.21 = (bf16[384,2048]{1,0:T(8,128)(2,1)}, bf16[384,2048]{1,0:T(8,128)(2,1)}, u32[]{:S(2)}, u32[]{:S(2)}) collective-permute-start(bf16[384,2048]{1,0:T(8,128)(2,1)} %add_convert_fusion.4), channel_id=1, source_target_pairs={{1,0},{2,3},{5,4},{6,7},{9,8},{10,11},{13,12},{14,15},{17,16},{18,... | collective-permute-start | bytes 4718600 | tf_op jit(solution)/shard_map/ppermute | solution.py:163
  698.5 150.8 %collective-permute-start.20 = (bf16[384,2048]{1,0:T(8,128)(2,1)}, bf16[384,2048]{1,0:T(8,128)(2,1)}, u32[]{:S(2)}, u32[]{:S(2)}) collective-permute-start(bf16[384,2048]{1,0:T(8,128)(2,1)} %add_convert_fusion.5), channel_id=1, source_target_pairs={{1,0},{2,3},{5,4},{6,7},{9,8},{10,11},{13,12},{14,15},{17,16},{18,... | collective-permute-start | bytes 4718600 | tf_op jit(solution)/shard_map/ppermute | solution.py:163
  725.7 123.7 %collective-permute-start.19 = (bf16[384,2048]{1,0:T(8,128)(2,1)}, bf16[384,2048]{1,0:T(8,128)(2,1)}, u32[]{:S(2)}, u32[]{:S(2)}) collective-permute-start(bf16[384,2048]{1,0:T(8,128)(2,1)} %get-tuple-element.101), channel_id=1, source_target_pairs={{0,1},{3,2},{4,5},{7,6},{8,9},{11,10},{12,13},{15,14},{16,17},{19,... | collective-permute-start | bytes 4718600 | tf_op jit(solution)/shard_map/ppermute | solution.py:163
  762.2 87.2 %collective-permute-start.18 = (bf16[384,2048]{1,0:T(8,128)(2,1)}, bf16[384,2048]{1,0:T(8,128)(2,1)}, u32[]{:S(2)}, u32[]{:S(2)}) collective-permute-start(bf16[384,2048]{1,0:T(8,128)(2,1)} %add_convert_fusion.6), channel_id=1, source_target_pairs={{1,2},{2,1},{5,6},{6,5},{9,10},{10,9},{13,14},{14,13},{17,18},{18,... | collective-permute-start | bytes 4718600 | tf_op jit(solution)/shard_map/ppermute | solution.py:163
  853.2 87.2 %collective-permute-start.40 = (bf16[384,2048]{1,0:T(8,128)(2,1)}, bf16[384,2048]{1,0:T(8,128)(2,1)}, u32[]{:S(2)}, u32[]{:S(2)}) collective-permute-start(bf16[384,2048]{1,0:T(8,128)(2,1)} %add_convert_fusion.1), channel_id=1, source_target_pairs={{1,2},{2,1},{5,6},{6,5},{9,10},{10,9},{13,14},{14,13},{17,18},{18,... | collective-permute-start | bytes 4718600 | tf_op jit(solution)/shard_map/ppermute | solution.py:163
  858.1 81.0 %collective-permute-start.32 = (bf16[384,2048]{1,0:T(8,128)(2,1)}, bf16[384,2048]{1,0:T(8,128)(2,1)}, u32[]{:S(2)}, u32[]{:S(2)}) collective-permute-start(bf16[384,2048]{1,0:T(8,128)(2,1)} %broadcast_select_fusion.4), channel_id=1, source_target_pairs={{0,16},{4,20},{8,24},{12,28},{16,0},{20,4},{24,8},{28,12},{1,17},{... | collective-permute-start | bytes 4718600 | tf_op jit(solution)/shard_map/ppermute | solution.py:380
  868.7 67.7 %collective-permute-start.33 = (bf16[256,2048]{1,0:T(8,128)(2,1)S(1)}, bf16[256,2048]{1,0:T(8,128)(2,1)S(1)}, u32[]{:S(2)}, u32[]{:S(2)}) collective-permute-start(bf16[256,2048]{1,0:T(8,128)(2,1)S(1)} %get-tuple-element.159), channel_id=1, source_target_pairs={{0,1},{3,2},{4,5},{7,6},{8,9},{11,10},{12,13},{15,14},{16,17},{19,... | collective-permute-start | bytes 3145736 | tf_op jit(solution)/shard_map/ppermute | solution.py:163
  892.3 64.7 %collective-permute-start.28 = (bf16[384,2048]{1,0:T(8,128)(2,1)S(1)}, bf16[384,2048]{1,0:T(8,128)(2,1)}, u32[]{:S(2)}, u32[]{:S(2)}) collective-permute-start(bf16[384,2048]{1,0:T(8,128)(2,1)S(1)} %broadcast_select_fusion.5), channel_id=1, source_target_pairs={{0,16},{4,20},{8,24},{12,28},{16,0},{20,4},{24,8},{28,12},{1,17},{... | collective-permute-start | bytes 4718600 | tf_op jit(solution)/shard_map/ppermute | solution.py:380
  939.0 70.3 %collective-permute-start.39 = (bf16[384,2048]{1,0:T(8,128)(2,1)}, bf16[384,2048]{1,0:T(8,128)(2,1)}, u32[]{:S(2)}, u32[]{:S(2)}) collective-permute-start(bf16[384,2048]{1,0:T(8,128)(2,1)} %add_convert_fusion.2), channel_id=1, source_target_pairs={{1,0},{2,3},{5,4},{6,7},{9,8},{10,11},{13,12},{14,15},{17,16},{18,... | collective-permute-start | bytes 4718600 | tf_op jit(solution)/shard_map/ppermute | solution.py:163
  940.3 70.6 %collective-permute-start.37 = (bf16[256,2048]{1,0:T(8,128)(2,1)}, bf16[256,2048]{1,0:T(8,128)(2,1)}, u32[]{:S(2)}, u32[]{:S(2)}) collective-permute-start(bf16[256,2048]{1,0:T(8,128)(2,1)} %add_convert_fusion.13), channel_id=1, source_target_pairs={{1,2},{2,1},{5,6},{6,5},{9,10},{10,9},{13,14},{14,13},{17,18},{18,... | collective-permute-start | bytes 3145736 | tf_op jit(solution)/shard_map/ppermute | solution.py:163
  955.7 87.4 %collective-permute-start.41 = (bf16[384,2048]{1,0:T(8,128)(2,1)}, bf16[384,2048]{1,0:T(8,128)(2,1)}, u32[]{:S(2)}, u32[]{:S(2)}) collective-permute-start(bf16[384,2048]{1,0:T(8,128)(2,1)} %add_convert_fusion), channel_id=1, source_target_pairs={{1,0},{2,3},{5,4},{6,7},{9,8},{10,11},{13,12},{14,15},{17,16},{18,... | collective-permute-start | bytes 4718600 | tf_op jit(solution)/shard_map/ppermute | solution.py:163
  979.3 69.0 %all-to-all-start.7 = ((bf16[8,256,768]{2,1,0:T(8,128)(2,1)}), bf16[8,256,768]{2,1,0:T(8,128)(2,1)}, u32[]{:S(2)}, u32[]{:S(2)}) async-start(bf16[8,256,768]{2,1,0:T(8,128)(2,1)} %bitcast.210), calls=%async_computation.10 | async-start | bytes 6291456 | tf_op jit(solution)/shard_map/all_to_all | solution.py:402
  1017.3 70.7 %collective-permute-start.31 = (bf16[256,2048]{1,0:T(8,128)(2,1)}, bf16[256,2048]{1,0:T(8,128)(2,1)}, u32[]{:S(2)}, u32[]{:S(2)}) collective-permute-start(bf16[256,2048]{1,0:T(8,128)(2,1)} %add_convert_fusion.16), channel_id=1, source_target_pairs={{1,0},{2,3},{5,4},{6,7},{9,8},{10,11},{13,12},{14,15},{17,16},{18,... | collective-permute-start | bytes 3145736 | tf_op jit(solution)/shard_map/ppermute | solution.py:163
  1021.5 84.7 %collective-permute-start.35 = (bf16[256,2048]{1,0:T(8,128)(2,1)}, bf16[256,2048]{1,0:T(8,128)(2,1)}, u32[]{:S(2)}, u32[]{:S(2)}) collective-permute-start(bf16[256,2048]{1,0:T(8,128)(2,1)} %add_convert_fusion.14), channel_id=1, source_target_pairs={{1,0},{2,3},{5,4},{6,7},{9,8},{10,11},{13,12},{14,15},{17,16},{18,... | collective-permute-start | bytes 3145736 | tf_op jit(solution)/shard_map/ppermute | solution.py:163
  (127 other events, 2780.0 us)
Sparse Core Ops, SparseCore 0:
  9.9 92.4 all-gather.5
  104.3 54.2 all-gather.7
  248.1 102.2 all-gather.11
  352.1 75.0 all-gather.9
  487.0 71.1 reduce-scatter.3
  574.7 72.4 reduce-scatter.7
  649.0 54.2 all-gather.13
  725.8 69.6 reduce-scatter.5

commit v6 on v5

--- a/solution.py
+++ b/solution.py
@@ -197,16 +197,29 @@
     return tied[0]
 
 
-def turn(blocks, ways):
+def column_blocks(array, ways):
     me = lax.axis_index("fsdp")
-    result = lax.dynamic_update_slice_in_dim(
-        jnp.zeros_like(blocks), lax.dynamic_slice_in_dim(blocks, me, 1, 0), me, 0
-    )
+    half = ways // 2
+    size = array.shape[1] // ways
+    blocks = []
+    for shift in range(ways):
+        device = (me + shift) % ways
+        block = 2 * (device % half) + device // half
+        blocks.append(lax.dynamic_slice_in_dim(array, block * size, size, 1))
+    return blocks
+
+
+def turn(blocks):
+    me = lax.axis_index("fsdp")
+    ways = len(blocks)
+    size = blocks[0].shape[0]
+    result = jnp.zeros((ways * size, blocks[0].shape[1]), blocks[0].dtype)
+    result = lax.dynamic_update_slice_in_dim(result, blocks[0], me * size, 0)
     for shift in range(1, ways):
-        block = lax.dynamic_slice_in_dim(blocks, (me + shift) % ways, 1, 0)
         pairs = [(f, (f + shift) % ways) for f in range(ways)]
-        arrived = lax.ppermute(block, "fsdp", pairs)
-        result = lax.dynamic_update_slice_in_dim(result, arrived, (me - shift) % ways, 0)
+        arrived = lax.ppermute(blocks[shift], "fsdp", pairs)
+        source = (me - shift) % ways
+        result = lax.dynamic_update_slice_in_dim(result, arrived, source * size, 0)
     return result
 
 
@@ -252,17 +265,17 @@
     swap = [(f, (f + pairs_of) % ways) for f in range(ways)]
 
     qkv_full = gather_rows(qkv_weight)
-    qkv_full, gate_up_late, down_late, out_late, cotangent_late = lax.optimization_barrier(
-        (qkv_full, gate_up_weight, down_weight, out_weight, cotangent)
+    kept = lax.dynamic_slice_in_dim(gate_up_weight, side * units, units, 0)
+    sent = lax.dynamic_slice_in_dim(gate_up_weight, (1 - side) * units, units, 0)
+    down_blocks = column_blocks(down_weight, ways)
+    qkv_full, sent, down_blocks, out_late, cotangent_late = lax.optimization_barrier(
+        (qkv_full, sent, down_blocks, out_weight, cotangent)
     )
     out_full = gather_rows(out_late)
     cotangent_all = gather_rows(cotangent_late)
-    kept = lax.dynamic_slice_in_dim(gate_up_late, side * units, units, 0)
-    sent = lax.dynamic_slice_in_dim(gate_up_late, (1 - side) * units, units, 0)
     swapped = lax.ppermute(sent, "fsdp", swap)
     gate_up_own = jnp.concatenate([kept, swapped], 0)
-    down_split = down_late.reshape(-1, pairs_of, 2, units).transpose(2, 1, 0, 3)
-    down_own = turn(down_split.reshape(ways, -1, units), ways).reshape(width, units)
+    down_own = turn(down_blocks)
     hidden = hidden_in.astype(f32)
     normed1, inverse1 = rms_forward(hidden, attn_gain)
     normed1_low = normed1.astype(low)
@@ -396,7 +409,7 @@
     q1.send()
     meet((), [out_chain])
     meet((), [k1])
-    swapped_back = [meet(swapped_back[0], [q0]), meet(swapped_back[1], [q1])]
+    swapped_back = [meet(swapped_back[0], [q0, d0]), meet(swapped_back[1], [q1])]
     grad_swapped = jnp.concatenate(swapped_back, 0)
     grad_down_sum = jnp.concatenate([d0.finish(), d1.finish()], 0)
     down_back = lax.all_to_all(
@@ -406,14 +419,12 @@
         concat_axis=0,
         tiled=True,
     )
-    down_back, terms = meet((down_back, terms), [])
+    columns = [
+        down_back[(b % 2) * pairs_of + b // 2] for b in range(ways)
+    ]
+    grad_down = jnp.concatenate(columns, 1).astype(f32)
+    grad_down, terms = meet((grad_down, terms), [])
     sums = sum_all(terms, (("fsdp", ways), ("sp", line)))
-    grad_down = (
-        down_back.reshape(2, pairs_of, -1, units)
-        .transpose(2, 1, 0, 3)
-        .reshape(down_weight.shape)
-        .astype(f32)
-    )
     grad_kept = jnp.concatenate([k0.finish(), k1.finish()], 0)
     grad_gate_up = jnp.concatenate(
         [

time: 1140 us -> 1100 us (0.965)
  waiting for transfers between devices: 489 us -> 448 us
    ppermute x27, waiting for transfers between devices: 193 us -> 156 us  [send(): self.flying = lax.ppermute(self.value, 'sp', self.hops[self.at][0])]
    convert_element_type x2 -> x0, local copies, waits for them, and re-layouts: 16.4 us -> none  [layer(): grad_down = down_back.reshape(2, pairs_of, -1, units).transpose(2, 1, 0,...]
    unnamed x212 -> x221, local copies, waits for them, and re-layouts: 32.4 us -> 35.4 us
  transfers between devices with their start and end apart: 57 -> 57, of which waited for: 23 -> 26; matrix products, arithmetic and copies ran while one was open for 33% -> 34% of each run, Pallas kernels for 0% -> 0%
where the time goes in v6:
time: 1100 us; the launch traced here: 1090 us
  waiting for transfers between devices  448 us (41%)
  matrix products  172 us (16%)
  other arithmetic  156 us (14%)
  starting transfers between devices  149 us (14%)
  local copies, waits for them, and re-layouts  122 us (11%)
  blocking collectives  28.6 us (3%)
  between operations  16.6 us (2%)
    ppermute x27, waiting for transfers between devices, send(): self.flying = lax.ppermute(self.value, 'sp', self.hops[self.at][0])  156 us
    ppermute x7, waiting for transfers between devices, turn(): arrived = lax.ppermute(blocks[shift], 'fsdp', pairs)  141 us
    ppermute x27, starting transfers between devices, send(): self.flying = lax.ppermute(self.value, 'sp', self.hops[self.at][0])  88.2 us
    all_gather x5, waiting for transfers between devices, gather_rows(): return lax.all_gather(array, 'fsdp', axis=0, tiled=True)  85.8 us
    convert_element_type x16, other arithmetic, take(): self.value = total.astype(jnp.bfloat16)  54.2 us
    dot_general x4, matrix products, product_nt(): lax.dot_general(inputs, weight, (((1,), (1,)), ((), ())), preferred_eleme...  45.7 us
    dot_general x5, matrix products, product_tn(): lax.dot_general(left, right, (((0,), (0,)), ((), ())), preferred_element_...  42.1 us
    unnamed x221, local copies, waits for them, and re-layouts  35.4 us
  transfers between devices with their start and end apart: 57, of which 26 were waited for; matrix products, arithmetic and copies ran while one was open for 34% of the time, Pallas kernels for 0%

profile of v6, /device:TPU:0, one launch (start us, length us, event | category | flops | bytes accessed | tf_op | source)
XLA Modules:
  0.0 1092.7 jit_solution(11251423181948970953)
XLA Ops:
  16.5 85.8 %all-gather.6.cloned.1.call-done = bf16[4096,2048]{1,0:T(8,128)(2,1)} async-done(((bf16[512,2048]{1,0:T(8,128)(2,1)}), bf16[4096,2048]{1,0:T(8,128)(2,1)}) %all-gather.6.cloned.1.call-update) | async-done | bytes 16777232 | tf_op jit(solution)/shard_map/all_gather | solution.py:123
  104.4 10.5 fusion.66
  182.5 8.1 all-to-all-done.1
  209.3 28.6 %all_to_all.126 = bf16[4,256,512]{1,2,0:T(8,128)(2,1)} all-to-all(bf16[4,256,512]{1,2,0:T(8,128)(2,1)S(1)} %copy.282), channel_id=1, replica_groups=mesh['fsdp'=8,'sp'=4] {'sp'}, dimensions={0} | all-to-all | bytes 2097152 | tf_op jit(solution)/shard_map/all_to_all | solution.py:302
  253.8 9.0 collective-permute-done
  267.7 115.1 %collective-permute-done.2 = bf16[256,768]{1,0:T(8,128)(2,1)S(1)} collective-permute-done((bf16[256,768]{1,0:T(8,128)(2,1)}, bf16[256,768]{1,0:T(8,128)(2,1)S(1)}, u32[]{:S(2)}, u32[]{:S(2)}) %collective-permute-start.2) | collective-permute-done | bytes 393248 | tf_op jit(solution)/shard_map/ppermute | solution.py:220
  388.5 12.4 %collective-permute-done.4 = bf16[256,768]{1,0:T(8,128)(2,1)S(1)} collective-permute-done((bf16[256,768]{1,0:T(8,128)(2,1)S(1)}, bf16[256,768]{1,0:T(8,128)(2,1)S(1)}, u32[]{:S(2)}, u32[]{:S(2)}) %collective-permute-start.4) | collective-permute-done | bytes 393248 | tf_op jit(solution)/shard_map/ppermute | solution.py:220
  403.2 17.9 %fusion.5 = f32[2048,1536]{0,1:T(8,128)S(1)} fusion(bf16[2048,2048]{1,0:T(8,128)(2,1)} %all-gather.12.cloned.1.call-done, bf16[768,2048]{1,0:T(8,128)(2,1)} %collective-permute-done.7, bf16[768,2048]{1,0:T(8,128)(2,1)} %get-tuple-element.154), kind=kOutput, calls=%fused_computation.32 | convolution fusion | flops 12897484800 | bytes 27262976 | tf_op jit(solution)/shard_map/dot_general | solution.py:127
  430.6 19.1 %select_convert_fusion.1 = (bf16[2048,768]{0,1:T(8,128)(2,1)}, bf16[2048,768]{0,1:T(8,128)(2,1)}, f32[2048,768]{0,1:T(8,128)}) fusion(pred[]{:T(512)S(6)} %eq.43, f32[2048,768]{0,1:T(8,128)} %get-tuple-element.147, f32[2048,1536]{0,1:T(8,128)} %copy-done.10, bf16[2048,2048]{1,0:T(8,128)(2,1)} %all-gather.10.cloned.1.call-done, ...), kind=kOutput, calls=%fused_computation.15 | convolution fusion | flops 6464471040 | bytes 42991616 | tf_op jit(solution)/shard_map/dot_general | solution.py:311
  457.1 18.7 %convolution_convert_fusion.2 = bf16[2048,2048]{1,0:T(8,128)(2,1)} fusion(bf16[2048,768]{0,1:T(8,128)(2,1)S(1)} %select_convert_fusion, bf16[2048,768]{0,1:T(8,128)(2,1)} %get-tuple-element.148, bf16[768,2048]{1,0:T(8,128)(2,1)} %collective-permute-done.7, bf16[768,2048]{1,0:T(8,128)(2,1)S(1)} %copy-done.49), kind=kOutput, calls=%fused_computation.6 | convolution fusion | flops 12914262016 | bytes 20971520 | tf_op jit(solution)/shard_map/dot_general | solution.py:323
  475.9 10.0 convolution_convert_fusion.4
  492.9 9.6 convolution_convert_fusion.5
  502.6 8.1 convolution_convert_fusion.3
  510.6 13.5 %collective-permute-done.8 = bf16[384,2048]{1,0:T(8,128)(2,1)S(1)} collective-permute-done((bf16[384,2048]{1,0:T(8,128)(2,1)S(1)}, bf16[384,2048]{1,0:T(8,128)(2,1)S(1)}, u32[]{:S(2)}, u32[]{:S(2)}) %collective-permute-start.8) | collective-permute-done | bytes 1572896 | tf_op jit(solution)/shard_map/ppermute | solution.py:163
  527.2 19.4 %reduce-scatter.4.cloned.1.call-done = bf16[256,2048]{1,0:T(8,128)(2,1)} async-done(((bf16[2048,2048]{1,0:T(8,128)(2,1)}), bf16[256,2048]{1,0:T(8,128)(2,1)}) %reduce-scatter.4.cloned.1.call-update) | async-done | bytes 1048592 | tf_op jit(solution)/shard_map/reduce_scatter | solution.py:139
  549.9 8.1 collective-permute-done.10
  652.4 26.1 %all-to-all-start.5 = ((bf16[4,256,1024]{1,2,0:T(8,128)(2,1)}), bf16[4,256,1024]{1,2,0:T(8,128)(2,1)}, u32[]{:S(2)}, u32[]{:S(2)}) async-start(bf16[4,256,1024]{1,2,0:T(8,128)(2,1)} %copy.298), calls=%async_computation.7 | async-start | bytes 4194304 | tf_op jit(solution)/shard_map/all_to_all | solution.py:359
  694.4 11.0 %collective-permute-start.15 = (bf16[384,2048]{1,0:T(8,128)(2,1)}, bf16[384,2048]{1,0:T(8,128)(2,1)}, u32[]{:S(2)}, u32[]{:S(2)}) collective-permute-start(bf16[384,2048]{1,0:T(8,128)(2,1)} %get-tuple-element.111), channel_id=1, source_target_pairs={{0,1},{3,2},{4,5},{7,6},{8,9},{11,10},{12,13},{15,14},{16,17},{19,... | collective-permute-start | bytes 4718600 | tf_op jit(solution)/shard_map/ppermute | solution.py:163
  705.5 10.9 convolution_convert_fusion.1
  718.9 9.3 all-to-all-done.5
  786.1 12.5 %fusion.23 = (f32[2048]{0:T(1024)S(1)}, f32[256]{0:T(256)S(1)}, f32[256,2048]{1,0:T(8,128)}) fusion(bf16[256,2048]{1,0:T(8,128)(2,1)S(1)} %copy-done.14, f32[256]{0:T(256)S(1)} %copy-done.84, f32[2048]{0:T(1024)S(1)} %copy-done.82, bf16[4096,2048]{1,0:T(8,128)(2,1)} %all-gather.6.cloned.1.call-done, bf16[256,1024]{0,1:T(8,128)(2,1)} %bitcast.269, ...), kind=kOutput, calls=%fused_computation.73 | convolution fusion | flops 4304926720 | bytes 22038528 | tf_op jit(solution)/shard_map/dot_general | solution.py:394
  802.0 8.5 all-to-all-done.6
  825.0 8.7 convolution_convert_fusion.6
  833.7 26.1 %collective-permute-start.36 = (bf16[256,2048]{1,0:T(8,128)(2,1)S(1)}, bf16[256,2048]{1,0:T(8,128)(2,1)S(1)}, u32[]{:S(2)}, u32[]{:S(2)}) collective-permute-start(bf16[256,2048]{1,0:T(8,128)(2,1)S(1)} %copy-done.67), channel_id=1, source_target_pairs={{0,1},{3,2},{4,5},{7,6},{8,9},{11,10},{12,13},{15,14},{16,17},{19,... | collective-permute-start | bytes 3145736 | tf_op jit(solution)/shard_map/ppermute | solution.py:163
  865.3 18.0 %collective-permute-done.36 = bf16[256,2048]{1,0:T(8,128)(2,1)S(1)} collective-permute-done((bf16[256,2048]{1,0:T(8,128)(2,1)S(1)}, bf16[256,2048]{1,0:T(8,128)(2,1)S(1)}, u32[]{:S(2)}, u32[]{:S(2)}) %collective-permute-start.36) | collective-permute-done | bytes 1048608 | tf_op jit(solution)/shard_map/ppermute | solution.py:163
  887.1 16.2 %collective-permute-done.33 = bf16[256,2048]{1,0:T(8,128)(2,1)S(1)} collective-permute-done((bf16[256,2048]{1,0:T(8,128)(2,1)S(1)}, bf16[256,2048]{1,0:T(8,128)(2,1)S(1)}, u32[]{:S(2)}, u32[]{:S(2)}) %collective-permute-start.33) | collective-permute-done | bytes 1048608 | tf_op jit(solution)/shard_map/ppermute | solution.py:163
  917.2 10.7 collective-permute-done.22
  934.6 12.3 %collective-permute-done.24 = bf16[1024,768]{1,0:T(8,128)(2,1)S(1)} collective-permute-done((bf16[1024,768]{1,0:T(8,128)(2,1)S(1)}, bf16[1024,768]{1,0:T(8,128)(2,1)S(1)}, u32[]{:S(2)}, u32[]{:S(2)}) %collective-permute-start.24) | collective-permute-done | bytes 1572896 | tf_op jit(solution)/shard_map/ppermute | solution.py:163
  962.2 18.5 %collective-permute-done.39 = bf16[384,2048]{1,0:T(8,128)(2,1)} collective-permute-done((bf16[384,2048]{1,0:T(8,128)(2,1)}, bf16[384,2048]{1,0:T(8,128)(2,1)}, u32[]{:S(2)}, u32[]{:S(2)}) %collective-permute-start.39) | collective-permute-done | bytes 1572896 | tf_op jit(solution)/shard_map/ppermute | solution.py:163
  995.2 19.2 %collective-permute-done.41 = bf16[384,2048]{1,0:T(8,128)(2,1)} collective-permute-done((bf16[384,2048]{1,0:T(8,128)(2,1)}, bf16[384,2048]{1,0:T(8,128)(2,1)}, u32[]{:S(2)}, u32[]{:S(2)}) %collective-permute-start.41) | collective-permute-done | bytes 1572896 | tf_op jit(solution)/shard_map/ppermute | solution.py:163
  1041.7 17.7 %collective-permute-done.31 = bf16[256,2048]{1,0:T(8,128)(2,1)} collective-permute-done((bf16[256,2048]{1,0:T(8,128)(2,1)}, bf16[256,2048]{1,0:T(8,128)(2,1)}, u32[]{:S(2)}, u32[]{:S(2)}) %collective-permute-start.31) | collective-permute-done | bytes 1048608 | tf_op jit(solution)/shard_map/ppermute | solution.py:163
  1060.8 17.6 %collective-permute-done.35 = bf16[256,2048]{1,0:T(8,128)(2,1)} collective-permute-done((bf16[256,2048]{1,0:T(8,128)(2,1)}, bf16[256,2048]{1,0:T(8,128)(2,1)}, u32[]{:S(2)}, u32[]{:S(2)}) %collective-permute-start.35) | collective-permute-done | bytes 1048608 | tf_op jit(solution)/shard_map/ppermute | solution.py:163
  (504 shorter events, 438.8 us)
Async XLA Ops:
  7.2 95.2 %all-gather.6.cloned.1.call-start = ((), (), s32[]{:S(2)}) async-start(), calls=%async_computation.11 | async-start | bytes 18874368 | tf_op jit(solution)/shard_map/all_gather | solution.py:123
  7.9 230.0 %all-gather.8.cloned.1.call-start = ((), (), s32[]{:S(2)}) async-start(), calls=%async_computation.12 | async-start | bytes 9437184 | tf_op jit(solution)/shard_map/all_gather | solution.py:123
  165.3 237.9 %all-gather.12.cloned.1.call-start = ((), (), s32[]{:S(2)}) async-start(), calls=%async_computation.14 | async-start | bytes 9437184 | tf_op jit(solution)/shard_map/all_gather | solution.py:123
  245.5 185.1 %all-gather.10.cloned.1.call-start = ((), (), s32[]{:S(2)}) async-start(), calls=%async_computation.13 | async-start | bytes 9437184 | tf_op jit(solution)/shard_map/all_gather | solution.py:123
  246.1 300.5 %reduce-scatter.4.cloned.1.call-start = ((), (), s32[]{:S(2)}) async-start(), calls=%async_computation.15 | async-start | bytes 9437184 | tf_op jit(solution)/shard_map/reduce_scatter | solution.py:139
  246.2 157.1 %collective-permute-start.7 = (bf16[768,2048]{1,0:T(8,128)(2,1)}, bf16[768,2048]{1,0:T(8,128)(2,1)}, u32[]{:S(2)}, u32[]{:S(2)}) collective-permute-start(bf16[768,2048]{1,0:T(8,128)(2,1)} %get-tuple-element.98), channel_id=1, source_target_pairs={{0,16},{4,20},{8,24},{12,28},{16,0},{20,4},{24,8},{28,12},{1,17},{... | collective-permute-start | bytes 9437192 | tf_op jit(solution)/shard_map/ppermute | solution.py:276
  248.3 134.6 %collective-permute-start.2 = (bf16[256,768]{1,0:T(8,128)(2,1)}, bf16[256,768]{1,0:T(8,128)(2,1)S(1)}, u32[]{:S(2)}, u32[]{:S(2)}) collective-permute-start(bf16[256,768]{1,0:T(8,128)(2,1)} %get-tuple-element.93), channel_id=1, source_target_pairs={{0,12},{4,16},{8,20},{12,24},{16,28},{20,0},{24,4},{28,8},{1,13},{... | collective-permute-start | bytes 1179656 | tf_op jit(solution)/shard_map/ppermute | solution.py:220
  250.6 137.1 %collective-permute-start.3 = (bf16[256,768]{1,0:T(8,128)(2,1)}, bf16[256,768]{1,0:T(8,128)(2,1)S(1)}, u32[]{:S(2)}, u32[]{:S(2)}) collective-permute-start(bf16[256,768]{1,0:T(8,128)(2,1)} %get-tuple-element.94), channel_id=1, source_target_pairs={{0,16},{4,20},{8,24},{12,28},{16,0},{20,4},{24,8},{28,12},{1,17},{... | collective-permute-start | bytes 1179656 | tf_op jit(solution)/shard_map/ppermute | solution.py:220
  262.8 138.1 %collective-permute-start.4 = (bf16[256,768]{1,0:T(8,128)(2,1)S(1)}, bf16[256,768]{1,0:T(8,128)(2,1)S(1)}, u32[]{:S(2)}, u32[]{:S(2)}) collective-permute-start(bf16[256,768]{1,0:T(8,128)(2,1)S(1)} %copy-done.75), channel_id=1, source_target_pairs={{0,20},{4,24},{8,28},{12,0},{16,4},{20,8},{24,12},{28,16},{1,21},{... | collective-permute-start | bytes 1179656 | tf_op jit(solution)/shard_map/ppermute | solution.py:220
  265.0 136.7 %collective-permute-start.5 = (bf16[256,768]{1,0:T(8,128)(2,1)S(1)}, bf16[256,768]{1,0:T(8,128)(2,1)S(1)}, u32[]{:S(2)}, u32[]{:S(2)}) collective-permute-start(bf16[256,768]{1,0:T(8,128)(2,1)S(1)} %copy-done.74), channel_id=1, source_target_pairs={{0,24},{4,28},{8,0},{12,4},{16,8},{20,12},{24,16},{28,20},{1,25},{... | collective-permute-start | bytes 1179656 | tf_op jit(solution)/shard_map/ppermute | solution.py:220
  475.9 339.9 %reduce-scatter.8.cloned.1.call-start = ((), (), s32[]{:S(2)}) async-start(), calls=%async_computation.17 | async-start | bytes 9437184 | tf_op jit(solution)/shard_map/reduce_scatter | solution.py:139
  490.3 67.7 %collective-permute-start.10 = (bf16[384,2048]{1,0:T(8,128)(2,1)}, bf16[384,2048]{1,0:T(8,128)(2,1)}, u32[]{:S(2)}, u32[]{:S(2)}) collective-permute-start(bf16[384,2048]{1,0:T(8,128)(2,1)} %get-tuple-element.162), channel_id=1, source_target_pairs={{0,1},{3,2},{4,5},{7,6},{8,9},{11,10},{12,13},{15,14},{16,17},{19,... | collective-permute-start | bytes 4718600 | tf_op jit(solution)/shard_map/ppermute | solution.py:163
  563.7 261.3 %all-gather.14.cloned.1.call-start = ((), (), s32[]{:S(2)}) async-start(), calls=%async_computation.18 | async-start | bytes 9437184 | tf_op jit(solution)/shard_map/all_gather | solution.py:123
  588.8 59.7 %collective-permute-start.11 = (bf16[384,2048]{1,0:T(8,128)(2,1)}, bf16[384,2048]{1,0:T(8,128)(2,1)}, u32[]{:S(2)}, u32[]{:S(2)}) collective-permute-start(bf16[384,2048]{1,0:T(8,128)(2,1)} %get-tuple-element.158), channel_id=1, source_target_pairs={{1,2},{2,1},{5,6},{6,5},{9,10},{10,9},{13,14},{14,13},{17,18},{18,... | collective-permute-start | bytes 4718600 | tf_op jit(solution)/shard_map/ppermute | solution.py:163
  590.6 57.8 %collective-permute-start.12 = (bf16[1024,768]{1,0:T(8,128)(2,1)}, bf16[1024,768]{1,0:T(8,128)(2,1)}, u32[]{:S(2)}, u32[]{:S(2)}) collective-permute-start(bf16[1024,768]{1,0:T(8,128)(2,1)} %get-tuple-element.104), channel_id=1, source_target_pairs={{0,1},{3,2},{4,5},{7,6},{8,9},{11,10},{12,13},{15,14},{16,17},{19,... | collective-permute-start | bytes 4718600 | tf_op jit(solution)/shard_map/ppermute | solution.py:163
  598.1 118.3 %collective-permute-start.13 = (bf16[1024,768]{1,0:T(8,128)(2,1)}, bf16[1024,768]{1,0:T(8,128)(2,1)}, u32[]{:S(2)}, u32[]{:S(2)}) collective-permute-start(bf16[1024,768]{1,0:T(8,128)(2,1)} %get-tuple-element.108), channel_id=1, source_target_pairs={{0,1},{3,2},{4,5},{7,6},{8,9},{11,10},{12,13},{15,14},{16,17},{19,... | collective-permute-start | bytes 4718600 | tf_op jit(solution)/shard_map/ppermute | solution.py:163
  652.4 75.8 %all-to-all-start.5 = ((bf16[4,256,1024]{1,2,0:T(8,128)(2,1)}), bf16[4,256,1024]{1,2,0:T(8,128)(2,1)}, u32[]{:S(2)}, u32[]{:S(2)}) async-start(bf16[4,256,1024]{1,2,0:T(8,128)(2,1)} %copy.298), calls=%async_computation.7 | async-start | bytes 4194304 | tf_op jit(solution)/shard_map/all_to_all | solution.py:359
  678.5 276.6 %reduce-scatter.6.cloned.1.call-start = ((), (), s32[]{:S(2)}) async-start(), calls=%async_computation.16 | async-start | bytes 9437184 | tf_op jit(solution)/shard_map/reduce_scatter | solution.py:139
  682.6 131.9 %collective-permute-start.20 = (bf16[384,2048]{1,0:T(8,128)(2,1)}, bf16[384,2048]{1,0:T(8,128)(2,1)}, u32[]{:S(2)}, u32[]{:S(2)}) collective-permute-start(bf16[384,2048]{1,0:T(8,128)(2,1)} %add_convert_fusion.5), channel_id=1, source_target_pairs={{1,0},{2,3},{5,4},{6,7},{9,8},{10,11},{13,12},{14,15},{17,16},{18,... | collective-permute-start | bytes 4718600 | tf_op jit(solution)/shard_map/ppermute | solution.py:163
  687.6 128.2 %collective-permute-start.19 = (bf16[384,2048]{1,0:T(8,128)(2,1)}, bf16[384,2048]{1,0:T(8,128)(2,1)}, u32[]{:S(2)}, u32[]{:S(2)}) collective-permute-start(bf16[384,2048]{1,0:T(8,128)(2,1)} %add_convert_fusion.6), channel_id=1, source_target_pairs={{1,0},{2,3},{5,4},{6,7},{9,8},{10,11},{13,12},{14,15},{17,16},{18,... | collective-permute-start | bytes 4718600 | tf_op jit(solution)/shard_map/ppermute | solution.py:163
  716.4 99.4 %collective-permute-start.18 = (bf16[384,2048]{1,0:T(8,128)(2,1)}, bf16[384,2048]{1,0:T(8,128)(2,1)}, u32[]{:S(2)}, u32[]{:S(2)}) collective-permute-start(bf16[384,2048]{1,0:T(8,128)(2,1)} %get-tuple-element.115), channel_id=1, source_target_pairs={{0,1},{3,2},{4,5},{7,6},{8,9},{11,10},{12,13},{15,14},{16,17},{19,... | collective-permute-start | bytes 4718600 | tf_op jit(solution)/shard_map/ppermute | solution.py:163
  751.2 64.6 %collective-permute-start.17 = (bf16[384,2048]{1,0:T(8,128)(2,1)}, bf16[384,2048]{1,0:T(8,128)(2,1)}, u32[]{:S(2)}, u32[]{:S(2)}) collective-permute-start(bf16[384,2048]{1,0:T(8,128)(2,1)} %add_convert_fusion.7), channel_id=1, source_target_pairs={{1,2},{2,1},{5,6},{6,5},{9,10},{10,9},{13,14},{14,13},{17,18},{18,... | collective-permute-start | bytes 4718600 | tf_op jit(solution)/shard_map/ppermute | solution.py:163
  756.6 59.2 %collective-permute-start.16 = (bf16[1024,768]{1,0:T(8,128)(2,1)}, bf16[1024,768]{1,0:T(8,128)(2,1)}, u32[]{:S(2)}, u32[]{:S(2)}) collective-permute-start(bf16[1024,768]{1,0:T(8,128)(2,1)} %add_convert_fusion.8), channel_id=1, source_target_pairs={{1,2},{2,1},{5,6},{6,5},{9,10},{10,9},{13,14},{14,13},{17,18},{18,... | collective-permute-start | bytes 4718600 | tf_op jit(solution)/shard_map/ppermute | solution.py:163
  814.5 100.9 %collective-permute-start.23 = (bf16[1024,768]{1,0:T(8,128)(2,1)}, bf16[1024,768]{1,0:T(8,128)(2,1)}, u32[]{:S(2)}, u32[]{:S(2)}) collective-permute-start(bf16[1024,768]{1,0:T(8,128)(2,1)} %add_convert_fusion.4), channel_id=1, source_target_pairs={{1,0},{2,3},{5,4},{6,7},{9,8},{10,11},{13,12},{14,15},{17,16},{18,... | collective-permute-start | bytes 4718600 | tf_op jit(solution)/shard_map/ppermute | solution.py:163
  819.6 90.9 %collective-permute-start.40 = (bf16[384,2048]{1,0:T(8,128)(2,1)}, bf16[384,2048]{1,0:T(8,128)(2,1)}, u32[]{:S(2)}, u32[]{:S(2)}) collective-permute-start(bf16[384,2048]{1,0:T(8,128)(2,1)} %add_convert_fusion.1), channel_id=1, source_target_pairs={{1,2},{2,1},{5,6},{6,5},{9,10},{10,9},{13,14},{14,13},{17,18},{18,... | collective-permute-start | bytes 4718600 | tf_op jit(solution)/shard_map/ppermute | solution.py:163
  824.5 83.2 %collective-permute-start.32 = (bf16[384,2048]{1,0:T(8,128)(2,1)}, bf16[384,2048]{1,0:T(8,128)(2,1)}, u32[]{:S(2)}, u32[]{:S(2)}) collective-permute-start(bf16[384,2048]{1,0:T(8,128)(2,1)} %broadcast_select_fusion.4), channel_id=1, source_target_pairs={{0,16},{4,20},{8,24},{12,28},{16,0},{20,4},{24,8},{28,12},{1,17},{... | collective-permute-start | bytes 4718600 | tf_op jit(solution)/shard_map/ppermute | solution.py:393
  910.4 70.3 %collective-permute-start.39 = (bf16[384,2048]{1,0:T(8,128)(2,1)}, bf16[384,2048]{1,0:T(8,128)(2,1)}, u32[]{:S(2)}, u32[]{:S(2)}) collective-permute-start(bf16[384,2048]{1,0:T(8,128)(2,1)} %add_convert_fusion.2), channel_id=1, source_target_pairs={{1,0},{2,3},{5,4},{6,7},{9,8},{10,11},{13,12},{14,15},{17,16},{18,... | collective-permute-start | bytes 4718600 | tf_op jit(solution)/shard_map/ppermute | solution.py:163
  915.4 66.9 %collective-permute-start.37 = (bf16[256,2048]{1,0:T(8,128)(2,1)}, bf16[256,2048]{1,0:T(8,128)(2,1)}, u32[]{:S(2)}, u32[]{:S(2)}) collective-permute-start(bf16[256,2048]{1,0:T(8,128)(2,1)} %add_convert_fusion.13), channel_id=1, source_target_pairs={{1,2},{2,1},{5,6},{6,5},{9,10},{10,9},{13,14},{14,13},{17,18},{18,... | collective-permute-start | bytes 3145736 | tf_op jit(solution)/shard_map/ppermute | solution.py:163
  927.9 86.6 %collective-permute-start.41 = (bf16[384,2048]{1,0:T(8,128)(2,1)}, bf16[384,2048]{1,0:T(8,128)(2,1)}, u32[]{:S(2)}, u32[]{:S(2)}) collective-permute-start(bf16[384,2048]{1,0:T(8,128)(2,1)} %add_convert_fusion), channel_id=1, source_target_pairs={{1,0},{2,3},{5,4},{6,7},{9,8},{10,11},{13,12},{14,15},{17,16},{18,... | collective-permute-start | bytes 4718600 | tf_op jit(solution)/shard_map/ppermute | solution.py:163
  950.6 68.7 %all-to-all-start.7 = ((bf16[8,256,768]{2,1,0:T(8,128)(2,1)}), bf16[8,256,768]{2,1,0:T(8,128)(2,1)}, u32[]{:S(2)}, u32[]{:S(2)}) async-start(bf16[8,256,768]{2,1,0:T(8,128)(2,1)} %bitcast.231), calls=%async_computation.10 | async-start | bytes 6291456 | tf_op jit(solution)/shard_map/all_to_all | solution.py:415
  989.7 69.7 %collective-permute-start.31 = (bf16[256,2048]{1,0:T(8,128)(2,1)}, bf16[256,2048]{1,0:T(8,128)(2,1)}, u32[]{:S(2)}, u32[]{:S(2)}) collective-permute-start(bf16[256,2048]{1,0:T(8,128)(2,1)} %add_convert_fusion.16), channel_id=1, source_target_pairs={{1,0},{2,3},{5,4},{6,7},{9,8},{10,11},{13,12},{14,15},{17,16},{18,... | collective-permute-start | bytes 3145736 | tf_op jit(solution)/shard_map/ppermute | solution.py:163
  993.9 84.5 %collective-permute-start.35 = (bf16[256,2048]{1,0:T(8,128)(2,1)}, bf16[256,2048]{1,0:T(8,128)(2,1)}, u32[]{:S(2)}, u32[]{:S(2)}) collective-permute-start(bf16[256,2048]{1,0:T(8,128)(2,1)} %add_convert_fusion.14), channel_id=1, source_target_pairs={{1,0},{2,3},{5,4},{6,7},{9,8},{10,11},{13,12},{14,15},{17,16},{18,... | collective-permute-start | bytes 3145736 | tf_op jit(solution)/shard_map/ppermute | solution.py:163
  (128 other events, 2313.4 us)
Sparse Core Ops, SparseCore 0:
  9.9 92.4 all-gather.5
  104.2 54.2 all-gather.7
  245.7 98.9 all-gather.11
  346.4 71.7 all-gather.9
  476.0 70.5 reduce-scatter.3
  563.9 71.6 reduce-scatter.7
  637.4 54.2 all-gather.13
  716.5 69.0 reduce-scatter.5

commit v7 on v6

--- a/solution.py
+++ b/solution.py
@@ -309,6 +309,7 @@
     normed1_all = gather_rows(normed1_late)
 
     grad_act = jnp.dot(cotangent_all, down_own, preferred_element_type=f32)
+    grad_act = lax.optimization_barrier(grad_act)
     both = product_nt(normed2_all, gate_up_own)
     first, second = both[:, :units], both[:, units:]
     gate = jnp.where(side == 0, first, second)
@@ -358,7 +359,8 @@
     grads_send, activation = meet((grads_send, activation), [s1, d0], [k0, k1])
     grads_low = lax.all_to_all(grads_send, "sp", split_axis=0, concat_axis=1, tiled=True)
     hidden_out = (middle + scatter_sum(product_nt(activation, down_own))).astype(low)
-    grads_low = meet(grads_low, [d1])
+    out_chain = Chain(grad_out, line)
+    grads_low = meet(grads_low, [d1], [out_chain])
     grads_low = grads_low.reshape(rows, line, -1)
     cuts = (grad_query_send.shape[1], grad_query_send.shape[1] + grad_key_send.shape[1])
     grad_query_low = grads_low[:, :, : cuts[0]]
@@ -386,8 +388,7 @@
         1,
     )
     grad_columns = lax.all_to_all(grad_projected, "fsdp", split_axis=1, concat_axis=0, tiled=True)
-    out_chain = Chain(grad_out, line)
-    grad_columns = meet(grad_columns, [d1, k0, k1, s0, s1], [out_chain])
+    grad_columns = meet(grad_columns, [d1, k0, k1, s0, s1, out_chain])
     swapped_back = []
     for chain in (s0, s1):
         swapped_back.append(lax.ppermute(chain.finish(), "fsdp", swap))

time: 1100 us -> 1130 us (1.027)
  waiting for transfers between devices: 448 us -> 463 us
  starting transfers between devices: 149 us -> 162 us
    ppermute x27, waiting for transfers between devices: 156 us -> 202 us  [send(): self.flying = lax.ppermute(self.value, 'sp', self.hops[self.at][0])]
    ppermute x7, waiting for transfers between devices: 141 us -> 125 us  [turn(): arrived = lax.ppermute(blocks[shift], 'fsdp', pairs)]
    ppermute x27, starting transfers between devices: 88.2 us -> 100 us  [send(): self.flying = lax.ppermute(self.value, 'sp', self.hops[self.at][0])]
    unnamed x221 -> x219, local copies, waits for them, and re-layouts: 35.4 us -> 26.3 us
  transfers between devices with their start and end apart: 57 -> 57, of which waited for: 26 -> 24; matrix products, arithmetic and copies ran while one was open for 34% -> 32% of each run, Pallas kernels for 0% -> 0%
where the time goes in v7:
time: 1130 us; the launch traced here: 1120 us
  waiting for transfers between devices  463 us (41%)
  matrix products  165 us (15%)
  starting transfers between devices  162 us (14%)
  other arithmetic  160 us (14%)
  local copies, waits for them, and re-layouts  113 us (10%)
  blocking collectives  38.9 us (3%)
  between operations  16.8 us (1%)
    ppermute x27, waiting for transfers between devices, send(): self.flying = lax.ppermute(self.value, 'sp', self.hops[self.at][0])  202 us
    ppermute x7, waiting for transfers between devices, turn(): arrived = lax.ppermute(blocks[shift], 'fsdp', pairs)  125 us
    ppermute x27, starting transfers between devices, send(): self.flying = lax.ppermute(self.value, 'sp', self.hops[self.at][0])  100 us
    all_gather x5, waiting for transfers between devices, gather_rows(): return lax.all_gather(array, 'fsdp', axis=0, tiled=True)  85.9 us
    convert_element_type x16, other arithmetic, take(): self.value = total.astype(jnp.bfloat16)  51.5 us
    dot_general x4, matrix products, product_nt(): lax.dot_general(inputs, weight, (((1,), (1,)), ((), ())), preferred_eleme...  46.9 us
    dot_general x5, matrix products, product_tn(): lax.dot_general(left, right, (((0,), (0,)), ((), ())), preferred_element_...  42.6 us
    all_to_all x1, blocking collectives, layer(): lax.all_to_all(mixed_heads.reshape(length, -1), 'sp', split_axis=0, conca...  38.9 us
  transfers between devices with their start and end apart: 57, of which 24 were waited for; matrix products, arithmetic and copies ran while one was open for 32% of the time, Pallas kernels for 0%

profile of v7, /device:TPU:0, one launch (start us, length us, event | category | flops | bytes accessed | tf_op | source)
XLA Modules:
  0.0 1118.9 jit_solution(13487660588563424540)
XLA Ops:
  16.5 85.8 %all-gather.6.cloned.1.call-done = bf16[4096,2048]{1,0:T(8,128)(2,1)} async-done(((bf16[512,2048]{1,0:T(8,128)(2,1)}), bf16[4096,2048]{1,0:T(8,128)(2,1)}) %all-gather.6.cloned.1.call-update) | async-done | bytes 16777232 | tf_op jit(solution)/shard_map/all_gather | solution.py:123
  104.5 10.5 fusion.66
  182.5 8.0 all-to-all-done.1
  209.3 38.9 %all_to_all.126 = bf16[4,256,512]{1,2,0:T(8,128)(2,1)} all-to-all(bf16[4,256,512]{1,2,0:T(8,128)(2,1)S(1)} %copy.298), channel_id=1, replica_groups=mesh['fsdp'=8,'sp'=4] {'sp'}, dimensions={0} | all-to-all | bytes 2097152 | tf_op jit(solution)/shard_map/all_to_all | solution.py:302
  274.0 19.5 %collective-permute-done.2 = bf16[256,768]{1,0:T(8,128)(2,1)S(1)} collective-permute-done((bf16[256,768]{1,0:T(8,128)(2,1)}, bf16[256,768]{1,0:T(8,128)(2,1)S(1)}, u32[]{:S(2)}, u32[]{:S(2)}) %collective-permute-start.2) | collective-permute-done | bytes 393248 | tf_op jit(solution)/shard_map/ppermute | solution.py:220
  295.0 98.1 %collective-permute-done.4 = bf16[256,768]{1,0:T(8,128)(2,1)S(1)} collective-permute-done((bf16[256,768]{1,0:T(8,128)(2,1)S(1)}, bf16[256,768]{1,0:T(8,128)(2,1)S(1)}, u32[]{:S(2)}, u32[]{:S(2)}) %collective-permute-start.4) | collective-permute-done | bytes 393248 | tf_op jit(solution)/shard_map/ppermute | solution.py:220
  395.5 11.7 %fusion.67 = f32[2048,768]{1,0:T(8,128)} fusion(bf16[2048,2048]{1,0:T(8,128)(2,1)} %all-gather.10.cloned.1.call-done, bf16[2048,768]{1,0:T(8,128)(2,1)} %constant_dynamic-update-slice_fusion.2), kind=kOutput, calls=%fused_computation.239 | convolution fusion | flops 6442450944 | bytes 17825792 | tf_op jit(solution)/shard_map/dot_general | solution.py:311
  407.1 18.8 %fusion.5 = f32[2048,1536]{1,0:T(8,128)S(1)} fusion(bf16[2048,2048]{1,0:T(8,128)(2,1)} %all-gather.12.cloned.1.call-done, bf16[768,2048]{1,0:T(8,128)(2,1)} %collective-permute-done.7, bf16[768,2048]{1,0:T(8,128)(2,1)} %get-tuple-element.156), kind=kOutput, calls=%fused_computation.32 | convolution fusion | flops 12897484800 | bytes 27262976 | tf_op jit(solution)/shard_map/dot_general | solution.py:127
  441.9 17.9 %convolution_convert_fusion.2 = bf16[2048,2048]{1,0:T(8,128)(2,1)} fusion(bf16[2048,768]{1,0:T(8,128)(2,1)} %select_convert_fusion, bf16[2048,768]{1,0:T(8,128)(2,1)S(1)} %copy-done.49, bf16[768,2048]{1,0:T(8,128)(2,1)} %collective-permute-done.7, bf16[768,2048]{1,0:T(8,128)(2,1)S(1)} %copy-done.52), kind=kOutput, calls=%fused_computation.6 | convolution fusion | flops 12914262016 | bytes 20971520 | tf_op jit(solution)/shard_map/dot_general | solution.py:324
  459.8 10.1 convolution_convert_fusion.4
  477.8 9.6 convolution_convert_fusion.5
  487.4 8.5 convolution_convert_fusion.3
  495.9 13.5 %collective-permute-done.8 = bf16[384,2048]{1,0:T(8,128)(2,1)S(1)} collective-permute-done((bf16[384,2048]{1,0:T(8,128)(2,1)S(1)}, bf16[384,2048]{1,0:T(8,128)(2,1)S(1)}, u32[]{:S(2)}, u32[]{:S(2)}) %collective-permute-start.8) | collective-permute-done | bytes 1572896 | tf_op jit(solution)/shard_map/ppermute | solution.py:163
  512.4 19.9 %reduce-scatter.4.cloned.1.call-done = bf16[256,2048]{1,0:T(8,128)(2,1)} async-done(((bf16[2048,2048]{1,0:T(8,128)(2,1)}), bf16[256,2048]{1,0:T(8,128)(2,1)}) %reduce-scatter.4.cloned.1.call-update) | async-done | bytes 1048592 | tf_op jit(solution)/shard_map/reduce_scatter | solution.py:139
  633.1 11.2 %convolution_convert_fusion.1 = bf16[2048,2048]{1,0:T(8,128)(2,1)} fusion(bf16[2048,768]{1,0:T(8,128)(2,1)S(1)} %copy-done.48, bf16[2048,768]{1,0:T(8,128)(2,1)} %constant_dynamic-update-slice_fusion.2), kind=kOutput, calls=%fused_computation.5 | convolution fusion | flops 6446645248 | bytes 14680064 | tf_op jit(solution)/shard_map/dot_general | solution.py:127
  649.0 26.6 %all-to-all-start.5 = ((bf16[4,256,1024]{1,2,0:T(8,128)(2,1)}), bf16[4,256,1024]{1,2,0:T(8,128)(2,1)}, u32[]{:S(2)}, u32[]{:S(2)}) async-start(bf16[4,256,1024]{1,2,0:T(8,128)(2,1)} %copy.316), calls=%async_computation.7 | async-start | bytes 4194304 | tf_op jit(solution)/shard_map/all_to_all | solution.py:360
  697.3 9.3 collective-permute-start.15
  706.6 37.9 %collective-permute-done.13 = bf16[1024,768]{1,0:T(8,128)(2,1)} collective-permute-done((bf16[1024,768]{1,0:T(8,128)(2,1)}, bf16[1024,768]{1,0:T(8,128)(2,1)}, u32[]{:S(2)}, u32[]{:S(2)}) %collective-permute-start.13) | collective-permute-done | bytes 1572896 | tf_op jit(solution)/shard_map/ppermute | solution.py:163
  765.3 12.9 %collective-permute-done.15 = bf16[384,2048]{1,0:T(8,128)(2,1)} collective-permute-done((bf16[384,2048]{1,0:T(8,128)(2,1)}, bf16[384,2048]{1,0:T(8,128)(2,1)}, u32[]{:S(2)}, u32[]{:S(2)}) %collective-permute-start.15) | collective-permute-done | bytes 1572896 | tf_op jit(solution)/shard_map/ppermute | solution.py:163
  814.9 12.5 %fusion.23 = (f32[2048]{0:T(1024)S(1)}, f32[256]{0:T(256)S(1)}, f32[256,2048]{1,0:T(8,128)}) fusion(bf16[256,2048]{1,0:T(8,128)(2,1)S(1)} %copy-done.12, f32[256]{0:T(256)S(1)} %copy-done.85, f32[2048]{0:T(1024)S(1)} %copy-done.83, bf16[4096,2048]{1,0:T(8,128)(2,1)} %all-gather.6.cloned.1.call-done, bf16[256,1024]{0,1:T(8,128)(2,1)} %bitcast.269, ...), kind=kOutput, calls=%fused_computation.73 | convolution fusion | flops 4304926720 | bytes 22038528 | tf_op jit(solution)/shard_map/dot_general | solution.py:395
  829.5 8.5 collective-permute-start.21
  852.3 8.1 collective-permute-done.21
  869.1 8.7 convolution_convert_fusion.6
  880.3 7.8 collective-permute-start.34
  896.1 13.2 %collective-permute-done.34 = bf16[256,2048]{1,0:T(8,128)(2,1)S(1)} collective-permute-done((bf16[256,2048]{1,0:T(8,128)(2,1)S(1)}, bf16[256,2048]{1,0:T(8,128)(2,1)S(1)}, u32[]{:S(2)}, u32[]{:S(2)}) %collective-permute-start.34) | collective-permute-done | bytes 1048608 | tf_op jit(solution)/shard_map/ppermute | solution.py:163
  909.3 23.6 %collective-permute-start.23 = (bf16[256,2048]{1,0:T(8,128)(2,1)S(1)}, bf16[256,2048]{1,0:T(8,128)(2,1)S(1)}, u32[]{:S(2)}, u32[]{:S(2)}) collective-permute-start(bf16[256,2048]{1,0:T(8,128)(2,1)S(1)} %get-tuple-element.177), channel_id=1, source_target_pairs={{0,1},{3,2},{4,5},{7,6},{8,9},{11,10},{12,13},{15,14},{16,17},{19,... | collective-permute-start | bytes 3145736 | tf_op jit(solution)/shard_map/ppermute | solution.py:163
  941.3 12.5 %collective-permute-done.23 = bf16[256,2048]{1,0:T(8,128)(2,1)S(1)} collective-permute-done((bf16[256,2048]{1,0:T(8,128)(2,1)S(1)}, bf16[256,2048]{1,0:T(8,128)(2,1)S(1)}, u32[]{:S(2)}, u32[]{:S(2)}) %collective-permute-start.23) | collective-permute-done | bytes 1048608 | tf_op jit(solution)/shard_map/ppermute | solution.py:163
  960.5 11.5 %collective-permute-done.25 = bf16[1024,768]{1,0:T(8,128)(2,1)S(1)} collective-permute-done((bf16[1024,768]{1,0:T(8,128)(2,1)S(1)}, bf16[1024,768]{1,0:T(8,128)(2,1)S(1)}, u32[]{:S(2)}, u32[]{:S(2)}) %collective-permute-start.25) | collective-permute-done | bytes 1572896 | tf_op jit(solution)/shard_map/ppermute | solution.py:163
  984.9 21.0 %collective-permute-done.39 = bf16[384,2048]{1,0:T(8,128)(2,1)} collective-permute-done((bf16[384,2048]{1,0:T(8,128)(2,1)}, bf16[384,2048]{1,0:T(8,128)(2,1)}, u32[]{:S(2)}, u32[]{:S(2)}) %collective-permute-start.39) | collective-permute-done | bytes 1572896 | tf_op jit(solution)/shard_map/ppermute | solution.py:163
  1008.6 19.8 %collective-permute-done.38 = bf16[256,2048]{1,0:T(8,128)(2,1)} collective-permute-done((bf16[256,2048]{1,0:T(8,128)(2,1)}, bf16[256,2048]{1,0:T(8,128)(2,1)}, u32[]{:S(2)}, u32[]{:S(2)}) %collective-permute-start.38) | collective-permute-done | bytes 1048608 | tf_op jit(solution)/shard_map/ppermute | solution.py:163
  1039.7 22.3 %collective-permute-done.41 = bf16[384,2048]{1,0:T(8,128)(2,1)} collective-permute-done((bf16[384,2048]{1,0:T(8,128)(2,1)}, bf16[384,2048]{1,0:T(8,128)(2,1)}, u32[]{:S(2)}, u32[]{:S(2)}) %collective-permute-start.41) | collective-permute-done | bytes 1572896 | tf_op jit(solution)/shard_map/ppermute | solution.py:163
  1086.0 18.4 %collective-permute-done.36 = bf16[256,2048]{1,0:T(8,128)(2,1)} collective-permute-done((bf16[256,2048]{1,0:T(8,128)(2,1)}, bf16[256,2048]{1,0:T(8,128)(2,1)}, u32[]{:S(2)}, u32[]{:S(2)}) %collective-permute-start.36) | collective-permute-done | bytes 1048608 | tf_op jit(solution)/shard_map/ppermute | solution.py:163
  (503 shorter events, 445.6 us)
Async XLA Ops:
  7.2 95.2 %all-gather.6.cloned.1.call-start = ((), (), s32[]{:S(2)}) async-start(), calls=%async_computation.11 | async-start | bytes 18874368 | tf_op jit(solution)/shard_map/all_gather | solution.py:123
  7.9 240.3 %all-gather.8.cloned.1.call-start = ((), (), s32[]{:S(2)}) async-start(), calls=%async_computation.12 | async-start | bytes 9437184 | tf_op jit(solution)/shard_map/all_gather | solution.py:123
  102.4 293.1 %all-gather.10.cloned.1.call-start = ((), (), s32[]{:S(2)}) async-start(), calls=%async_computation.13 | async-start | bytes 9437184 | tf_op jit(solution)/shard_map/all_gather | solution.py:123
  165.3 241.9 %all-gather.12.cloned.1.call-start = ((), (), s32[]{:S(2)}) async-start(), calls=%async_computation.14 | async-start | bytes 9437184 | tf_op jit(solution)/shard_map/all_gather | solution.py:123
  255.9 276.5 %reduce-scatter.4.cloned.1.call-start = ((), (), s32[]{:S(2)}) async-start(), calls=%async_computation.15 | async-start | bytes 9437184 | tf_op jit(solution)/shard_map/reduce_scatter | solution.py:139
  260.4 146.8 %collective-permute-start.7 = (bf16[768,2048]{1,0:T(8,128)(2,1)}, bf16[768,2048]{1,0:T(8,128)(2,1)}, u32[]{:S(2)}, u32[]{:S(2)}) collective-permute-start(bf16[768,2048]{1,0:T(8,128)(2,1)} %get-tuple-element.99), channel_id=1, source_target_pairs={{0,16},{4,20},{8,24},{12,28},{16,0},{20,4},{24,8},{28,12},{1,17},{... | collective-permute-start | bytes 9437192 | tf_op jit(solution)/shard_map/ppermute | solution.py:276
  270.3 122.8 %collective-permute-start.4 = (bf16[256,768]{1,0:T(8,128)(2,1)S(1)}, bf16[256,768]{1,0:T(8,128)(2,1)S(1)}, u32[]{:S(2)}, u32[]{:S(2)}) collective-permute-start(bf16[256,768]{1,0:T(8,128)(2,1)S(1)} %copy-done.76), channel_id=1, source_target_pairs={{0,20},{4,24},{8,28},{12,0},{16,4},{20,8},{24,12},{28,16},{1,21},{... | collective-permute-start | bytes 1179656 | tf_op jit(solution)/shard_map/ppermute | solution.py:220
  272.8 121.1 %collective-permute-start.5 = (bf16[256,768]{1,0:T(8,128)(2,1)S(1)}, bf16[256,768]{1,0:T(8,128)(2,1)S(1)}, u32[]{:S(2)}, u32[]{:S(2)}) collective-permute-start(bf16[256,768]{1,0:T(8,128)(2,1)S(1)} %copy-done.75), channel_id=1, source_target_pairs={{0,24},{4,28},{8,0},{12,4},{16,8},{20,12},{24,16},{28,20},{1,25},{... | collective-permute-start | bytes 1179656 | tf_op jit(solution)/shard_map/ppermute | solution.py:220
  293.5 101.2 %collective-permute-start.6 = (bf16[256,768]{1,0:T(8,128)(2,1)S(1)}, bf16[256,768]{1,0:T(8,128)(2,1)S(1)}, u32[]{:S(2)}, u32[]{:S(2)}) collective-permute-start(bf16[256,768]{1,0:T(8,128)(2,1)S(1)} %copy-done.74), channel_id=1, source_target_pairs={{0,28},{4,0},{8,4},{12,8},{16,12},{20,16},{24,20},{28,24},{1,29},{... | collective-permute-start | bytes 1179656 | tf_op jit(solution)/shard_map/ppermute | solution.py:220
  459.8 290.3 %reduce-scatter.8.cloned.1.call-start = ((), (), s32[]{:S(2)}) async-start(), calls=%async_computation.17 | async-start | bytes 9437184 | tf_op jit(solution)/shard_map/reduce_scatter | solution.py:139
  475.3 67.9 %collective-permute-start.10 = (bf16[384,2048]{1,0:T(8,128)(2,1)}, bf16[384,2048]{1,0:T(8,128)(2,1)}, u32[]{:S(2)}, u32[]{:S(2)}) collective-permute-start(bf16[384,2048]{1,0:T(8,128)(2,1)} %get-tuple-element.164), channel_id=1, source_target_pairs={{0,1},{3,2},{4,5},{7,6},{8,9},{11,10},{12,13},{15,14},{16,17},{19,... | collective-permute-start | bytes 4718600 | tf_op jit(solution)/shard_map/ppermute | solution.py:163
  563.0 278.5 %reduce-scatter.6.cloned.1.call-start = ((), (), s32[]{:S(2)}) async-start(), calls=%async_computation.16 | async-start | bytes 9437184 | tf_op jit(solution)/shard_map/reduce_scatter | solution.py:139
  644.4 224.7 %all-gather.14.cloned.1.call-start = ((), (), s32[]{:S(2)}) async-start(), calls=%async_computation.18 | async-start | bytes 9437184 | tf_op jit(solution)/shard_map/all_gather | solution.py:123
  649.0 101.0 %all-to-all-start.5 = ((bf16[4,256,1024]{1,2,0:T(8,128)(2,1)}), bf16[4,256,1024]{1,2,0:T(8,128)(2,1)}, u32[]{:S(2)}, u32[]{:S(2)}) async-start(bf16[4,256,1024]{1,2,0:T(8,128)(2,1)} %copy.316), calls=%async_computation.7 | async-start | bytes 4194304 | tf_op jit(solution)/shard_map/all_to_all | solution.py:360
  675.6 68.9 %collective-permute-start.13 = (bf16[1024,768]{1,0:T(8,128)(2,1)}, bf16[1024,768]{1,0:T(8,128)(2,1)}, u32[]{:S(2)}, u32[]{:S(2)}) collective-permute-start(bf16[1024,768]{1,0:T(8,128)(2,1)} %get-tuple-element.109), channel_id=1, source_target_pairs={{0,1},{3,2},{4,5},{7,6},{8,9},{11,10},{12,13},{15,14},{16,17},{19,... | collective-permute-start | bytes 4718600 | tf_op jit(solution)/shard_map/ppermute | solution.py:163
  685.7 143.8 %collective-permute-start.20 = (bf16[384,2048]{1,0:T(8,128)(2,1)}, bf16[384,2048]{1,0:T(8,128)(2,1)}, u32[]{:S(2)}, u32[]{:S(2)}) collective-permute-start(bf16[384,2048]{1,0:T(8,128)(2,1)} %add_convert_fusion.5), channel_id=1, source_target_pairs={{1,0},{2,3},{5,4},{6,7},{9,8},{10,11},{13,12},{14,15},{17,16},{18,... | collective-permute-start | bytes 4718600 | tf_op jit(solution)/shard_map/ppermute | solution.py:163
  690.7 160.1 %collective-permute-start.19 = (bf16[384,2048]{1,0:T(8,128)(2,1)}, bf16[384,2048]{1,0:T(8,128)(2,1)}, u32[]{:S(2)}, u32[]{:S(2)}) collective-permute-start(bf16[384,2048]{1,0:T(8,128)(2,1)} %add_convert_fusion.6), channel_id=1, source_target_pairs={{1,0},{2,3},{5,4},{6,7},{9,8},{10,11},{13,12},{14,15},{17,16},{18,... | collective-permute-start | bytes 4718600 | tf_op jit(solution)/shard_map/ppermute | solution.py:163
  695.5 69.8 %collective-permute-start.14 = (bf16[1024,768]{1,0:T(8,128)(2,1)}, bf16[1024,768]{1,0:T(8,128)(2,1)}, u32[]{:S(2)}, u32[]{:S(2)}) collective-permute-start(bf16[1024,768]{1,0:T(8,128)(2,1)} %add_convert_fusion.9), channel_id=1, source_target_pairs={{1,2},{2,1},{5,6},{6,5},{9,10},{10,9},{13,14},{14,13},{17,18},{18,... | collective-permute-start | bytes 4718600 | tf_op jit(solution)/shard_map/ppermute | solution.py:163
  697.3 80.9 %collective-permute-start.15 = (bf16[384,2048]{1,0:T(8,128)(2,1)}, bf16[384,2048]{1,0:T(8,128)(2,1)}, u32[]{:S(2)}, u32[]{:S(2)}) collective-permute-start(bf16[384,2048]{1,0:T(8,128)(2,1)} %get-tuple-element.113), channel_id=1, source_target_pairs={{0,1},{3,2},{4,5},{7,6},{8,9},{11,10},{12,13},{15,14},{16,17},{19,... | collective-permute-start | bytes 4718600 | tf_op jit(solution)/shard_map/ppermute | solution.py:163
  744.5 107.8 %collective-permute-start.18 = (bf16[384,2048]{1,0:T(8,128)(2,1)}, bf16[384,2048]{1,0:T(8,128)(2,1)}, u32[]{:S(2)}, u32[]{:S(2)}) collective-permute-start(bf16[384,2048]{1,0:T(8,128)(2,1)} %get-tuple-element.117), channel_id=1, source_target_pairs={{0,1},{3,2},{4,5},{7,6},{8,9},{11,10},{12,13},{15,14},{16,17},{19,... | collective-permute-start | bytes 4718600 | tf_op jit(solution)/shard_map/ppermute | solution.py:163
  781.9 78.5 %collective-permute-start.17 = (bf16[384,2048]{1,0:T(8,128)(2,1)}, bf16[384,2048]{1,0:T(8,128)(2,1)}, u32[]{:S(2)}, u32[]{:S(2)}) collective-permute-start(bf16[384,2048]{1,0:T(8,128)(2,1)} %add_convert_fusion.7), channel_id=1, source_target_pairs={{1,2},{2,1},{5,6},{6,5},{9,10},{10,9},{13,14},{14,13},{17,18},{18,... | collective-permute-start | bytes 4718600 | tf_op jit(solution)/shard_map/ppermute | solution.py:163
  786.8 73.6 %collective-permute-start.16 = (bf16[1024,768]{1,0:T(8,128)(2,1)}, bf16[1024,768]{1,0:T(8,128)(2,1)}, u32[]{:S(2)}, u32[]{:S(2)}) collective-permute-start(bf16[1024,768]{1,0:T(8,128)(2,1)} %add_convert_fusion.8), channel_id=1, source_target_pairs={{1,2},{2,1},{5,6},{6,5},{9,10},{10,9},{13,14},{14,13},{17,18},{18,... | collective-permute-start | bytes 4718600 | tf_op jit(solution)/shard_map/ppermute | solution.py:163
  850.8 89.3 %collective-permute-start.24 = (bf16[1024,768]{1,0:T(8,128)(2,1)S(1)}, bf16[1024,768]{1,0:T(8,128)(2,1)}, u32[]{:S(2)}, u32[]{:S(2)}) collective-permute-start(bf16[1024,768]{1,0:T(8,128)(2,1)S(1)} %copy-done.28), channel_id=1, source_target_pairs={{1,0},{2,3},{5,4},{6,7},{9,8},{10,11},{13,12},{14,15},{17,16},{18,... | collective-permute-start | bytes 4718600 | tf_op jit(solution)/shard_map/ppermute | solution.py:163
  862.9 72.7 %collective-permute-start.40 = (bf16[384,2048]{1,0:T(8,128)(2,1)S(1)}, bf16[384,2048]{1,0:T(8,128)(2,1)}, u32[]{:S(2)}, u32[]{:S(2)}) collective-permute-start(bf16[384,2048]{1,0:T(8,128)(2,1)S(1)} %add_convert_fusion.1), channel_id=1, source_target_pairs={{1,2},{2,1},{5,6},{6,5},{9,10},{10,9},{13,14},{14,13},{17,18},{18,... | collective-permute-start | bytes 4718600 | tf_op jit(solution)/shard_map/ppermute | solution.py:163
  867.5 65.5 %collective-permute-start.33 = (bf16[384,2048]{1,0:T(8,128)(2,1)}, bf16[384,2048]{1,0:T(8,128)(2,1)}, u32[]{:S(2)}, u32[]{:S(2)}) collective-permute-start(bf16[384,2048]{1,0:T(8,128)(2,1)} %broadcast_select_fusion.4), channel_id=1, source_target_pairs={{0,16},{4,20},{8,24},{12,28},{16,0},{20,4},{24,8},{28,12},{1,17},{... | collective-permute-start | bytes 4718600 | tf_op jit(solution)/shard_map/ppermute | solution.py:394
  935.6 70.3 %collective-permute-start.39 = (bf16[384,2048]{1,0:T(8,128)(2,1)}, bf16[384,2048]{1,0:T(8,128)(2,1)}, u32[]{:S(2)}, u32[]{:S(2)}) collective-permute-start(bf16[384,2048]{1,0:T(8,128)(2,1)} %add_convert_fusion.2), channel_id=1, source_target_pairs={{1,0},{2,3},{5,4},{6,7},{9,8},{10,11},{13,12},{14,15},{17,16},{18,... | collective-permute-start | bytes 4718600 | tf_op jit(solution)/shard_map/ppermute | solution.py:163
  940.1 88.3 %collective-permute-start.38 = (bf16[256,2048]{1,0:T(8,128)(2,1)}, bf16[256,2048]{1,0:T(8,128)(2,1)}, u32[]{:S(2)}, u32[]{:S(2)}) collective-permute-start(bf16[256,2048]{1,0:T(8,128)(2,1)} %add_convert_fusion.12), channel_id=1, source_target_pairs={{1,0},{2,3},{5,4},{6,7},{9,8},{10,11},{13,12},{14,15},{17,16},{18,... | collective-permute-start | bytes 3145736 | tf_op jit(solution)/shard_map/ppermute | solution.py:163
  953.8 108.3 %collective-permute-start.41 = (bf16[384,2048]{1,0:T(8,128)(2,1)}, bf16[384,2048]{1,0:T(8,128)(2,1)}, u32[]{:S(2)}, u32[]{:S(2)}) collective-permute-start(bf16[384,2048]{1,0:T(8,128)(2,1)} %add_convert_fusion), channel_id=1, source_target_pairs={{1,0},{2,3},{5,4},{6,7},{9,8},{10,11},{13,12},{14,15},{17,16},{18,... | collective-permute-start | bytes 4718600 | tf_op jit(solution)/shard_map/ppermute | solution.py:163
  957.3 73.8 %collective-permute-start.31 = (bf16[256,2048]{1,0:T(8,128)(2,1)}, bf16[256,2048]{1,0:T(8,128)(2,1)}, u32[]{:S(2)}, u32[]{:S(2)}) collective-permute-start(bf16[256,2048]{1,0:T(8,128)(2,1)} %get-tuple-element.174), channel_id=1, source_target_pairs={{1,2},{2,1},{5,6},{6,5},{9,10},{10,9},{13,14},{14,13},{17,18},{18,... | collective-permute-start | bytes 3145736 | tf_op jit(solution)/shard_map/ppermute | solution.py:163
  972.1 63.4 %collective-permute-start.35 = (bf16[256,2048]{1,0:T(8,128)(2,1)}, bf16[256,2048]{1,0:T(8,128)(2,1)}, u32[]{:S(2)}, u32[]{:S(2)}) collective-permute-start(bf16[256,2048]{1,0:T(8,128)(2,1)} %get-tuple-element.175), channel_id=1, source_target_pairs={{1,2},{2,1},{5,6},{6,5},{9,10},{10,9},{13,14},{14,13},{17,18},{18,... | collective-permute-start | bytes 3145736 | tf_op jit(solution)/shard_map/ppermute | solution.py:163
  975.8 89.0 %all-to-all-start.7 = ((bf16[8,256,768]{2,1,0:T(8,128)(2,1)}), bf16[8,256,768]{2,1,0:T(8,128)(2,1)S(1)}, u32[]{:S(2)}, u32[]{:S(2)}) async-start(bf16[8,256,768]{2,1,0:T(8,128)(2,1)} %bitcast.231), calls=%async_computation.10 | async-start | bytes 6291456 | tf_op jit(solution)/shard_map/all_to_all | solution.py:416
  1038.5 65.9 %collective-permute-start.36 = (bf16[256,2048]{1,0:T(8,128)(2,1)}, bf16[256,2048]{1,0:T(8,128)(2,1)}, u32[]{:S(2)}, u32[]{:S(2)}) collective-permute-start(bf16[256,2048]{1,0:T(8,128)(2,1)} %add_convert_fusion.14), channel_id=1, source_target_pairs={{1,0},{2,3},{5,4},{6,7},{9,8},{10,11},{13,12},{14,15},{17,16},{18,... | collective-permute-start | bytes 3145736 | tf_op jit(solution)/shard_map/ppermute | solution.py:163
  (127 other events, 2171.6 us)
Sparse Core Ops, SparseCore 0:
  9.9 92.4 all-gather.5
  104.2 54.2 all-gather.7
  160.4 54.2 all-gather.9
  256.0 103.1 all-gather.11
  459.9 72.4 reduce-scatter.3
  549.1 72.9 reduce-scatter.7
  644.5 95.3 reduce-scatter.5
  741.8 54.2 all-gather.13
